TPU v7x, 8 devices: a whole 2x2x1 slice. The times are simulated.
8 devices in a mesh: col: 4 (over z, y, x), row: 2 (over core).
Axes of the slice: x: 2, y: 2, z: 1, core: 2. Of those that a mesh axis runs over, the one named last changes fastest.
Arguments:
- vel_u: float32 [16, 512, 2048], P(None, 'row', 'col')
- vel_v: float32 [16, 512, 2048], P(None, 'row', 'col')
- temperature: float32 [16, 512, 2048], P(None, 'row', 'col')
- salinity: float32 [16, 512, 2048], P(None, 'row', 'col')
- sea_level: float32 [512, 2048], P('row', 'col')
- trans_u: float32 [512, 2048], P('row', 'col')
- trans_v: float32 [512, 2048], P('row', 'col')
- bathymetry: float32 [512, 2048], P('row', 'col')
- kmt_levels: int32 [512, 2048], P('row', 'col')
- tide_force: float32 [30, 2], replicated
Outputs:
- output 1: float32 [512, 2048], P('row', 'col')
- output 2: float32 [512, 2048], P('row', 'col')
- output 3: float32 [512, 2048], P('row', 'col')
- output 4: float32 [16, 512, 2048], P(None, 'row', 'col')
- output 5: float32 [16, 512, 2048], P(None, 'row', 'col')
- output 6: float32 [16, 512, 2048], P(None, 'row', 'col')
- output 7: float32 [16, 512, 2048], P(None, 'row', 'col')
All inputs are finite; a program needn't handle non-finite values.
Results may differ from a plain program's by a relative error of at most 0.001.
Values sent between devices are 32-bit elements.
A program may use at most 1 GiB of HBM per device.

v0:
```python
import jax
import jax.numpy as jnp
from jax import lax
from jax.sharding import PartitionSpec as P

GRAVITY = 1.0
GRID_DX = 1.0
TIME_STEP = 4.0
ALPHA_T = 0.02
BETA_S = 0.015
T_REF = 1.0
S_REF = 1.0
VISC_KV = 0.001
DIFF_KT = 0.0005


def level_mask(count, n_levels):
    levels = jnp.arange(n_levels, dtype=jnp.int32)[:, None, None]
    return (levels < count[None]).astype(jnp.float32)


def interface_coef(count, thick, kappa, n_levels):
    levels = jnp.arange(n_levels - 1, dtype=jnp.int32)[:, None, None]
    active = (levels + 1 < count[None]).astype(jnp.float32)
    safe = jnp.where(count > 0, thick, 1.0)
    return active * (TIME_STEP * kappa / (safe * safe))[None]


def column_solve(source, couple):
    edge = jnp.zeros_like(source[:1])
    upper = jnp.concatenate([couple, edge], axis=0)
    lower = jnp.concatenate([edge, couple], axis=0)
    diag = 1.0 + upper + lower

    def forward(carry, slab):
        gain_prev, part_prev = carry
        lower_k, diag_k, upper_k, source_k = slab
        pivot = diag_k - lower_k * gain_prev
        gain = upper_k / pivot
        part = (source_k + lower_k * part_prev) / pivot
        return (gain, part), (gain, part)

    start = (jnp.zeros_like(source[0]), jnp.zeros_like(source[0]))
    _, (gains, parts) = lax.scan(forward, start, (lower, diag, upper, source))

    def backward(below, slab):
        gain, part = slab
        here = part + gain * below
        return here, here

    _, profile = lax.scan(backward, jnp.zeros_like(source[0]), (gains, parts), reverse=True)
    return profile


def geometry(kmt_ext, depth_ext):
    kmt_cell = kmt_ext[1:-1, 1:-1]
    thick_ext = depth_ext / jnp.maximum(kmt_ext, 1).astype(jnp.float32)
    thick_cell = thick_ext[1:-1, 1:-1]
    return {"k_cell": kmt_cell, "k_u": jnp.minimum(kmt_cell, kmt_ext[1:-1, 2:]), "k_v": jnp.minimum(kmt_cell, kmt_ext[2:, 1:-1]), "dz_cell": thick_cell, "dz_u": 0.5 * (thick_cell + thick_ext[1:-1, 2:]), "dz_v": 0.5 * (thick_cell + thick_ext[2:, 1:-1])}


def surface_fields(layout):
    k_faces = jnp.stack([layout["k_u"], layout["k_v"]])
    face_depth = k_faces.astype(jnp.float32) * jnp.stack([layout["dz_u"], layout["dz_v"]])
    face_wet = (k_faces > 0).astype(jnp.float32)
    wet_cell = (layout["k_cell"] > 0).astype(jnp.float32)
    return face_depth, face_wet, wet_cell


def momentum_tend(u_ext, v_ext, p_ext):
    cen_u = 0.5 * (u_ext[:, 1:-1, :-1] + u_ext[:, 1:-1, 1:])
    corner_v = 0.5 * (v_ext[:, :-1, 1:-1] + v_ext[:, :-1, 2:])
    corner_u = 0.5 * (u_ext[:, :-1, 1:-1] + u_ext[:, 1:, 1:-1])
    flux_uu = cen_u * cen_u
    flux_vu = corner_v * corner_u
    tend_u = -(flux_uu[:, :, 1:] - flux_uu[:, :, :-1] + flux_vu[:, 1:, :] - flux_vu[:, :-1, :] + p_ext[:, 1:-1, 2:] - p_ext[:, 1:-1, 1:-1]) / GRID_DX
    cen_v = 0.5 * (v_ext[:, :-1, 1:-1] + v_ext[:, 1:, 1:-1])
    side_u = 0.5 * (u_ext[:, 1:-1, :-1] + u_ext[:, 2:, :-1])
    side_v = 0.5 * (v_ext[:, 1:-1, :-1] + v_ext[:, 1:-1, 1:])
    flux_vv = cen_v * cen_v
    flux_uv = side_u * side_v
    tend_v = -(flux_vv[:, 1:, :] - flux_vv[:, :-1, :] + flux_uv[:, :, 1:] - flux_uv[:, :, :-1] + p_ext[:, 2:, 1:-1] - p_ext[:, 1:-1, 1:-1]) / GRID_DX
    return tend_u, tend_v


def baroclinic_predict(vel_u, vel_v, value_a11, salinity, layout, halo_fn):
    n_levels = vel_u.shape[0]
    mask_c = level_mask(layout["k_cell"], n_levels)
    mask_u = level_mask(layout["k_u"], n_levels)
    mask_v = level_mask(layout["k_v"], n_levels)
    vel_um = vel_u * mask_u
    vel_vm = vel_v * mask_v
    density = mask_c * (BETA_S * (salinity - S_REF) - ALPHA_T * (value_a11 - T_REF))
    pressure = GRAVITY * layout["dz_cell"] * (jnp.cumsum(density, axis=0) - 0.5 * density)
    cell_coef = interface_coef(layout["k_cell"], layout["dz_cell"], DIFF_KT, n_levels)
    temp_mix = column_solve(value_a11 * mask_c, cell_coef)
    salt_mix = column_solve(salinity * mask_c, cell_coef)
    edges = halo_fn(jnp.stack([vel_um, vel_vm, pressure, temp_mix, salt_mix]))
    tend_u, tend_v = momentum_tend(edges[0], edges[1], edges[2])
    u_star = column_solve(mask_u * (vel_um + TIME_STEP * tend_u), interface_coef(layout["k_u"], layout["dz_u"], VISC_KV, n_levels))
    v_star = column_solve(mask_v * (vel_vm + TIME_STEP * tend_v), interface_coef(layout["k_v"], layout["dz_v"], VISC_KV, n_levels))
    forcing = jnp.stack([jnp.sum(layout["dz_u"] * (u_star - vel_um), axis=0), jnp.sum(layout["dz_v"] * (v_star - vel_vm), axis=0)]) / TIME_STEP
    return u_star, v_star, forcing, edges[3:], (mask_c, mask_u, mask_v)


def barotropic(eta_start, trans_start, face_depth, face_wet, wet_cell, forcing, tide_force, halo_fn):
    n_sub = tide_force.shape[0]
    dt_sub = TIME_STEP / n_sub
    weight_norm = 6.0 / (n_sub * (n_sub + 1) * (n_sub + 2))

    def substep(step, carry):
        eta_now, trans_now, trans_avg = carry
        trans_ext = halo_fn(trans_now)
        divergence = (trans_now[0] - trans_ext[0, 1:-1, :-2] + trans_now[1] - trans_ext[1, :-2, 1:-1]) / GRID_DX
        eta_next = wet_cell * (eta_now - dt_sub * divergence)
        eta_ext = halo_fn(eta_next)
        slope = jnp.stack([eta_ext[1:-1, 2:] - eta_next, eta_ext[2:, 1:-1] - eta_next]) / GRID_DX
        tide_now = lax.dynamic_index_in_dim(tide_force, step, 0, keepdims=False)
        trans_next = face_wet * (trans_now + dt_sub * (face_depth * (tide_now[:, None, None] - GRAVITY * slope) + forcing))
        weight = weight_norm * ((step + 1) * (n_sub - step)).astype(jnp.float32)
        return eta_next, trans_next, trans_avg + weight * trans_next

    return lax.fori_loop(0, n_sub, substep, (eta_start, trans_start, jnp.zeros_like(trans_start)))


def correct_velocity(star, dz_face, depth_face, mean_trans, mask):
    safe = jnp.where(depth_face > 0, depth_face, 1.0)
    return mask * (star + ((mean_trans - jnp.sum(dz_face * star, axis=0)) / safe)[None])


def advect_tracers(tracer_ext, flow_ext, mask_c):
    flux_x = flow_ext[0, :, 1:-1, :-1] * (0.5 * (tracer_ext[..., 1:-1, :-1] + tracer_ext[..., 1:-1, 1:]))
    flux_y = flow_ext[1, :, :-1, 1:-1] * (0.5 * (tracer_ext[..., :-1, 1:-1] + tracer_ext[..., 1:, 1:-1]))
    divergence = (flux_x[..., 1:] - flux_x[..., :-1] + flux_y[..., 1:, :] - flux_y[..., :-1, :]) / GRID_DX
    return mask_c * (tracer_ext[..., 1:-1, 1:-1] - TIME_STEP * divergence)


def baroclinic_finish(u_star, v_star, trans_avg, face_depth, layout, tracer_ext, masks, halo_fn):
    mask_c, mask_u, mask_v = masks
    vel_uc = correct_velocity(u_star, layout["dz_u"], face_depth[0], trans_avg[0], mask_u)
    vel_vc = correct_velocity(v_star, layout["dz_v"], face_depth[1], trans_avg[1], mask_v)
    flows = halo_fn(jnp.stack([vel_uc, vel_vc]))
    tracers = advect_tracers(tracer_ext, flows, mask_c)
    return vel_uc, vel_vc, tracers[0], tracers[1]


def ocean_step(vel_u, vel_v, value_a11, salinity, sea_level, trans_u, trans_v, bathymetry, kmt_levels, tide_force, halo_fn):
    layout = geometry(halo_fn(kmt_levels), halo_fn(bathymetry))
    u_star, v_star, forcing, tracer_ext, masks = baroclinic_predict(vel_u, vel_v, value_a11, salinity, layout, halo_fn)
    face_depth, face_wet, wet_cell = surface_fields(layout)
    eta_new, trans_new, trans_avg = barotropic(wet_cell * sea_level, face_wet * jnp.stack([trans_u, trans_v]), face_depth, face_wet, wet_cell, forcing, tide_force, halo_fn)
    vel_uc, vel_vc, temp_new, salt_new = baroclinic_finish(u_star, v_star, trans_avg, face_depth, layout, tracer_ext, masks, halo_fn)
    return eta_new, trans_new[0], trans_new[1], vel_uc, vel_vc, temp_new, salt_new


def solution(mesh):
    n_cols = mesh.shape["col"]
    n_rows = mesh.shape["row"]
    east_perm = [(member, (member - 1) % n_cols) for member in range(n_cols)]
    west_perm = [(member, (member + 1) % n_cols) for member in range(n_cols)]
    north_perm = [(member, member - 1) for member in range(1, n_rows)]
    south_perm = [(member, member + 1) for member in range(n_rows - 1)]

    def halo_swap(field):
        from_east = lax.ppermute(field[..., :1], "col", east_perm)
        from_west = lax.ppermute(field[..., -1:], "col", west_perm)
        wide = jnp.concatenate([from_west, field, from_east], axis=-1)
        from_north = lax.ppermute(wide[..., :1, :], "row", north_perm)
        from_south = lax.ppermute(wide[..., -1:, :], "row", south_perm)
        return jnp.concatenate([from_south, wide, from_north], axis=-2)

    def local_step(vel_u, vel_v, value_a11, salinity, sea_level, trans_u, trans_v, bathymetry, kmt_levels, tide_force):
        return ocean_step(vel_u, vel_v, value_a11, salinity, sea_level, trans_u, trans_v, bathymetry, kmt_levels, tide_force, halo_swap)

    spec_cube = P(None, "row", "col")
    spec_plane = P("row", "col")
    return jax.shard_map(local_step, mesh=mesh, in_specs=(spec_cube, spec_cube, spec_cube, spec_cube, spec_plane, spec_plane, spec_plane, spec_plane, spec_plane, P(None, None)), out_specs=(spec_plane, spec_plane, spec_plane, spec_cube, spec_cube, spec_cube, spec_cube), check_vma=False)
```

profile of v0, /device:TPU:0, one launch (start us, length us, event | category | flops | bytes accessed | tf_op | source)
XLA Modules:
  0.0 1944.0 jit_solution(1546447630048644386)
XLA Ops:
  10.0 11.4 fusion.61
  37.2 7.3 compare_select_fusion.2
  44.6 10.4 fusion.99
  63.9 55.8 %while.156 = (s32[]{:T(128)}, f32[256,512]{1,0:T(8,128)}, f32[256,512]{1,0:T(8,128)}, f32[16,256,512]{2,1,0:T(8,128)}, f32[16,256,512]{2,1,0:T(8,128)}, /*index=...) while((s32[]{:T(128)}, f32[256,512]{1,0:T(8,128)}, ...), condition=%wide.region_6.7_spmd.clone, body=%wide.region_5.6_spmd.clone.sunk | while | flops 1048579 | bytes 5243511 | solution.py:44
  124.1 39.4 %while.157 = (s32[]{:T(128)}, f32[256,512]{1,0:T(8,128)S(1)}, f32[16,256,512]{2,1,0:T(8,128)}, f32[16,256,512]{2,1,0:T(8,128)}, f32[16,256,512]{2,1,0:T(8,128)}, /*index=5*/s32[]{:T(128)}, s32[]{:T(128)}, s32[]{:T(128)}) while((s32[]{:T(128)}, f32[256,512]{1,0:T(8,128)S(1)}, f32[16,256,512]{2,1,0:T(8,128)}, ...), condition=%wide.region_8.9_spmd.clone, body=%wide.region_7.8_spmd.clone.sunk | while | flops 393220 | bytes 2621551 | solution.py:51
  172.4 46.9 %while.154 = (s32[]{:T(128)}, f32[256,512]{1,0:T(8,128)S(1)}, f32[256,512]{1,0:T(8,128)S(1)}, f32[16,256,512]{2,1,0:T(8,128)}, f32[16,256,512]{2,1,0:T(8,128)}, ...) while((s32[]{:T(128)}, f32[256,512]{1,0:T(8,128)S(1)}, ...), condition=%wide.region_2.3_spmd.clone, body=%wide.region_1.2_spmd.clone.sunk | while | flops 1048579 | bytes 5243511 | solution.py:44
  223.6 39.4 %while.155 = (s32[]{:T(128)}, f32[256,512]{1,0:T(8,128)S(1)}, f32[16,256,512]{2,1,0:T(8,128)}, f32[16,256,512]{2,1,0:T(8,128)}, f32[16,256,512]{2,1,0:T(8,128)}, /*index=5*/s32[]{:T(128)}, s32[]{:T(128)}, s32[]{:T(128)}) while((s32[]{:T(128)}, f32[256,512]{1,0:T(8,128)S(1)}, f32[16,256,512]{2,1,0:T(8,128)}, ...), condition=%wide.region_4.5_spmd.clone, body=%wide.region_3.4_spmd.clone.sunk | while | flops 393220 | bytes 2621551 | solution.py:51
  263.0 8.4 bitcast_dynamic-update-slice_fusion.14
  271.4 8.4 bitcast_dynamic-update-slice_fusion.13
  286.5 8.0 constant_dynamic-update-slice_fusion.1
  294.5 8.0 constant_dynamic-update-slice_fusion
  302.5 16.1 fusion.97
  333.6 13.8 fusion.98
  347.4 14.0 fusion.100
  382.9 25.6 %maximum_bitcast_fusion.1 = (f32[16,258,514]{2,1,0:T(8,128)S(1)}, f32[16,258,514]{2,1,0:T(8,128)}, f32[16,258,514]{2,1,0:T(8,128)}) fusion(f32[5,16,1,514]{3,2,1,0:T(1,128)S(1)} %collective-permute-done.17, f32[5,16,1,514]{3,2,1,0:T(1,128)S(1)} %collective-permute-done.16, f32[5,16,256,1]{3,2,1,0:T(8,128)} %copy.21, ...), kind=kLoop, calls=%fused_computation.99 | loop fusion | flops 25461504 | bytes 67897344 | tf_op jit(solution)/shard_map/squeeze | solution.py:99
  412.5 19.6 %fusion.42 = (f32[16,256,513]{2,1,0:T(8,128)}, f32[16,256,513]{2,1,0:T(8,128)}) fusion(f32[16,258,514]{2,1,0:T(8,128)S(1)} %get-tuple-element.1206, f32[16,258,514]{2,1,0:T(8,128)} %get-tuple-element.1207), kind=kLoop, calls=%fused_computation.111 | loop fusion | flops 16809984 | bytes 58834944 | tf_op jit(solution)/shard_map/mul | solution.py:74
  432.1 28.2 %fusion.48 = (f32[16,257,512]{2,1,0:T(8,128)}, f32[16,257,512]{2,1,0:T(8,128)}) fusion(f32[16,258,514]{2,1,0:T(8,128)} %copy-done.1, f32[16,258,514]{2,1,0:T(8,128)} %get-tuple-element.1207), kind=kLoop, calls=%fused_computation.123 | loop fusion | flops 16842752 | bytes 58949632 | tf_op jit(solution)/shard_map/mul | solution.py:75
  460.3 45.1 %fusion.59 = (f32[16,256,512]{2,1,0:T(8,128)}, f32[16,256,512]{2,1,0:T(8,128)}) fusion(f32[16,258,514]{2,1,0:T(8,128)} %get-tuple-element.1208, f32[16,257,512]{2,1,0:T(8,128)} %get-tuple-element.1221, f32[16,256,513]{2,1,0:T(8,128)} %get-tuple-element.1219, f32[16,256,512]{2,1,0:T(8,128)} %param.28, s32[256,512]{1,0:T(8,128)S(1)} %get-tuple-element.1186, ...), kind=kLoop, calls=%fused_computation.142 | loop fusion | flops 46137344 | bytes 126877696 | tf_op jit(solution)/shard_map/mul | solution.py:100
  514.3 46.9 %while.158 = (s32[]{:T(128)}, f32[256,512]{1,0:T(8,128)S(1)}, f32[256,512]{1,0:T(8,128)S(1)}, f32[16,256,512]{2,1,0:T(8,128)}, f32[16,256,512]{2,1,0:T(8,128)}, ...) while((s32[]{:T(128)}, f32[256,512]{1,0:T(8,128)S(1)}, ...), condition=%wide.region_10.11_spmd.clone, body=%wide.region_9.10_spmd.clone.sunk | while | flops 1048579 | bytes 5243511 | solution.py:44
  565.4 39.5 %while.159 = (s32[]{:T(128)}, f32[256,512]{1,0:T(8,128)S(1)}, f32[16,256,512]{2,1,0:T(8,128)}, f32[16,256,512]{2,1,0:T(8,128)}, f32[16,256,512]{2,1,0:T(8,128)}, /*index=5*/s32[]{:T(128)}, s32[]{:T(128)}, s32[]{:T(128)}) while((s32[]{:T(128)}, f32[256,512]{1,0:T(8,128)S(1)}, f32[16,256,512]{2,1,0:T(8,128)}, ...), condition=%wide.region_12.13_spmd.clone, body=%wide.region_11.12_spmd.clone.sunk | while | flops 393220 | bytes 2621551 | solution.py:51
  604.9 8.1 multiply_reduce_fusion.1
  621.9 46.9 %while.160 = (s32[]{:T(128)}, f32[256,512]{1,0:T(8,128)S(1)}, f32[256,512]{1,0:T(8,128)S(1)}, f32[16,256,512]{2,1,0:T(8,128)}, f32[16,256,512]{2,1,0:T(8,128)}, ...) while((s32[]{:T(128)}, f32[256,512]{1,0:T(8,128)S(1)}, ...), condition=%wide.region_15.16_spmd.clone, body=%wide.region_14.15_spmd.clone.sunk | while | flops 1048579 | bytes 5243511 | solution.py:44
  673.3 39.3 %while.161 = (s32[]{:T(128)}, f32[256,512]{1,0:T(8,128)S(1)}, f32[16,256,512]{2,1,0:T(8,128)}, f32[16,256,512]{2,1,0:T(8,128)}, f32[16,256,512]{2,1,0:T(8,128)}, /*index=5*/s32[]{:T(128)}, s32[]{:T(128)}, s32[]{:T(128)}) while((s32[]{:T(128)}, f32[256,512]{1,0:T(8,128)S(1)}, f32[16,256,512]{2,1,0:T(8,128)}, ...), condition=%wide.region_17.18_spmd.clone, body=%wide.region_16.17_spmd.clone.sunk | while | flops 393220 | bytes 2621551 | solution.py:51
  712.6 8.2 multiply_reduce_fusion
  721.9 1070.6 %while.162 = (s32[]{:T(128)}, f32[256,512]{1,0:T(8,128)S(1)}, f32[2,256,512]{2,1,0:T(8,128)S(1)}, f32[2,256,512]{2,1,0:T(8,128)}, f32[256,512]{1,0:T(8,128)}, /*...) while((s32[]{:T(128)}, f32[256,512]{1,0:T(8,128)S(1)}, ...), condition=%wide.region_20.21_spmd.clone, body=%wide.region_19.20_spmd.clone.sunk | while | flops 4721683 | bytes 15812171 | solution.py:123
  1794.5 9.7 add_select_fusion
  1804.2 9.9 pad_maximum_fusion.31
  1826.4 10.1 fusion.37
  1842.7 27.3 %fusion.29 = f32[2,16,256,513]{3,2,1,0:T(8,128)} fusion(f32[5,16,256,1]{3,2,1,0:T(8,128)} %copy.21, f32[5,16,256,512]{3,2,1,0:T(8,128)} %constant_dynamic-update-slice_fusion, f32[5,16,256,1]{3,2,1,0:T(8,128)} %copy.20, f32[16,256,513]{2,1,0:T(8,128)} %fusion.37), kind=kLoop, calls=%fused_computation.77 | loop fusion | flops 16809984 | bytes 67321856 | tf_op jit(solution)/shard_map/mul | solution.py:132
  1874.6 20.3 %fusion.31 = f32[2,16,257,512]{3,2,1,0:T(8,128)} fusion(f32[5,16,1,514]{3,2,1,0:T(1,128)S(1)} %copy-done.23, f32[5,16,256,1]{3,2,1,0:T(8,128)} %copy.21, f32[5,16,256,512]{3,2,1,0:T(8,128)} %constant_dynamic-update-slice_fusion, f32[5,16,256,1]{3,2,1,0:T(8,128)S(1)} %bitcast.257, f32[5,16,1,514]{3,2,1,0:T(1,128)S(1)} %copy-done.21, f32[16,257,512]{2,1,0:T(8,128)} %fusion.44), kind=kLoop, calls=%fused_computation.81 | loop fusion | flops 33685504 | bytes 67699968 | tf_op jit(solution)/shard_map/mul | solution.py:133
  1894.9 38.2 %fusion.34 = f32[2,16,256,512]{3,2,1,0:T(8,128)} fusion(f32[2,16,257,512]{3,2,1,0:T(8,128)} %fusion.31, f32[2,16,256,513]{3,2,1,0:T(8,128)} %fusion.29, f32[1,16,256,512]{3,2,1,0:T(8,128)} %bitcast.272, f32[1,16,256,512]{3,2,1,0:T(8,128)} %bitcast.273, f32[16,256,512]{2,1,0:T(8,128)} %fusion.60), kind=kLoop, calls=%fused_computation.90 | loop fusion | flops 29360128 | bytes 109051904 | tf_op jit(solution)/shard_map/mul | solution.py:135
  1933.1 10.7 slice_bitcast_fusion
  (890 shorter events, 1574.4 us)
Async XLA Ops:
  1.7 24.2 %collective-permute-start.6 = (s32[256,1]{1,0:T(8,128)S(1)}, s32[256,1]{1,0:T(8,128)S(1)}, u32[]{:S(2)}, u32[]{:S(2)}) collective-permute-start(s32[256,1]{1,0:T(8,128)S(1)} %get-tuple-element.1249), channel_id=1, source_target_pairs={{0,6},{2,0},{4,2},{6,4},{1,7},{3,1},{5,3},{7,5}} | collective-permute-start | bytes 3080 | tf_op jit(solution)/shard_map/ppermute | solution.py:165
  6.0 19.9 %collective-permute-start.7 = (s32[256,1]{1,0:T(8,128)S(1)}, s32[256,1]{1,0:T(8,128)S(1)}, u32[]{:S(2)}, u32[]{:S(2)}) collective-permute-start(s32[256,1]{1,0:T(8,128)S(1)} %get-tuple-element.1248), channel_id=1, source_target_pairs={{0,2},{2,4},{4,6},{6,0},{1,3},{3,5},{5,7},{7,1}} | collective-permute-start | bytes 3080 | tf_op jit(solution)/shard_map/ppermute | solution.py:166
  7.1 23.2 %collective-permute-start.10 = (f32[256,1]{1,0:T(8,128)S(1)}, f32[256,1]{1,0:T(8,128)S(1)}, u32[]{:S(2)}, u32[]{:S(2)}) collective-permute-start(f32[256,1]{1,0:T(8,128)S(1)} %get-tuple-element.1251), channel_id=1, source_target_pairs={{0,6},{2,0},{4,2},{6,4},{1,7},{3,1},{5,3},{7,5}} | collective-permute-start | bytes 3080 | tf_op jit(solution)/shard_map/ppermute | solution.py:165
  10.0 20.3 %collective-permute-start.9 = (f32[256,1]{1,0:T(8,128)S(1)}, f32[256,1]{1,0:T(8,128)S(1)}, u32[]{:S(2)}, u32[]{:S(2)}) collective-permute-start(f32[256,1]{1,0:T(8,128)S(1)} %get-tuple-element.1250), channel_id=1, source_target_pairs={{0,2},{2,4},{4,6},{6,0},{1,3},{3,5},{5,7},{7,1}} | collective-permute-start | bytes 3080 | tf_op jit(solution)/shard_map/ppermute | solution.py:166
  324.6 39.2 %collective-permute-start.14 = (f32[5,16,256,1]{2,1,3,0:T(8,128)S(1)}, f32[5,16,256,1]{2,1,3,0:T(8,128)S(1)}, u32[]{:S(2)}, u32[]{:S(2)}) collective-permute-start(f32[5,16,256,1]{2,1,3,0:T(8,128)S(1)} %copy.18), channel_id=1, source_target_pairs={{0,2},{2,4},{4,6},{6,0},{1,3},{3,5},{5,7},{7,1}} | collective-permute-start | bytes 245768 | tf_op jit(solution)/shard_map/ppermute | solution.py:166
  332.5 36.6 %collective-permute-start.15 = (f32[5,16,256,1]{2,1,3,0:T(8,128)S(1)}, f32[5,16,256,1]{2,1,3,0:T(8,128)S(1)}, u32[]{:S(2)}, u32[]{:S(2)}) collective-permute-start(f32[5,16,256,1]{2,1,3,0:T(8,128)S(1)} %copy.19), channel_id=1, source_target_pairs={{0,6},{2,0},{4,2},{6,4},{1,7},{3,1},{5,3},{7,5}} | collective-permute-start | bytes 245768 | tf_op jit(solution)/shard_map/ppermute | solution.py:165
  864.7 14.2 collective-permute-start.1
  900.4 14.2 collective-permute-start.1
  936.0 14.2 collective-permute-start.1
  971.7 14.2 collective-permute-start.1
  1007.4 14.2 collective-permute-start.1
  1043.1 14.2 collective-permute-start.1
  1078.8 14.2 collective-permute-start.1
  1114.5 14.2 collective-permute-start.1
  1150.2 14.2 collective-permute-start.1
  1185.8 14.2 collective-permute-start.1
  1221.5 14.2 collective-permute-start.1
  1257.2 14.2 collective-permute-start.1
  1292.9 14.2 collective-permute-start.1
  1328.6 14.2 collective-permute-start.1
  1364.3 14.2 collective-permute-start.1
  1399.9 14.2 collective-permute-start.1
  1471.3 14.2 collective-permute-start.1
  1507.0 14.2 collective-permute-start.1
  1542.7 14.2 collective-permute-start.1
  1578.4 14.2 collective-permute-start.1
  1614.1 14.2 collective-permute-start.1
  1685.4 14.2 collective-permute-start.1
  1721.1 14.2 collective-permute-start.1
  1756.8 14.2 collective-permute-start.1
  1819.8 16.7 collective-permute-start.19
  1840.8 29.2 %collective-permute-start.20 = (f32[2,16,1,514]{3,2,1,0:T(1,128)S(1)}, f32[2,16,1,514]{3,2,1,0:T(1,128)S(1)}, u32[]{:S(2)}, u32[]{:S(2)}) collective-permute-start(f32[2,16,1,514]{3,2,1,0:T(1,128)S(1)} %pad_maximum_fusion.35), channel_id=1, source_target_pairs={{0,1},{2,3},{4,5},{6,7}} | collective-permute-start | bytes 197384 | tf_op jit(solution)/shard_map/ppermute | solution.py:169
  (200 other events, 1976.3 us)
where the time goes:
time: 1950 us; the launch traced here: 1940 us
  other arithmetic  880 us (45%)
  waiting for transfers between devices  654 us (34%)
  starting transfers between devices  224 us (11%)
  local copies, waits for them, and re-layouts  183 us (9%)
    dynamic_update_slice x128, other arithmetic, column_solve(): _, (gains, parts) = lax.scan(forward, start, (lower, diag, upper, source))  354 us
    ppermute x64, waiting for transfers between devices, halo_swap(): from_east = lax.ppermute(field[..., :1], 'col', east_perm)  345 us
    ppermute x64, waiting for transfers between devices, halo_swap(): from_west = lax.ppermute(field[..., -1:], 'col', west_perm)  250 us
    add x30, other arithmetic, substep(): return (eta_next, trans_next, trans_avg + weight * trans_next)  116 us
    ppermute x64, starting transfers between devices, halo_swap(): from_west = lax.ppermute(field[..., -1:], 'col', west_perm)  111 us
    another operation x12, local copies, waits for them, and re-layouts  53.1 us
    slice x65, local copies, waits for them, and re-layouts, halo_swap(): from_west = lax.ppermute(field[..., -1:], 'col', west_perm)  51.5 us
    ppermute x34, starting transfers between devices, halo_swap(): from_south = lax.ppermute(wide[..., -1:, :], 'row', south_perm)  46.6 us
  transfers between devices with their start and end apart: 195, of which 182 were waited for; matrix products, arithmetic and copies ran while one was open for 6% of the time, Pallas kernels for 0%

commit v1 on v0

--- a/solution.py
+++ b/solution.py
@@ -1,6 +1,10 @@
+import functools
+
 import jax
 import jax.numpy as jnp
 from jax import lax
+from jax.experimental import pallas as pl
+from jax.experimental.pallas import tpu as pltpu
 from jax.sharding import PartitionSpec as P
 
 GRAVITY = 1.0
@@ -103,24 +107,148 @@
     return u_star, v_star, forcing, edges[3:], (mask_c, mask_u, mask_v)
 
 
-def barotropic(eta_start, trans_start, face_depth, face_wet, wet_cell, forcing, tide_force, halo_fn):
-    n_sub = tide_force.shape[0]
+NY = 256
+NX = 512
+WIDE = 32
+SUB = 36
+EXT_Y = 8 * SUB
+EXT_X = 640
+LANES = 128
+CHUNKS = EXT_X // LANES
+
+
+def east_of(x):
+    return pltpu.roll(x, EXT_X - 1, 1)
+
+
+def west_of(x):
+    return pltpu.roll(x, 1, 1)
+
+
+def north_wrap(x):
+    return pltpu.roll(x, 7, 0)
+
+
+def south_wrap(x):
+    return pltpu.roll(x, 1, 0)
+
+
+def barotropic_kernel(n_sub, planes_hbm, force_hbm, tide_ref, eta_hbm, u_hbm, v_hbm, ubar_hbm, vbar_hbm, nat, eta, u, v, au, fu, av, fv, ub, vb, sem, out_sem):
     dt_sub = TIME_STEP / n_sub
     weight_norm = 6.0 / (n_sub * (n_sub + 1) * (n_sub + 2))
-
-    def substep(step, carry):
-        eta_now, trans_now, trans_avg = carry
-        trans_ext = halo_fn(trans_now)
-        divergence = (trans_now[0] - trans_ext[0, 1:-1, :-2] + trans_now[1] - trans_ext[1, :-2, 1:-1]) / GRID_DX
-        eta_next = wet_cell * (eta_now - dt_sub * divergence)
-        eta_ext = halo_fn(eta_next)
-        slope = jnp.stack([eta_ext[1:-1, 2:] - eta_next, eta_ext[2:, 1:-1] - eta_next]) / GRID_DX
-        tide_now = lax.dynamic_index_in_dim(tide_force, step, 0, keepdims=False)
-        trans_next = face_wet * (trans_now + dt_sub * (face_depth * (tide_now[:, None, None] - GRAVITY * slope) + forcing))
-        weight = weight_norm * ((step + 1) * (n_sub - step)).astype(jnp.float32)
-        return eta_next, trans_next, trans_avg + weight * trans_next
-
-    return lax.fori_loop(0, n_sub, substep, (eta_start, trans_start, jnp.zeros_like(trans_start)))
+    row = lax.axis_index("row")
+
+    def load_copy(p, c):
+        src = planes_hbm.at[p, :, pl.ds(c * LANES, LANES)] if p < 5 else force_hbm.at[p - 5, :, pl.ds(c * LANES, LANES)]
+        return pltpu.make_async_copy(src, nat.at[p, c], sem.at[p, c])
+
+    for p in range(7):
+        for c in range(CHUNKS):
+            load_copy(p, c).start()
+    for p in range(7):
+        for c in range(CHUNKS):
+            load_copy(p, c).wait()
+
+    def plane(p, t):
+        return jnp.concatenate([nat[p, c, pl.ds(t, 8, stride=SUB), :] for c in range(CHUNKS)], axis=1)
+
+    cut = jnp.where(row == 0, EXT_Y - 1, NY - 1)
+    sub_id = lax.broadcasted_iota(jnp.int32, (8, EXT_X), 0)
+
+    def prepare(t, k_next, h_next):
+        k = plane(0, t)
+        dz = plane(1, t) / jnp.maximum(k, 1.0)
+        k_n = jnp.where(sub_id * SUB + t == cut, 0.0, k_next)
+        dz_n = h_next / jnp.maximum(k_next, 1.0)
+        k_e = east_of(k)
+        dz_e = east_of(dz)
+        k_u = jnp.minimum(k, k_e)
+        k_v = jnp.minimum(k, k_n)
+        depth_u = k_u * (0.5 * (dz + dz_e))
+        depth_v = k_v * (0.5 * (dz + dz_n))
+        wet_u = k_u > 0
+        wet_v = k_v > 0
+        eta[t] = jnp.where(k > 0, plane(2, t), 0.0)
+        u[t] = jnp.where(wet_u, dt_sub * plane(3, t), 0.0)
+        v[t] = jnp.where(wet_v, dt_sub * plane(4, t), 0.0)
+        au[t] = (dt_sub * dt_sub) * jnp.where(wet_u, depth_u, 0.0)
+        av[t] = (dt_sub * dt_sub) * jnp.where(wet_v, depth_v, 0.0)
+        fu[t] = jnp.where(wet_u, (dt_sub * dt_sub) * plane(5, t), 0.0)
+        fv[t] = jnp.where(wet_v, (dt_sub * dt_sub) * plane(6, t), 0.0)
+        ub[t] = jnp.zeros((8, EXT_X), jnp.float32)
+        vb[t] = jnp.zeros((8, EXT_X), jnp.float32)
+
+    @pl.loop(0, SUB - 1)
+    def _(t):
+        prepare(t, plane(0, t + 1), plane(1, t + 1))
+
+    prepare(SUB - 1, north_wrap(plane(0, 0)), north_wrap(plane(1, 0)))
+
+    @pl.loop(0, n_sub)
+    def _(n):
+        tide_x = tide_ref[n, 0]
+        tide_y = tide_ref[n, 1]
+        weight = (weight_norm / dt_sub) * ((n + 1) * (n_sub - n)).astype(jnp.float32)
+
+        def level(t, v_south):
+            u_now = u[t]
+            v_now = v[t]
+            return eta[t] - ((u_now - west_of(u_now)) + (v_now - v_south)), v_now
+
+        def accelerate(t, eta_now, eta_north):
+            u_new = u[t] + (au[t] * ((tide_x + eta_now) - east_of(eta_now)) + fu[t])
+            v_new = v[t] + (av[t] * ((tide_y + eta_now) - eta_north) + fv[t])
+            u[t] = u_new
+            v[t] = v_new
+            ub[t] = ub[t] + weight * u_new
+            vb[t] = vb[t] + weight * v_new
+
+        eta_first, v_first = level(0, south_wrap(v[SUB - 1]))
+        eta[0] = eta_first
+
+        def sweep(t, carry):
+            eta_now, v_now = carry
+            eta_north, v_north = level(t + 1, v_now)
+            eta[t + 1] = eta_north
+            accelerate(t, eta_now, eta_north)
+            return eta_north, v_north
+
+        eta_last, _ = lax.fori_loop(0, SUB - 1, sweep, (eta_first, v_first))
+        accelerate(SUB - 1, eta_last, north_wrap(eta_first))
+
+    @pl.loop(0, SUB)
+    def _(t):
+        wet = plane(0, t) > 0
+        for q, val in enumerate((jnp.where(wet, eta[t], 0.0), (1.0 / dt_sub) * u[t], (1.0 / dt_sub) * v[t], ub[t], vb[t])):
+            for c in range(4):
+                nat[q, c, pl.ds(t, 8, stride=SUB), :] = val[:, c * LANES : (c + 1) * LANES]
+
+    outs = (eta_hbm, u_hbm, v_hbm, ubar_hbm, vbar_hbm)
+
+    def store_copy(q, c):
+        return pltpu.make_async_copy(nat.at[q, c, pl.ds(0, NY), :], outs[q].at[:, pl.ds(c * LANES, LANES)], out_sem.at[q, c])
+
+    for q in range(5):
+        for c in range(4):
+            store_copy(q, c).start()
+    for q in range(5):
+        for c in range(4):
+            store_copy(q, c).wait()
+
+
+def barotropic(planes, force, tide_force):
+    n_sub = tide_force.shape[0]
+    big = pltpu.VMEM((SUB, 8, EXT_X), jnp.float32)
+    out = jax.ShapeDtypeStruct((NY, NX), jnp.float32)
+    return pl.pallas_call(
+        functools.partial(barotropic_kernel, n_sub),
+        out_shape=[out] * 5,
+        in_specs=[pl.BlockSpec(memory_space=pl.ANY)] * 2 + [pl.BlockSpec(memory_space=pltpu.SMEM)],
+        out_specs=[pl.BlockSpec(memory_space=pl.ANY)] * 5,
+        scratch_shapes=[pltpu.VMEM((7, CHUNKS, EXT_Y, LANES), jnp.float32)] + [big] * 9 + [pltpu.SemaphoreType.DMA((7, CHUNKS)), pltpu.SemaphoreType.DMA((5, 4))],
+        compiler_params=pltpu.CompilerParams(vmem_limit_bytes=40 * 1024 * 1024),
+        name="barotropic",
+    )(planes, force, tide_force)
 
 
 def correct_velocity(star, dz_face, depth_face, mean_trans, mask):
@@ -144,13 +272,15 @@
     return vel_uc, vel_vc, tracers[0], tracers[1]
 
 
-def ocean_step(vel_u, vel_v, value_a11, salinity, sea_level, trans_u, trans_v, bathymetry, kmt_levels, tide_force, halo_fn):
+def ocean_step(vel_u, vel_v, value_a11, salinity, sea_level, trans_u, trans_v, bathymetry, kmt_levels, tide_force, halo_fn, wide_fn):
     layout = geometry(halo_fn(kmt_levels), halo_fn(bathymetry))
+    planes = wide_fn(jnp.stack([kmt_levels.astype(jnp.float32), bathymetry, sea_level, trans_u, trans_v]))
     u_star, v_star, forcing, tracer_ext, masks = baroclinic_predict(vel_u, vel_v, value_a11, salinity, layout, halo_fn)
     face_depth, face_wet, wet_cell = surface_fields(layout)
-    eta_new, trans_new, trans_avg = barotropic(wet_cell * sea_level, face_wet * jnp.stack([trans_u, trans_v]), face_depth, face_wet, wet_cell, forcing, tide_force, halo_fn)
+    eta_new, u_new, v_new, u_avg, v_avg = barotropic(planes, wide_fn(forcing), tide_force)
+    trans_avg = (u_avg, v_avg)
     vel_uc, vel_vc, temp_new, salt_new = baroclinic_finish(u_star, v_star, trans_avg, face_depth, layout, tracer_ext, masks, halo_fn)
-    return eta_new, trans_new[0], trans_new[1], vel_uc, vel_vc, temp_new, salt_new
+    return eta_new, u_new, v_new, vel_uc, vel_vc, temp_new, salt_new
 
 
 def solution(mesh):
@@ -169,8 +299,17 @@
         from_south = lax.ppermute(wide[..., -1:, :], "row", south_perm)
         return jnp.concatenate([from_south, wide, from_north], axis=-2)
 
+    def wide_swap(field):
+        from_east = lax.ppermute(field[..., :WIDE], "col", east_perm)
+        from_west = lax.ppermute(field[..., -WIDE:], "col", west_perm)
+        gap = jnp.zeros(field.shape[:-1] + (EXT_X - NX - 2 * WIDE,), field.dtype)
+        wide = jnp.concatenate([field, from_east, gap, from_west], axis=-1)
+        edge = jnp.where(lax.axis_index("row") == 0, wide[..., -WIDE:, :], wide[..., :WIDE, :])
+        other = lax.ppermute(edge, "row", [(0, 1), (1, 0)])
+        return jnp.concatenate([wide, other], axis=-2)
+
     def local_step(vel_u, vel_v, value_a11, salinity, sea_level, trans_u, trans_v, bathymetry, kmt_levels, tide_force):
-        return ocean_step(vel_u, vel_v, value_a11, salinity, sea_level, trans_u, trans_v, bathymetry, kmt_levels, tide_force, halo_swap)
+        return ocean_step(vel_u, vel_v, value_a11, salinity, sea_level, trans_u, trans_v, bathymetry, kmt_levels, tide_force, halo_swap, wide_swap)
 
     spec_cube = P(None, "row", "col")
     spec_plane = P("row", "col")

time: 1950 us -> 1020 us (0.52)
  waiting for transfers between devices: 654 us -> 12.8 us
  starting transfers between devices: 224 us -> 29.6 us
  other arithmetic: 880 us -> 717 us
  Pallas kernels: 0 us -> 105 us
  local copies, waits for them, and re-layouts: 183 us -> 149 us
    ppermute x64 -> x4, waiting for transfers between devices: 345 us -> 0.01 us  [halo_swap(): from_east = lax.ppermute(field[..., :1], 'col', east_perm)]
    ppermute x64 -> x4, waiting for transfers between devices: 250 us -> 0.01 us  [halo_swap(): from_west = lax.ppermute(field[..., -1:], 'col', west_perm)]
    add x31 -> x0, other arithmetic: 118 us -> none  [the longest x30 116 us: substep(): return (eta_next, trans_next, trans_avg + weight * trans_next)]
    ppermute x64 -> x4, starting transfers between devices: 111 us -> 4.96 us  [halo_swap(): from_west = lax.ppermute(field[..., -1:], 'col', west_perm)]
    pallas_call x0 -> x1, Pallas kernels: none -> 105 us  [barotropic(): pl.pallas_call(functools.partial(barotropic_kernel, n_sub), out_shape=[ou...]
    mul x32 -> x0, other arithmetic: 45.2 us -> none  [the longest x30 43.9 us: substep(): eta_next = wet_cell * (eta_now - dt_sub * divergence)]
    ppermute x34 -> x4, starting transfers between devices: 46.6 us -> 7.71 us  [halo_swap(): from_south = lax.ppermute(wide[..., -1:, :], 'row', south_perm)]
    ppermute x33 -> x3, starting transfers between devices: 42.4 us -> 3.87 us  [halo_swap(): from_north = lax.ppermute(wide[..., :1, :], 'row', north_perm)]
  transfers between devices with their start and end apart: 195 -> 21, of which waited for: 182 -> 3; matrix products, arithmetic and copies ran while one was open for 6% -> 12% of each run, Pallas kernels for 0% -> 0%
where the time goes in v1:
time: 1020 us
  other arithmetic  717 us (70%)
  local copies, waits for them, and re-layouts  149 us (15%)
  Pallas kernels  105 us (10%)
  starting transfers between devices  29.6 us (3%)
  waiting for transfers between devices  12.8 us (1%)
    dynamic_update_slice x128, other arithmetic, column_solve(): _, (gains, parts) = lax.scan(forward, start, (lower, diag, upper, source))  353 us
    pallas_call x1, Pallas kernels, barotropic(): pl.pallas_call(functools.partial(barotropic_kernel, n_sub), out_shape=[ou...  105 us
    another operation x12, local copies, waits for them, and re-layouts  53 us
    mul x1, other arithmetic, baroclinic_predict(): mask_u * (vel_um + TIME_STEP * tend_u)  45 us
    mul x1, other arithmetic, advect_tracers(): return mask_c * (tracer_ext[..., 1:-1, 1:-1] - TIME_STEP * divergence)  38.2 us
    mul x2, other arithmetic, advect_tracers(): flow_ext[0, :, 1:-1, :-1]  37.4 us
    concatenate x2, other arithmetic, column_solve(): lower = jnp.concatenate([edge, couple], axis=0)  36.9 us
    mul x1, other arithmetic, momentum_tend(): flux_vu = corner_v * corner_u  28.4 us
  transfers between devices with their start and end apart: 21, of which 3 were waited for; matrix products, arithmetic and copies ran while one was open for 12% of the time, Pallas kernels for 0%

profile of v1, /device:TPU:0, one launch (start us, length us, event | category | flops | bytes accessed | tf_op | source)
XLA Modules:
  0.0 1015.2 jit_solution(3067121747843645478)
XLA Ops:
  13.9 11.3 %fusion.45 = (f32[16,256,512]{2,1,0:T(8,128)}, f32[16,256,512]{2,1,0:T(8,128)}) fusion(f32[16,256,512]{2,1,0:T(8,128)} %param.29, s32[256,512]{1,0:T(8,128)} %param.34, f32[16,256,512]{2,1,0:T(8,128)} %param.28), kind=kLoop, calls=%fused_computation.129 | loop fusion | flops 6291456 | bytes 34078720 | tf_op jit(solution)/shard_map/mul | solution.py:101
  40.0 7.6 compare_select_fusion.2
  47.6 22.4 %fusion.77 = (f32[16,256,512]{2,1,0:T(8,128)}, f32[16,256,512]{2,1,0:T(8,128)}, f32[16,256,512]{2,1,0:T(8,128)}, f32[16,256,512]{2,1,0:T(8,128)}, f32[16,256,512]{2,1,0:T(8,128)}, /*index=5*/f32[16,256,512]{2,1,0:T(8,128)}) fusion(f32[15,256,512]{2,1,0:T(8,128)S(1)} %get-tuple-element.1026, f32[15,256,512]{2,1,0:T(8,128)} %get-tuple-element.1027), kind=kLoop, calls=%fused_computation.202 | loop fusion | flops 8388608 | bytes 66060288 | tf_op jit(solution)/shard_map/concatenate | solution.py:36
  78.9 55.8 %while.138 = (s32[]{:T(128)}, f32[256,512]{1,0:T(8,128)}, f32[256,512]{1,0:T(8,128)}, f32[16,256,512]{2,1,0:T(8,128)}, f32[16,256,512]{2,1,0:T(8,128)}, /*index=...) while((s32[]{:T(128)}, f32[256,512]{1,0:T(8,128)}, ...), condition=%wide.region_6.7_spmd.clone, body=%wide.region_5.6_spmd.clone.sunk | while | flops 1048579 | bytes 5243511 | solution.py:48
  139.2 39.5 %while.139 = (s32[]{:T(128)}, f32[256,512]{1,0:T(8,128)S(1)}, f32[16,256,512]{2,1,0:T(8,128)}, f32[16,256,512]{2,1,0:T(8,128)}, f32[16,256,512]{2,1,0:T(8,128)}, /*index=5*/s32[]{:T(128)}, s32[]{:T(128)}, s32[]{:T(128)}) while((s32[]{:T(128)}, f32[256,512]{1,0:T(8,128)S(1)}, f32[16,256,512]{2,1,0:T(8,128)}, ...), condition=%wide.region_8.9_spmd.clone, body=%wide.region_7.8_spmd.clone.sunk | while | flops 393220 | bytes 2621551 | solution.py:55
  187.6 46.3 %while.136 = (s32[]{:T(128)}, f32[256,512]{1,0:T(8,128)S(1)}, f32[256,512]{1,0:T(8,128)S(1)}, f32[16,256,512]{2,1,0:T(8,128)}, f32[16,256,512]{2,1,0:T(8,128)}, ...) while((s32[]{:T(128)}, f32[256,512]{1,0:T(8,128)S(1)}, ...), condition=%wide.region_2.3_spmd.clone, body=%wide.region_1.2_spmd.clone.sunk | while | flops 1048579 | bytes 5243511 | solution.py:48
  238.2 39.5 %while.137 = (s32[]{:T(128)}, f32[256,512]{1,0:T(8,128)S(1)}, f32[16,256,512]{2,1,0:T(8,128)}, f32[16,256,512]{2,1,0:T(8,128)}, f32[16,256,512]{2,1,0:T(8,128)}, /*index=5*/s32[]{:T(128)}, s32[]{:T(128)}, s32[]{:T(128)}) while((s32[]{:T(128)}, f32[256,512]{1,0:T(8,128)S(1)}, f32[16,256,512]{2,1,0:T(8,128)}, ...), condition=%wide.region_4.5_spmd.clone, body=%wide.region_3.4_spmd.clone.sunk | while | flops 393220 | bytes 2621551 | solution.py:55
  277.7 8.4 bitcast_dynamic-update-slice_fusion.14
  286.1 8.4 bitcast_dynamic-update-slice_fusion.13
  294.5 6.8 bitcast_dynamic-update-slice_fusion.12
  301.3 8.0 constant_dynamic-update-slice_fusion.1
  309.3 8.0 constant_dynamic-update-slice_fusion
  317.3 16.0 %fusion.76 = (f32[5,16,256,1]{3,2,1,0:T(8,128)}, f32[5,16,256,1]{3,2,1,0:T(8,128)}) fusion(f32[5,16,256,512]{3,2,1,0:T(8,128)} %constant_dynamic-update-slice_fusion), kind=kLoop, calls=%fused_computation.201 | loop fusion | bytes 327680 | tf_op jit(solution)/shard_map/slice | solution.py:296
  333.3 6.0 copy.22
  370.2 14.5 %fusion.79 = (f32[16,256,512]{2,1,0:T(8,128)}, f32[16,256,512]{2,1,0:T(8,128)}, f32[16,256,512]{2,1,0:T(8,128)}) fusion(f32[15,256,512]{2,1,0:T(8,128)} %get-tuple-element.1028), kind=kLoop, calls=%fused_computation.204 | loop fusion | flops 4194304 | bytes 33030144 | tf_op jit(solution)/shard_map/concatenate | solution.py:36
  388.8 25.3 %maximum_bitcast_fusion.1 = (f32[16,258,514]{2,1,0:T(8,128)S(1)}, f32[16,258,514]{2,1,0:T(8,128)}, f32[16,258,514]{2,1,0:T(8,128)}) fusion(f32[5,16,1,514]{3,2,1,0:T(1,128)S(1)} %collective-permute-done.14, f32[5,16,1,514]{3,2,1,0:T(1,128)S(1)} %collective-permute-done.13, f32[5,16,256,1]{3,2,1,0:T(8,128)} %copy.25, ...), kind=kLoop, calls=%fused_computation.68 | loop fusion | flops 25461504 | bytes 67897344 | tf_op jit(solution)/shard_map/squeeze | solution.py:103
  418.1 19.6 %fusion.26 = (f32[16,256,513]{2,1,0:T(8,128)}, f32[16,256,513]{2,1,0:T(8,128)}) fusion(f32[16,258,514]{2,1,0:T(8,128)S(1)} %get-tuple-element.979, f32[16,258,514]{2,1,0:T(8,128)} %get-tuple-element.980), kind=kLoop, calls=%fused_computation.80 | loop fusion | flops 16809984 | bytes 58834944 | tf_op jit(solution)/shard_map/mul | solution.py:78
  437.6 28.4 %fusion.32 = (f32[16,257,512]{2,1,0:T(8,128)}, f32[16,257,512]{2,1,0:T(8,128)}) fusion(f32[16,258,514]{2,1,0:T(8,128)} %copy-done, f32[16,258,514]{2,1,0:T(8,128)} %get-tuple-element.980), kind=kLoop, calls=%fused_computation.92 | loop fusion | flops 16842752 | bytes 58949632 | tf_op jit(solution)/shard_map/mul | solution.py:79
  466.0 45.0 %fusion.43 = (f32[16,256,512]{2,1,0:T(8,128)}, f32[16,256,512]{2,1,0:T(8,128)}) fusion(f32[16,258,514]{2,1,0:T(8,128)} %get-tuple-element.981, f32[16,257,512]{2,1,0:T(8,128)} %get-tuple-element.994, f32[16,256,513]{2,1,0:T(8,128)} %get-tuple-element.992, f32[16,256,512]{2,1,0:T(8,128)} %param.26, s32[256,512]{1,0:T(8,128)S(1)} %get-tuple-element.967, ...), kind=kLoop, calls=%fused_computation.111 | loop fusion | flops 46137344 | bytes 126877696 | tf_op jit(solution)/shard_map/mul | solution.py:104
  519.7 46.6 %while.140 = (s32[]{:T(128)}, f32[256,512]{1,0:T(8,128)S(1)}, f32[256,512]{1,0:T(8,128)S(1)}, f32[16,256,512]{2,1,0:T(8,128)}, f32[16,256,512]{2,1,0:T(8,128)}, ...) while((s32[]{:T(128)}, f32[256,512]{1,0:T(8,128)S(1)}, ...), condition=%wide.region_10.11_spmd.clone, body=%wide.region_9.10_spmd.clone.sunk | while | flops 1048579 | bytes 5243511 | solution.py:48
  570.7 39.5 %while.141 = (s32[]{:T(128)}, f32[256,512]{1,0:T(8,128)S(1)}, f32[16,256,512]{2,1,0:T(8,128)}, f32[16,256,512]{2,1,0:T(8,128)}, f32[16,256,512]{2,1,0:T(8,128)}, /*index=5*/s32[]{:T(128)}, s32[]{:T(128)}, s32[]{:T(128)}) while((s32[]{:T(128)}, f32[256,512]{1,0:T(8,128)S(1)}, f32[16,256,512]{2,1,0:T(8,128)}, ...), condition=%wide.region_12.13_spmd.clone, body=%wide.region_11.12_spmd.clone.sunk | while | flops 393220 | bytes 2621551 | solution.py:55
  619.1 46.4 %while.142 = (s32[]{:T(128)}, f32[256,512]{1,0:T(8,128)S(1)}, f32[256,512]{1,0:T(8,128)S(1)}, f32[16,256,512]{2,1,0:T(8,128)}, f32[16,256,512]{2,1,0:T(8,128)}, ...) while((s32[]{:T(128)}, f32[256,512]{1,0:T(8,128)S(1)}, ...), condition=%wide.region_15.16_spmd.clone, body=%wide.region_14.15_spmd.clone.sunk | while | flops 1048579 | bytes 5243511 | solution.py:48
  670.0 39.3 %while.143 = (s32[]{:T(128)}, f32[256,512]{1,0:T(8,128)S(1)}, f32[16,256,512]{2,1,0:T(8,128)}, f32[16,256,512]{2,1,0:T(8,128)}, f32[16,256,512]{2,1,0:T(8,128)}, /*index=5*/s32[]{:T(128)}, s32[]{:T(128)}, s32[]{:T(128)}) while((s32[]{:T(128)}, f32[256,512]{1,0:T(8,128)S(1)}, f32[16,256,512]{2,1,0:T(8,128)}, ...), condition=%wide.region_17.18_spmd.clone, body=%wide.region_16.17_spmd.clone.sunk | while | flops 393220 | bytes 2621551 | solution.py:55
  709.4 8.2 multiply_reduce_fusion.1
  732.5 7.0 collective-permute-done.16
  750.8 105.0 %barotropic.1 = (f32[256,512]{1,0:T(8,128)}, f32[256,512]{1,0:T(8,128)}, f32[256,512]{1,0:T(8,128)}, f32[256,512]{1,0:T(8,128)S(1)}, f32[256,512]{1,0:T(8,128)S(1)}) custom-call(f32[5,288,640]{2,1,0:T(8,128)S(1)} %pad_maximum_fusion.20.planes_hbm, f32[2,288,640]{2,1,0:T(8,128)S(1)} %pad_maximum_fusion.21.force_hbm, f32[30,2]{1,0:T(8,128)S(1)} %copy.26.tide_ref), custom_call_target="tpu_custom_call" | custom-call | tf_op jit(solution)/shard_map/barotropic/pallas_call | solution.py:243
  880.8 8.0 add_select_fusion.1
  897.2 10.1 fusion.21
  913.7 27.3 %fusion.13 = f32[2,16,256,513]{3,2,1,0:T(8,128)} fusion(f32[5,16,256,1]{3,2,1,0:T(8,128)} %copy.25, f32[5,16,256,512]{3,2,1,0:T(8,128)} %constant_dynamic-update-slice_fusion, f32[5,16,256,1]{3,2,1,0:T(8,128)} %copy.24, f32[16,256,513]{2,1,0:T(8,128)} %fusion.21), kind=kLoop, calls=%fused_computation.46 | loop fusion | flops 16809984 | bytes 67321856 | tf_op jit(solution)/shard_map/mul | solution.py:260
  945.5 20.3 %fusion.15 = f32[2,16,257,512]{3,2,1,0:T(8,128)} fusion(f32[5,16,1,514]{3,2,1,0:T(1,128)S(1)} %copy-done.28, f32[5,16,256,1]{3,2,1,0:T(8,128)} %copy.25, f32[5,16,256,512]{3,2,1,0:T(8,128)} %constant_dynamic-update-slice_fusion, f32[5,16,256,1]{3,2,1,0:T(8,128)S(1)} %bitcast.241, f32[5,16,1,514]{3,2,1,0:T(1,128)S(1)} %copy-done.26, f32[16,257,512]{2,1,0:T(8,128)} %fusion.28), kind=kLoop, calls=%fused_computation.50 | loop fusion | flops 33685504 | bytes 67699968 | tf_op jit(solution)/shard_map/mul | solution.py:261
  965.8 38.2 %fusion.18 = f32[2,16,256,512]{3,2,1,0:T(8,128)} fusion(f32[2,16,257,512]{3,2,1,0:T(8,128)} %fusion.15, f32[2,16,256,513]{3,2,1,0:T(8,128)} %fusion.13, f32[1,16,256,512]{3,2,1,0:T(8,128)} %bitcast.250, f32[1,16,256,512]{3,2,1,0:T(8,128)} %bitcast.251, f32[16,256,512]{2,1,0:T(8,128)} %fusion.44), kind=kLoop, calls=%fused_computation.59 | loop fusion | flops 29360128 | bytes 109051904 | tf_op jit(solution)/shard_map/mul | solution.py:263
  1004.0 10.7 %slice_bitcast_fusion = (f32[16,256,512]{2,1,0:T(8,128)}, f32[16,256,512]{2,1,0:T(8,128)}) fusion(f32[2,16,256,512]{3,2,1,0:T(8,128)} %fusion.18), kind=kLoop, calls=%fused_computation.95 | loop fusion | bytes 33554432 | tf_op jit(solution)/shard_map/squeeze | solution.py:272
  (330 shorter events, 542.8 us)
Async XLA Ops:
  1.7 26.0 %collective-permute-start.7 = (s32[256,1]{1,0:T(8,128)S(1)}, s32[256,1]{1,0:T(8,128)S(1)}, u32[]{:S(2)}, u32[]{:S(2)}) collective-permute-start(s32[256,1]{1,0:T(8,128)S(1)} %get-tuple-element.1024), channel_id=1, source_target_pairs={{0,2},{2,4},{4,6},{6,0},{1,3},{3,5},{5,7},{7,1}} | collective-permute-start | bytes 3080 | tf_op jit(solution)/shard_map/ppermute | solution.py:296
  5.1 22.7 %collective-permute-start.8 = (s32[256,1]{1,0:T(8,128)S(1)}, s32[256,1]{1,0:T(8,128)S(1)}, u32[]{:S(2)}, u32[]{:S(2)}) collective-permute-start(s32[256,1]{1,0:T(8,128)S(1)} %get-tuple-element.1025), channel_id=1, source_target_pairs={{0,6},{2,0},{4,2},{6,4},{1,7},{3,1},{5,3},{7,5}} | collective-permute-start | bytes 3080 | tf_op jit(solution)/shard_map/ppermute | solution.py:295
  7.1 25.1 %collective-permute-start.3 = (f32[256,1]{1,0:T(8,128)S(1)}, f32[256,1]{1,0:T(8,128)S(1)}, u32[]{:S(2)}, u32[]{:S(2)}) collective-permute-start(f32[256,1]{1,0:T(8,128)S(1)} %get-tuple-element.1022), channel_id=1, source_target_pairs={{0,2},{2,4},{4,6},{6,0},{1,3},{3,5},{5,7},{7,1}} | collective-permute-start | bytes 3080 | tf_op jit(solution)/shard_map/ppermute | solution.py:296
  8.2 24.0 %collective-permute-start.4 = (f32[256,1]{1,0:T(8,128)S(1)}, f32[256,1]{1,0:T(8,128)S(1)}, u32[]{:S(2)}, u32[]{:S(2)}) collective-permute-start(f32[256,1]{1,0:T(8,128)S(1)} %get-tuple-element.1023), channel_id=1, source_target_pairs={{0,6},{2,0},{4,2},{6,4},{1,7},{3,1},{5,3},{7,5}} | collective-permute-start | bytes 3080 | tf_op jit(solution)/shard_map/ppermute | solution.py:295
  27.9 7.1 collective-permute-start.10
  29.2 5.8 collective-permute-start.9
  32.3 2.7 collective-permute-start.5
  33.6 3.1 collective-permute-start.6
  339.3 13.6 %collective-permute-start.11 = (f32[5,16,256,1]{2,1,3,0:T(8,128)S(1)}, f32[5,16,256,1]{2,1,3,0:T(8,128)S(1)}, u32[]{:S(2)}, u32[]{:S(2)}) collective-permute-start(f32[5,16,256,1]{2,1,3,0:T(8,128)S(1)} %copy.22), channel_id=1, source_target_pairs={{0,2},{2,4},{4,6},{6,0},{1,3},{3,5},{5,7},{7,1}} | collective-permute-start | bytes 245768 | tf_op jit(solution)/shard_map/ppermute | solution.py:296
  345.9 12.6 %collective-permute-start.12 = (f32[5,16,256,1]{2,1,3,0:T(8,128)S(1)}, f32[5,16,256,1]{2,1,3,0:T(8,128)S(1)}, u32[]{:S(2)}, u32[]{:S(2)}) collective-permute-start(f32[5,16,256,1]{2,1,3,0:T(8,128)S(1)} %copy.23), channel_id=1, source_target_pairs={{0,6},{2,0},{4,2},{6,4},{1,7},{3,1},{5,3},{7,5}} | collective-permute-start | bytes 245768 | tf_op jit(solution)/shard_map/ppermute | solution.py:295
  350.1 34.7 %collective-permute-start = (f32[5,256,32]{1,2,0:T(8,128)S(1)}, f32[5,256,32]{1,2,0:T(8,128)}, u32[]{:S(2)}, u32[]{:S(2)}) collective-permute-start(f32[5,256,32]{1,2,0:T(8,128)S(1)} %copy.18), channel_id=1, source_target_pairs={{0,6},{2,0},{4,2},{6,4},{1,7},{3,1},{5,3},{7,5}} | collective-permute-start | bytes 491528 | tf_op jit(solution)/shard_map/ppermute | solution.py:303
  351.5 35.3 %collective-permute-start.1 = (f32[5,256,32]{1,2,0:T(8,128)}, f32[5,256,32]{1,2,0:T(8,128)}, u32[]{:S(2)}, u32[]{:S(2)}) collective-permute-start(f32[5,256,32]{1,2,0:T(8,128)} %copy.19), channel_id=1, source_target_pairs={{0,2},{2,4},{4,6},{6,0},{1,3},{3,5},{5,7},{7,1}} | collective-permute-start | bytes 491528 | tf_op jit(solution)/shard_map/ppermute | solution.py:304
  367.6 21.1 %collective-permute-start.13 = (f32[5,16,1,514]{3,2,1,0:T(1,128)}, f32[5,16,1,514]{3,2,1,0:T(1,128)S(1)}, u32[]{:S(2)}, u32[]{:S(2)}) collective-permute-start(f32[5,16,1,514]{3,2,1,0:T(1,128)} %get-tuple-element.982), channel_id=1, source_target_pairs={{0,1},{2,3},{4,5},{6,7}} | collective-permute-start | bytes 493448 | tf_op jit(solution)/shard_map/ppermute | solution.py:299
  368.9 19.8 %collective-permute-start.14 = (f32[5,16,1,514]{3,2,1,0:T(1,128)S(1)}, f32[5,16,1,514]{3,2,1,0:T(1,128)S(1)}, u32[]{:S(2)}, u32[]{:S(2)}) collective-permute-start(f32[5,16,1,514]{3,2,1,0:T(1,128)S(1)} %get-tuple-element.983), channel_id=1, source_target_pairs={{1,0},{3,2},{5,4},{7,6}} | collective-permute-start | bytes 493448 | tf_op jit(solution)/shard_map/ppermute | solution.py:298
  388.8 25.3 %copy-start.25 = (f32[5,16,1,514]{3,2,1,0:T(1,128)}, f32[5,16,1,514]{3,2,1,0:T(1,128)S(1)}, u32[]{:S(2)}) copy-start(f32[5,16,1,514]{3,2,1,0:T(1,128)S(1)} %collective-permute-done.13) | copy-start | bytes 493444
  388.8 25.3 %copy-start.27 = (f32[5,16,1,514]{3,2,1,0:T(1,128)}, f32[5,16,1,514]{3,2,1,0:T(1,128)S(1)}, u32[]{:S(2)}) copy-start(f32[5,16,1,514]{3,2,1,0:T(1,128)S(1)} %collective-permute-done.14) | copy-start | bytes 493444
  670.0 39.3 %copy-start.15 = (f32[256,512]{1,0:T(8,128)S(1)}, f32[256,512]{1,0:T(8,128)}, u32[]{:S(2)}) copy-start(f32[256,512]{1,0:T(8,128)} %get-tuple-element.966) | copy-start | bytes 1572868
  723.5 9.0 collective-permute-start.15
  724.9 14.6 %collective-permute-start.16 = (f32[2,256,32]{2,1,0:T(8,128)S(1)}, f32[2,256,32]{2,1,0:T(8,128)S(1)}, u32[]{:S(2)}, u32[]{:S(2)}) collective-permute-start(f32[2,256,32]{2,1,0:T(8,128)S(1)} %get-tuple-element.1014), channel_id=1, source_target_pairs={{0,2},{2,4},{4,6},{6,0},{1,3},{3,5},{5,7},{7,1}} | collective-permute-start | bytes 196616 | tf_op jit(solution)/shard_map/ppermute | solution.py:304
  727.8 20.1 %collective-permute-start.2 = (f32[5,32,640]{2,1,0:T(8,128)}, f32[5,32,640]{2,1,0:T(8,128)}, u32[]{:S(2)}, u32[]{:S(2)}) collective-permute-start(f32[5,32,640]{2,1,0:T(8,128)} %fusion.58), channel_id=1, source_target_pairs={{0,1},{1,0},{2,3},{3,2},{4,5},{5,4},{6,7},{7,6}} | collective-permute-start | bytes 1228808 | tf_op jit(solution)/shard_map/ppermute | solution.py:308
  740.4 6.0 collective-permute-start.17
  746.4 109.5 %copy-start.19 = (f32[256,512]{1,0:T(8,128)S(1)}, f32[256,512]{1,0:T(8,128)}, u32[]{:S(2)}) copy-start(f32[256,512]{1,0:T(8,128)} %get-tuple-element.827) | copy-start | bytes 1572868
  746.4 109.5 %copy-start.20 = (f32[256,512]{1,0:T(8,128)S(1)}, f32[256,512]{1,0:T(8,128)}, u32[]{:S(2)}) copy-start(f32[256,512]{1,0:T(8,128)} %get-tuple-element.825) | copy-start | bytes 1572868
  880.7 13.8 %collective-permute-start.18 = (f32[2,16,256,1]{2,1,3,0:T(8,128)S(1)}, f32[2,16,256,1]{2,1,3,0:T(8,128)S(1)}, u32[]{:S(2)}, u32[]{:S(2)}) collective-permute-start(f32[2,16,256,1]{2,1,3,0:T(8,128)S(1)} %copy.29), channel_id=1, source_target_pairs={{0,2},{2,4},{4,6},{6,0},{1,3},{3,5},{5,7},{7,1}} | collective-permute-start | bytes 98312 | tf_op jit(solution)/shard_map/ppermute | solution.py:296
  891.6 15.7 %collective-permute-start.19 = (f32[2,16,256,1]{2,1,3,0:T(8,128)S(1)}, f32[2,16,256,1]{2,1,3,0:T(8,128)S(1)}, u32[]{:S(2)}, u32[]{:S(2)}) collective-permute-start(f32[2,16,256,1]{2,1,3,0:T(8,128)S(1)} %copy.31), channel_id=1, source_target_pairs={{0,6},{2,0},{4,2},{6,4},{1,7},{3,1},{5,3},{7,5}} | collective-permute-start | bytes 98312 | tf_op jit(solution)/shard_map/ppermute | solution.py:295
  910.0 31.0 %slice-start.3 = ((s8[8388608]{0:T(1024)(128)(4,1)}), s8[4194304]{0:T(1024)(128)(4,1)S(1)}, s32[]{:S(2)}) async-start(s8[8388608]{0:T(1024)(128)(4,1)} %bitcast.242), calls=%async_computation.3 | async-start | bytes 8388608
  910.0 35.5 %slice-start = ((s8[10485760]{0:T(1024)(128)(4,1)}), s8[4194304]{0:T(1024)(128)(4,1)S(1)}, s32[]{:S(2)}) async-start(s8[10485760]{0:T(1024)(128)(4,1)} %bitcast.240), calls=%async_computation | async-start | bytes 8388608
  911.6 29.5 %slice-start.4 = ((s8[8388608]{0:T(1024)(128)(4,1)}), s8[4194304]{0:T(1024)(128)(4,1)S(1)}, s32[]{:S(2)}) async-start(s8[8388608]{0:T(1024)(128)(4,1)} %bitcast.242), calls=%async_computation.4 | async-start | bytes 8388608
  911.6 29.5 %copy-start.4 = (f32[2,16,256,1]{3,2,1,0:T(8,128)S(1)}, f32[2,16,256,1]{3,2,1,0:T(8,128)}, u32[]{:S(2)}) copy-start(f32[2,16,256,1]{3,2,1,0:T(8,128)} %copy.30) | copy-start | bytes 98308
  911.6 33.9 %slice-start.1 = ((s8[10485760]{0:T(1024)(128)(4,1)}), s8[4194304]{0:T(1024)(128)(4,1)S(1)}, s32[]{:S(2)}) async-start(s8[10485760]{0:T(1024)(128)(4,1)} %bitcast.240), calls=%async_computation.1 | async-start | bytes 8388608
  911.6 33.9 %slice-start.2 = ((s8[10485760]{0:T(1024)(128)(4,1)}), s8[2097152]{0:T(1024)(128)(4,1)S(1)}, s32[]{:S(2)}) async-start(s8[10485760]{0:T(1024)(128)(4,1)} %bitcast.240), calls=%async_computation.2 | async-start | bytes 4194304
  911.6 29.4 %collective-permute-start.20 = (f32[2,16,1,514]{3,2,1,0:T(1,128)S(1)}, f32[2,16,1,514]{3,2,1,0:T(1,128)S(1)}, u32[]{:S(2)}, u32[]{:S(2)}) collective-permute-start(f32[2,16,1,514]{3,2,1,0:T(1,128)S(1)} %pad_maximum_fusion.31), channel_id=1, source_target_pairs={{0,1},{2,3},{4,5},{6,7}} | collective-permute-start | bytes 197384 | tf_op jit(solution)/shard_map/ppermute | solution.py:299
  (33 other events, 310.9 us)

commit v2 on v1

--- a/solution.py
+++ b/solution.py
@@ -23,39 +23,6 @@
     return (levels < count[None]).astype(jnp.float32)
 
 
-def interface_coef(count, thick, kappa, n_levels):
-    levels = jnp.arange(n_levels - 1, dtype=jnp.int32)[:, None, None]
-    active = (levels + 1 < count[None]).astype(jnp.float32)
-    safe = jnp.where(count > 0, thick, 1.0)
-    return active * (TIME_STEP * kappa / (safe * safe))[None]
-
-
-def column_solve(source, couple):
-    edge = jnp.zeros_like(source[:1])
-    upper = jnp.concatenate([couple, edge], axis=0)
-    lower = jnp.concatenate([edge, couple], axis=0)
-    diag = 1.0 + upper + lower
-
-    def forward(carry, slab):
-        gain_prev, part_prev = carry
-        lower_k, diag_k, upper_k, source_k = slab
-        pivot = diag_k - lower_k * gain_prev
-        gain = upper_k / pivot
-        part = (source_k + lower_k * part_prev) / pivot
-        return (gain, part), (gain, part)
-
-    start = (jnp.zeros_like(source[0]), jnp.zeros_like(source[0]))
-    _, (gains, parts) = lax.scan(forward, start, (lower, diag, upper, source))
-
-    def backward(below, slab):
-        gain, part = slab
-        here = part + gain * below
-        return here, here
-
-    _, profile = lax.scan(backward, jnp.zeros_like(source[0]), (gains, parts), reverse=True)
-    return profile
-
-
 def geometry(kmt_ext, depth_ext):
     kmt_cell = kmt_ext[1:-1, 1:-1]
     thick_ext = depth_ext / jnp.maximum(kmt_ext, 1).astype(jnp.float32)
@@ -69,42 +36,6 @@
     face_wet = (k_faces > 0).astype(jnp.float32)
     wet_cell = (layout["k_cell"] > 0).astype(jnp.float32)
     return face_depth, face_wet, wet_cell
-
-
-def momentum_tend(u_ext, v_ext, p_ext):
-    cen_u = 0.5 * (u_ext[:, 1:-1, :-1] + u_ext[:, 1:-1, 1:])
-    corner_v = 0.5 * (v_ext[:, :-1, 1:-1] + v_ext[:, :-1, 2:])
-    corner_u = 0.5 * (u_ext[:, :-1, 1:-1] + u_ext[:, 1:, 1:-1])
-    flux_uu = cen_u * cen_u
-    flux_vu = corner_v * corner_u
-    tend_u = -(flux_uu[:, :, 1:] - flux_uu[:, :, :-1] + flux_vu[:, 1:, :] - flux_vu[:, :-1, :] + p_ext[:, 1:-1, 2:] - p_ext[:, 1:-1, 1:-1]) / GRID_DX
-    cen_v = 0.5 * (v_ext[:, :-1, 1:-1] + v_ext[:, 1:, 1:-1])
-    side_u = 0.5 * (u_ext[:, 1:-1, :-1] + u_ext[:, 2:, :-1])
-    side_v = 0.5 * (v_ext[:, 1:-1, :-1] + v_ext[:, 1:-1, 1:])
-    flux_vv = cen_v * cen_v
-    flux_uv = side_u * side_v
-    tend_v = -(flux_vv[:, 1:, :] - flux_vv[:, :-1, :] + flux_uv[:, :, 1:] - flux_uv[:, :, :-1] + p_ext[:, 2:, 1:-1] - p_ext[:, 1:-1, 1:-1]) / GRID_DX
-    return tend_u, tend_v
-
-
-def baroclinic_predict(vel_u, vel_v, value_a11, salinity, layout, halo_fn):
-    n_levels = vel_u.shape[0]
-    mask_c = level_mask(layout["k_cell"], n_levels)
-    mask_u = level_mask(layout["k_u"], n_levels)
-    mask_v = level_mask(layout["k_v"], n_levels)
-    vel_um = vel_u * mask_u
-    vel_vm = vel_v * mask_v
-    density = mask_c * (BETA_S * (salinity - S_REF) - ALPHA_T * (value_a11 - T_REF))
-    pressure = GRAVITY * layout["dz_cell"] * (jnp.cumsum(density, axis=0) - 0.5 * density)
-    cell_coef = interface_coef(layout["k_cell"], layout["dz_cell"], DIFF_KT, n_levels)
-    temp_mix = column_solve(value_a11 * mask_c, cell_coef)
-    salt_mix = column_solve(salinity * mask_c, cell_coef)
-    edges = halo_fn(jnp.stack([vel_um, vel_vm, pressure, temp_mix, salt_mix]))
-    tend_u, tend_v = momentum_tend(edges[0], edges[1], edges[2])
-    u_star = column_solve(mask_u * (vel_um + TIME_STEP * tend_u), interface_coef(layout["k_u"], layout["dz_u"], VISC_KV, n_levels))
-    v_star = column_solve(mask_v * (vel_vm + TIME_STEP * tend_v), interface_coef(layout["k_v"], layout["dz_v"], VISC_KV, n_levels))
-    forcing = jnp.stack([jnp.sum(layout["dz_u"] * (u_star - vel_um), axis=0), jnp.sum(layout["dz_v"] * (v_star - vel_vm), axis=0)]) / TIME_STEP
-    return u_star, v_star, forcing, edges[3:], (mask_c, mask_u, mask_v)
 
 
 NY = 256
@@ -213,7 +144,10 @@
             accelerate(t, eta_now, eta_north)
             return eta_north, v_north
 
-        eta_last, _ = lax.fori_loop(0, SUB - 1, sweep, (eta_first, v_first))
+        carry = (eta_first, v_first)
+        for t in range(SUB - 1):
+            carry = sweep(t, carry)
+        eta_last = carry[0]
         accelerate(SUB - 1, eta_last, north_wrap(eta_first))
 
     @pl.loop(0, SUB)
@@ -251,6 +185,286 @@
     )(planes, force, tide_force)
 
 
+LEVELS = 16
+TILES = NY // 8
+RING = 4
+CONST_R = -BETA_S * S_REF + ALPHA_T * T_REF
+
+
+def lanes(x, c):
+    return x[:, c * LANES : (c + 1) * LANES]
+
+
+def shift_east(xs, after, lane):
+    nxt = list(xs[1:]) + [after]
+    return [pltpu.roll(jnp.where(lane == 0, n, x), LANES - 1, 1) for x, n in zip(xs, nxt)]
+
+
+def shift_west(xs, before, lane):
+    prv = [before] + list(xs[:-1])
+    return [pltpu.roll(jnp.where(lane == LANES - 1, p, x), 1, 1) for x, p in zip(xs, prv)]
+
+
+def shift_north(xs, above, sub):
+    return [pltpu.roll(jnp.where(sub == 0, a, x), 7, 0) for x, a in zip(xs, above)]
+
+
+def shift_south(xs, below, sub):
+    return [pltpu.roll(jnp.where(sub == 7, b, x), 1, 0) for x, b in zip(xs, below)]
+
+
+def predict_kernel(k_ref, h_ref, u_hbm, v_hbm, t_hbm, s_hbm, hx_hbm, hy_hbm, ustar_hbm, vstar_hbm, tmix_hbm, smix_hbm, force_ref, usum_ref, ring, hring, geo, carry, stage, part, in_sem, hx_sem, out_sem):
+    row = lax.axis_index("row")
+    lane = lax.broadcasted_iota(jnp.int32, (8, LANES), 1)
+    sub = lax.broadcasted_iota(jnp.int32, (8, LANES), 0)
+    cubes = (u_hbm, v_hbm, t_hbm, s_hbm)
+    outs = (ustar_hbm, vstar_hbm, tmix_hbm, smix_hbm)
+
+    def tile_copies(t, slot):
+        rows = pl.ds(pl.multiple_of(t * 8, 8), 8)
+        return [pltpu.make_async_copy(cubes[a].at[:, rows, :], ring.at[slot, a], in_sem.at[slot, a]) for a in range(4)] + [
+            pltpu.make_async_copy(hx_hbm.at[:, :, rows, :], hring.at[slot], hx_sem.at[slot])
+        ]
+
+    def edge_copies(e, slot):
+        rows = pl.ds(e * 8, 8)
+        return [pltpu.make_async_copy(hy_hbm.at[a, :, rows, pl.ds(0, NX)], ring.at[slot, a], in_sem.at[slot, a]) for a in range(4)] + [
+            pltpu.make_async_copy(hy_hbm.at[:, :, rows, pl.ds(NX, LANES)], hring.at[slot], hx_sem.at[slot])
+        ]
+
+    def out_copies(t, slot):
+        rows = pl.ds(pl.multiple_of(t * 8, 8), 8)
+        return [pltpu.make_async_copy(stage.at[slot, a], outs[a].at[:, rows, :], out_sem.at[slot, a]) for a in range(4)]
+
+    def start(copies):
+        for copy in copies:
+            copy.start()
+
+    def wait(copies):
+        for copy in copies:
+            copy.wait()
+
+    start(edge_copies(0, RING - 1))
+    start(tile_copies(0, 0))
+    start(tile_copies(1, 1))
+    start(tile_copies(2, 2))
+
+    cut = jnp.where(row == 0, EXT_Y - 1, NY - 1)
+
+    def layout(t, t_next):
+        k = [lanes(k_ref[pl.ds(pl.multiple_of(t * 8, 8), 8), :], c) for c in range(CHUNKS)]
+        h = [lanes(h_ref[pl.ds(pl.multiple_of(t * 8, 8), 8), :], c) for c in range(CHUNKS)]
+        kn = [lanes(k_ref[pl.ds(pl.multiple_of(t_next * 8, 8), 8), :], c) for c in range(CHUNKS)]
+        hn = [lanes(h_ref[pl.ds(pl.multiple_of(t_next * 8, 8), 8), :], c) for c in range(CHUNKS)]
+        dz = [a / jnp.maximum(b, 1.0) for a, b in zip(h, k)]
+        dzn = [a / jnp.maximum(b, 1.0) for a, b in zip(hn, kn)]
+        k_e = shift_east(k, k[0], lane)
+        dz_e = shift_east(dz, dz[0], lane)
+        k_n = [jnp.where(sub + t * 8 == cut, 0.0, x) for x in shift_north(k, kn, sub)]
+        dz_n = shift_north(dz, dzn, sub)
+        for c in range(CHUNKS):
+            at = pl.ds(c * LANES, LANES)
+            k_u = jnp.minimum(k[c], k_e[c])
+            k_v = jnp.minimum(k[c], k_n[c])
+            dz_u = 0.5 * (dz[c] + dz_e[c])
+            dz_v = 0.5 * (dz[c] + dz_n[c])
+            geo[0, t, :, at] = k[c]
+            geo[1, t, :, at] = k_u
+            geo[2, t, :, at] = k_v
+            geo[3, t, :, at] = dz[c]
+            geo[4, t, :, at] = dz_u
+            geo[5, t, :, at] = dz_v
+            safe_c = jnp.where(k[c] > 0, dz[c], 1.0)
+            safe_u = jnp.where(k_u > 0, dz_u, 1.0)
+            safe_v = jnp.where(k_v > 0, dz_v, 1.0)
+            geo[6, t, :, at] = (TIME_STEP * DIFF_KT) / (safe_c * safe_c)
+            geo[7, t, :, at] = (TIME_STEP * VISC_KV) / (safe_u * safe_u)
+            geo[8, t, :, at] = (TIME_STEP * VISC_KV) / (safe_v * safe_v)
+
+    @pl.loop(0, SUB - 1)
+    def _(t):
+        layout(t, t + 1)
+
+    layout(SUB - 1, 0)
+
+    def body(t, slot_now, slot_next, first, work):
+        g_next = lax.rem(t + 1 + SUB, SUB)
+
+        def plane(q, tt, n):
+            return [geo[q, tt, :, pl.ds(c * LANES, LANES)] for c in range(n)]
+
+        k1 = plane(0, g_next, 5)
+        ku1 = plane(1, g_next, 5)
+        kv1 = plane(2, g_next, 5)
+        dz1 = [(TIME_STEP * GRAVITY) * x for x in plane(3, g_next, 5)]
+        csum = [jnp.zeros((8, LANES), jnp.float32)] * 5
+        if work:
+            kc0 = plane(0, t, 4)
+            ku0 = plane(1, t, 4)
+            kv0 = plane(2, t, 4)
+            cc = plane(6, t, 4)
+            cu = plane(7, t, 4)
+            cv = plane(8, t, 4)
+            zero = [jnp.zeros((8, LANES), jnp.float32)] * 4
+            one = [jnp.ones((8, LANES), jnp.float32)] * 4
+            chains = {n: {"q": one, "cl": zero, "parts": {}} for n in "cuv"}
+            prev = {n: zero for n in ("u", "v", "T", "S")}
+            total_m = {"u": zero, "v": zero}
+
+        for k in range(LEVELS):
+
+            def tile(slot, a, n):
+                got = [ring[slot, a, k, :, pl.ds(c * LANES, LANES)] for c in range(4)]
+                return got + [hring[slot, a, k]] if n == 5 else got
+
+            raw_u, raw_v, raw_t, raw_s = (tile(slot_next, a, 5) for a in range(4))
+            um1 = [jnp.where(m > k, x, 0.0) for m, x in zip(ku1, raw_u)]
+            vm1 = [jnp.where(m > k, x, 0.0) for m, x in zip(kv1, raw_v)]
+            half = [jnp.where(m > k, (0.5 * BETA_S) * s - (0.5 * ALPHA_T) * x + 0.5 * CONST_R, 0.0) for m, x, s in zip(k1, raw_t, raw_s)]
+            mid = [a + b for a, b in zip(csum, half)]
+            csum = [a + b for a, b in zip(mid, half)]
+            p1 = [a * b for a, b in zip(mid, dz1)]
+            u_w = shift_west(um1, um1[4], lane)
+            e1 = [(a + b) * (a + b) + p for a, b, p in zip(u_w, um1, p1)]
+            e_e = shift_east(e1[:4], e1[4], lane)
+            ed1 = [a - b for a, b in zip(e_e, e1)]
+            v_e = shift_east(vm1, vm1[0], lane)
+            ve1 = [a + b for a, b in zip(vm1, v_e)]
+            old = lambda q, n: [carry[q, k, :, pl.ds(c * LANES, LANES)] for c in range(n)]
+            if first:
+                b1 = [jnp.zeros((8, LANES), jnp.float32)] * 4
+            else:
+                vm0 = old(1, 4)
+                um0 = old(0, 5)
+                ve0 = old(2, 5)
+                v_s = shift_south(vm1[:4], vm0, sub)
+                b1 = [(a + b) * (a + b) + p for a, b, p in zip(v_s, vm1, p1)]
+                u_n = shift_north(um0, um1, sub)
+                q0 = [(a + b) * x for a, b, x in zip(um0, u_n, ve0)]
+            if work:
+                ed0 = old(3, 4)
+                b0 = old(4, 4)
+                q_s = shift_south(q0[:4], old(5, 4), sub)
+                q_w = shift_west(q0[:4], q0[4], lane)
+                b_n = shift_north(b0, b1, sub)
+                src = {
+                    "u": [jnp.where(m > k, u - (e + (q - s)), 0.0) for m, u, e, q, s in zip(ku0, um0, ed0, q0, q_s)],
+                    "v": [jnp.where(m > k, v - ((bn - b) + (q - w)), 0.0) for m, v, bn, b, q, w in zip(kv0, vm0, b_n, b0, q0, q_w)],
+                    "T": [jnp.where(m > k, x, 0.0) for m, x in zip(kc0, tile(slot_now, 2, 4))],
+                    "S": [jnp.where(m > k, x, 0.0) for m, x in zip(kc0, tile(slot_now, 3, 4))],
+                }
+                total_m = {"u": [a + b for a, b in zip(total_m["u"], um0)], "v": [a + b for a, b in zip(total_m["v"], vm0)]}
+                for name, coef, mask, fields in (("u", cu, ku0, "u"), ("v", cv, kv0, "v"), ("c", cc, kc0, "TS")):
+                    chain = chains[name]
+                    down = [jnp.where(m > k + 1, c, 0.0) for m, c in zip(mask, coef)] if k < LEVELS - 1 else zero
+                    inv = [1.0 / (q + d) for q, d in zip(chain["q"], down)]
+                    gain = [d * r for d, r in zip(down, inv)]
+                    for f in fields:
+                        prev[f] = [(s + l * p) * r for s, l, p, r in zip(src[f], chain["cl"], prev[f], inv)]
+                        for c in range(4):
+                            part["uvTS".index(f), k, :, pl.ds(c * LANES, LANES)] = prev[f][c]
+                    for c in range(4):
+                        part[4 + "uvc".index(name), k, :, pl.ds(c * LANES, LANES)] = gain[c]
+                    chain["q"] = [1.0 + g * q for g, q in zip(gain, chain["q"])]
+                    chain["cl"] = down
+            new = [(0, um1, 5), (1, vm1, 4), (2, ve1, 5), (3, ed1, 4), (4, b1, 4)]
+            if not first:
+                new.append((5, q0, 4))
+            for q, vals, n in new:
+                for c in range(n):
+                    carry[q, k, :, pl.ds(c * LANES, LANES)] = vals[c]
+
+        if not work:
+            return
+        out_slot = lax.rem(t, 2)
+        below = dict(prev)
+        total = {"u": below["u"], "v": below["v"]}
+        for f in "uvTS":
+            for c in range(4):
+                stage[out_slot, "uvTS".index(f), LEVELS - 1, :, pl.ds(c * LANES, LANES)] = below[f][c]
+        for k in range(LEVELS - 2, -1, -1):
+            for f in "uvTS":
+                a = "uvTS".index(f)
+                g = 4 + "uvcc".index({"u": "u", "v": "v", "T": "c", "S": "c"}[f])
+                here = []
+                for c in range(4):
+                    at = pl.ds(c * LANES, LANES)
+                    val = part[a, k, :, at] + part[g, k, :, at] * below[f][c]
+                    stage[out_slot, a, k, :, at] = val
+                    here.append(val)
+                below[f] = here
+                if f in total:
+                    total[f] = [x + y for x, y in zip(total[f], here)]
+        rows = pl.ds(pl.multiple_of(t * 8, 8), 8)
+        dzu = plane(4, t, 4)
+        dzv = plane(5, t, 4)
+        for c in range(4):
+            at = pl.ds(c * LANES, LANES)
+            force_ref[0, rows, at] = (1.0 / TIME_STEP) * (dzu[c] * (total["u"][c] - total_m["u"][c]))
+            force_ref[1, rows, at] = (1.0 / TIME_STEP) * (dzv[c] * (total["v"][c] - total_m["v"][c]))
+            usum_ref[0, rows, at] = dzu[c] * total["u"][c]
+            usum_ref[1, rows, at] = dzv[c] * total["v"][c]
+
+    wait(edge_copies(0, RING - 1))
+    body(-2, 0, RING - 1, True, False)
+    wait(tile_copies(0, 0))
+    body(-1, RING - 1, 0, False, False)
+
+    @pl.loop(0, TILES)
+    def _(t):
+        @pl.when(t + 3 < TILES)
+        def _():
+            start(tile_copies(t + 3, lax.rem(t + 3, RING)))
+
+        @pl.when(t + 3 == TILES)
+        def _():
+            start(edge_copies(1, TILES % RING))
+
+        @pl.when(t >= 2)
+        def _():
+            wait(out_copies(t - 2, lax.rem(t, 2)))
+
+        @pl.when(t + 1 < TILES)
+        def _():
+            wait(tile_copies(t + 1, lax.rem(t + 1, RING)))
+
+        @pl.when(t + 1 == TILES)
+        def _():
+            wait(edge_copies(1, TILES % RING))
+
+        body(t, lax.rem(t, RING), lax.rem(t + 1, RING), False, True)
+        start(out_copies(t, lax.rem(t, 2)))
+
+    wait(out_copies(TILES - 2, 0))
+    wait(out_copies(TILES - 1, 1))
+
+
+def predict(k_ext, h_ext, u, v, temp, salt, hx, hy):
+    cube = jax.ShapeDtypeStruct((LEVELS, NY, NX), jnp.float32)
+    pair = jax.ShapeDtypeStruct((2, NY, NX), jnp.float32)
+    vmem = pl.BlockSpec(memory_space=pltpu.VMEM)
+    hbm = pl.BlockSpec(memory_space=pl.ANY)
+    return pl.pallas_call(
+        predict_kernel,
+        out_shape=[cube] * 4 + [pair, pair],
+        in_specs=[vmem, vmem] + [hbm] * 6,
+        out_specs=[hbm] * 4 + [vmem, vmem],
+        scratch_shapes=[
+            pltpu.VMEM((RING, 4, LEVELS, 8, NX), jnp.float32),
+            pltpu.VMEM((RING, 4, LEVELS, 8, LANES), jnp.float32),
+            pltpu.VMEM((9, SUB, 8, EXT_X), jnp.float32),
+            pltpu.VMEM((6, LEVELS, 8, EXT_X), jnp.float32),
+            pltpu.VMEM((2, 4, LEVELS, 8, NX), jnp.float32),
+            pltpu.VMEM((7, LEVELS, 8, NX), jnp.float32),
+            pltpu.SemaphoreType.DMA((RING, 4)),
+            pltpu.SemaphoreType.DMA((RING,)),
+            pltpu.SemaphoreType.DMA((2, 4)),
+        ],
+        compiler_params=pltpu.CompilerParams(vmem_limit_bytes=48 * 1024 * 1024),
+        name="predict",
+    )(k_ext, h_ext, u, v, temp, salt, hx, hy)
+
+
 def correct_velocity(star, dz_face, depth_face, mean_trans, mask):
     safe = jnp.where(depth_face > 0, depth_face, 1.0)
     return mask * (star + ((mean_trans - jnp.sum(dz_face * star, axis=0)) / safe)[None])
@@ -272,10 +486,13 @@
     return vel_uc, vel_vc, tracers[0], tracers[1]
 
 
-def ocean_step(vel_u, vel_v, value_a11, salinity, sea_level, trans_u, trans_v, bathymetry, kmt_levels, tide_force, halo_fn, wide_fn):
+def ocean_step(vel_u, vel_v, value_a11, salinity, sea_level, trans_u, trans_v, bathymetry, kmt_levels, tide_force, halo_fn, wide_fn, edge_fn):
     layout = geometry(halo_fn(kmt_levels), halo_fn(bathymetry))
     planes = wide_fn(jnp.stack([kmt_levels.astype(jnp.float32), bathymetry, sea_level, trans_u, trans_v]))
-    u_star, v_star, forcing, tracer_ext, masks = baroclinic_predict(vel_u, vel_v, value_a11, salinity, layout, halo_fn)
+    hx, hy = edge_fn(jnp.stack([vel_u, vel_v, value_a11, salinity]))
+    u_star, v_star, temp_mix, salt_mix, forcing, _ = predict(planes[0], planes[1], vel_u, vel_v, value_a11, salinity, hx, hy)
+    tracer_ext = halo_fn(jnp.stack([temp_mix, salt_mix]))
+    masks = tuple(level_mask(layout[n], LEVELS) for n in ("k_cell", "k_u", "k_v"))
     face_depth, face_wet, wet_cell = surface_fields(layout)
     eta_new, u_new, v_new, u_avg, v_avg = barotropic(planes, wide_fn(forcing), tide_force)
     trans_avg = (u_avg, v_avg)
@@ -308,8 +525,20 @@
         other = lax.ppermute(edge, "row", [(0, 1), (1, 0)])
         return jnp.concatenate([wide, other], axis=-2)
 
+    def edge_swap(field):
+        from_east = lax.ppermute(field[..., :1], "col", east_perm)
+        from_west = lax.ppermute(field[..., -1:], "col", west_perm)
+        gap = jnp.zeros(field.shape[:-1] + (LANES - 2,), field.dtype)
+        side = jnp.concatenate([from_east, gap, from_west], axis=-1)
+        first = jnp.concatenate([field[..., :1, :], side[..., :1, :]], axis=-1)
+        last = jnp.concatenate([field[..., -1:, :], side[..., -1:, :]], axis=-1)
+        from_north = lax.ppermute(first, "row", north_perm)
+        from_south = lax.ppermute(last, "row", south_perm)
+        gap = jnp.zeros(first.shape[:-2] + (7, EXT_X), field.dtype)
+        return side, jnp.concatenate([gap, from_south, from_north, gap], axis=-2)
+
     def local_step(vel_u, vel_v, value_a11, salinity, sea_level, trans_u, trans_v, bathymetry, kmt_levels, tide_force):
-        return ocean_step(vel_u, vel_v, value_a11, salinity, sea_level, trans_u, trans_v, bathymetry, kmt_levels, tide_force, halo_swap, wide_swap)
+        return ocean_step(vel_u, vel_v, value_a11, salinity, sea_level, trans_u, trans_v, bathymetry, kmt_levels, tide_force, halo_swap, wide_swap, edge_swap)
 
     spec_cube = P(None, "row", "col")
     spec_plane = P("row", "col")

time: 1020 us -> 409 us (0.40)
  other arithmetic: 717 us -> 188 us
  local copies, waits for them, and re-layouts: 149 us -> 89.9 us
  Pallas kernels: 105 us -> 86.6 us
  waiting for transfers between devices: 12.8 us -> 0.07 us
  starting transfers between devices: 29.6 us -> 41.8 us
    dynamic_update_slice x128 -> x0, other arithmetic: 353 us -> none  [column_solve(): _, (gains, parts) = lax.scan(forward, start, (lower, diag, upper, source))]
    mul x5 -> x1, other arithmetic: 112 us -> 1.44 us  [geometry(): 0.5 * (thick_cell + thick_ext[1:-1, 2:])]
    pallas_call x1, Pallas kernels: 105 us -> 41.2 us  [barotropic(): pl.pallas_call(functools.partial(barotropic_kernel, n_sub), out_shape=[ou...]
    another operation x13 -> x0, local copies, waits for them, and re-layouts: 61.1 us -> none
    pallas_call x0 -> x1, Pallas kernels: none -> 45.4 us  [predict(): pl.pallas_call(predict_kernel, out_shape=[cube] * 4 + [pair, pair], in_sp...]
    squeeze x1 -> x0, other arithmetic: 25.3 us -> none  [baroclinic_predict(): tend_u, tend_v = momentum_tend(edges[0], edges[1], edges[2])]
    concatenate x2 -> x3, other arithmetic: 36.9 us -> 12.7 us  [the longest x1 7.02 us: edge_swap(): side = jnp.concatenate([from_east, gap, from_west], axis=-1)]
    slice x0 -> x4, local copies, waits for them, and re-layouts: none -> 22.7 us  [the longest x2 16.8 us: edge_swap(): from_east = lax.ppermute(field[..., :1], 'col', east_perm)]
  transfers between devices with their start and end apart: 21 -> 25, of which waited for: 3 -> 0; matrix products, arithmetic and copies ran while one was open for 12% -> 43% of each run, Pallas kernels for 0% -> 0%
where the time goes in v2:
time: 409 us; the launch traced here: 408 us
  other arithmetic  188 us (46%)
  local copies, waits for them, and re-layouts  89.9 us (22%)
  Pallas kernels  86.6 us (21%)
  starting transfers between devices  41.8 us (10%)
    pallas_call x1, Pallas kernels, predict(): pl.pallas_call(predict_kernel, out_shape=[cube] * 4 + [pair, pair], in_sp...  45.4 us
    pallas_call x1, Pallas kernels, barotropic(): pl.pallas_call(functools.partial(barotropic_kernel, n_sub), out_shape=[ou...  41.2 us
    mul x1, other arithmetic, advect_tracers(): return mask_c * (tracer_ext[..., 1:-1, 1:-1] - TIME_STEP * divergence)  38.2 us
    mul x2, other arithmetic, advect_tracers(): flow_ext[0, :, 1:-1, :-1]  36.5 us
    mul x2, other arithmetic, advect_tracers(): flow_ext[1, :, :-1, 1:-1]  25.3 us
    another operation x1, other arithmetic, ocean_step(): hx, hy = edge_fn(jnp.stack([vel_u, vel_v, value_a11, salinity]))  23.2 us
    slice x2, local copies, waits for them, and re-layouts, edge_swap(): from_east = lax.ppermute(field[..., :1], 'col', east_perm)  16.8 us
    unnamed x62, local copies, waits for them, and re-layouts  11.2 us
  transfers between devices with their start and end apart: 25, of which 0 were waited for; matrix products, arithmetic and copies ran while one was open for 43% of the time, Pallas kernels for 0%

profile of v2, /device:TPU:0, one launch (start us, length us, event | category | flops | bytes accessed | tf_op | source)
XLA Modules:
  0.0 407.5 jit_solution(17621964644018954208)
XLA Ops:
  9.3 3.3 collective-permute-start.1
  18.4 23.2 %pad_maximum_fusion = f32[4,16,256,512]{3,2,1,0:T(8,128)} fusion(f32[1,16,256,512]{3,2,1,0:T(8,128)} %bitcast.72, f32[1,16,256,512]{3,2,1,0:T(8,128)} %bitcast.70, f32[1,16,256,512]{3,2,1,0:T(8,128)} %bitcast.68, f32[1,16,256,512]{3,2,1,0:T(8,128)} %bitcast.66), kind=kLoop, calls=%fused_computation | loop fusion | flops 25165824 | bytes 67108864 | tf_op jit(solution)/shard_map/stack | solution.py:492
  41.6 11.0 %fusion.25 = (f32[4,16,256,1]{3,2,1,0:T(8,128)}, f32[4,16,256,1]{3,2,1,0:T(8,128)}) fusion(f32[4,16,256,512]{3,2,1,0:T(8,128)} %pad_maximum_fusion), kind=kLoop, calls=%fused_computation.109 | loop fusion | bytes 262144 | tf_op jit(solution)/shard_map/slice | solution.py:529
  56.6 4.8 %collective-permute-start.13 = (f32[1,514]{1,0:T(1,128)}, f32[1,514]{1,0:T(1,128)}, u32[]{:S(2)}, u32[]{:S(2)}) collective-permute-start(f32[1,514]{1,0:T(1,128)} %get-tuple-element.51), channel_id=1, source_target_pairs={{0,1},{2,3},{4,5},{6,7}} | collective-permute-start | bytes 6176 | tf_op jit(solution)/shard_map/ppermute | solution.py:516
  63.2 4.4 %fusion.10 = f32[16,256,512]{2,1,0:T(8,128)} fusion(s32[256,512]{1,0:T(8,128)S(1)} %copy-done.6), kind=kLoop, calls=%fused_computation.44 | loop fusion | flops 4194304 | bytes 8912896 | tf_op jit(solution)/shard_map/convert_element_type | solution.py:23
  69.6 5.8 %copy.23 = f32[4,16,256,1]{2,1,3,0:T(8,128)} copy(f32[4,16,256,1]{3,2,1,0:T(8,128)} %get-tuple-element.30) | data formatting | bytes 131072 | tf_op jit(solution)/shard_map/slice | solution.py:530
  75.4 5.8 %copy.22 = f32[4,16,256,1]{2,1,3,0:T(8,128)} copy(f32[4,16,256,1]{3,2,1,0:T(8,128)} %get-tuple-element.29) | data formatting | bytes 131072 | tf_op jit(solution)/shard_map/slice | solution.py:529
  91.0 5.4 %copy.25 = f32[4,16,256,1]{3,2,1,0:T(8,128)} copy(f32[4,16,256,1]{2,1,3,0:T(8,128)} %collective-permute-done.4) | data formatting | bytes 131072 | tf_op jit(solution)/shard_map/ppermute | solution.py:530
  96.4 5.4 %copy.24 = f32[4,16,256,1]{3,2,1,0:T(8,128)} copy(f32[4,16,256,1]{2,1,3,0:T(8,128)} %collective-permute-done.3) | data formatting | bytes 131072 | tf_op jit(solution)/shard_map/ppermute | solution.py:529
  101.8 7.0 %pad_maximum_fusion.16.hx_hbm = f32[4,16,256,128]{3,2,1,0:T(8,128)S(1)} fusion(f32[4,16,256,1]{3,2,1,0:T(8,128)} %copy.25, f32[4,16,256,1]{3,2,1,0:T(8,128)} %copy.24, f32[128]{0:T(128)S(1)} %copy-done.22), kind=kLoop, calls=%fused_computation.36 | loop fusion | flops 4194304 | bytes 8520192 | tf_op jit(solution)/shard_map/concatenate | solution.py:532
  108.9 4.1 %fusion.24 = (f32[4,16,1,640]{3,2,1,0:T(1,128)}, f32[4,16,1,640]{3,2,1,0:T(1,128)}) fusion(f32[1,16,256,512]{3,2,1,0:T(8,128)} %bitcast.73, f32[1,16,256,512]{3,2,1,0:T(8,128)} %bitcast.71, f32[1,16,256,512]{3,2,1,0:T(8,128)} %bitcast.69, f32[1,16,256,512]{3,2,1,0:T(8,128)} %bitcast.67, f32[4,16,1,128]{3,2,1,0:T(1,128)S(1)} %get-tuple-element.39, ...), kind=kLoop, calls=%fused_computation.93 | loop fusion | flops 327680 | bytes 33947648 | tf_op jit(solution)/shard_map/concatenate | solution.py:534
  114.3 4.3 %collective-permute-start.5 = (f32[4,16,1,640]{3,2,1,0:T(1,128)}, f32[4,16,1,640]{3,2,1,0:T(1,128)}, u32[]{:S(2)}, u32[]{:S(2)}) collective-permute-start(f32[4,16,1,640]{3,2,1,0:T(1,128)} %get-tuple-element.27), channel_id=1, source_target_pairs={{0,1},{2,3},{4,5},{6,7}} | collective-permute-start | bytes 491528 | tf_op jit(solution)/shard_map/ppermute | solution.py:536
  125.0 2.8 fusion.13
  132.1 45.4 %predict.1 = (f32[16,256,512]{2,1,0:T(8,128)}, f32[16,256,512]{2,1,0:T(8,128)}, f32[16,256,512]{2,1,0:T(8,128)}, f32[16,256,512]{2,1,0:T(8,128)}, f32[2,256,512]{2,1,0:T(8,128)S(1)}, /*index=5*/f32[2,256,512]{2,1,0:T(8,128)}) custom-call(f32[288,640]{1,0:T(8,128)S(1)} %get-tuple-element.42.k_ref, f32[288,640]{1,0:T(8,128)S(1)} %get-tuple-element.41.h_ref, ...), custom_call_target="tpu_custom_call" | custom-call | tf_op jit(solution)/shard_map/predict/pallas_call | solution.py:447
  180.6 5.4 %multiply_reduce_fusion = f32[256,512]{1,0:T(8,128)} fusion(f32[16,256,512]{2,1,0:T(8,128)} %get-tuple-element.23, f32[256,512]{1,0:T(8,128)S(1)} %copy-done.15), kind=kLoop, calls=%fused_computation.39 | loop fusion | flops 4063232 | bytes 9437184 | tf_op jit(solution)/shard_map/reduce_sum | solution.py:470
  186.0 5.8 %fusion.11 = (f32[2,16,256,1]{3,2,1,0:T(8,128)}, f32[2,16,256,1]{3,2,1,0:T(8,128)}) fusion(f32[1,16,256,512]{3,2,1,0:T(8,128)S(1)} %bitcast.57, f32[1,16,256,512]{3,2,1,0:T(8,128)} %bitcast.61), kind=kLoop, calls=%fused_computation.45 | loop fusion | flops 16384 | bytes 16842752 | tf_op jit(solution)/shard_map/stack | solution.py:494
  191.7 2.9 copy.29
  196.1 2.8 copy.27
  200.3 5.3 %multiply_reduce_fusion.1 = f32[256,512]{1,0:T(8,128)} fusion(f32[16,256,512]{2,1,0:T(8,128)} %get-tuple-element.21, f32[256,512]{1,0:T(8,128)S(1)} %copy-done.14), kind=kLoop, calls=%fused_computation.42 | loop fusion | flops 4063232 | bytes 9437184 | tf_op jit(solution)/shard_map/reduce_sum | solution.py:470
  214.5 41.2 %barotropic.1 = (f32[256,512]{1,0:T(8,128)}, f32[256,512]{1,0:T(8,128)}, f32[256,512]{1,0:T(8,128)}, f32[256,512]{1,0:T(8,128)S(1)}, f32[256,512]{1,0:T(8,128)S(1)}) custom-call(f32[5,288,640]{2,1,0:T(8,128)S(1)} %copy-done.1, f32[2,288,640]{2,1,0:T(8,128)S(1)} %pad_maximum_fusion.21.force_hbm, f32[30,2]{1,0:T(8,128)S(1)} %copy.26.tide_ref), custom_call_target="tpu_custom_call" | custom-call | tf_op jit(solution)/shard_map/barotropic/pallas_call | solution.py:177
  257.1 7.6 %add_select_fusion = (f32[16,256,512]{2,1,0:T(8,128)S(1)}, f32[16,256,512]{2,1,0:T(8,128)S(1)}) fusion(f32[16,256,512]{2,1,0:T(8,128)} %get-tuple-element.23, f32[256,512]{1,0:T(8,128)} %get-tuple-element.45, s32[256,512]{1,0:T(8,128)S(1)} %copy-done.13, f32[16,256,512]{2,1,0:T(8,128)} %get-tuple-element.21, f32[256,512]{1,0:T(8,128)} %get-tuple-element.46, ...), kind=kLoop, calls=%fused_computation.38 | loop fusion | flops 12582912 | bytes 35651584 | tf_op jit(solution)/shard_map/mul | solution.py:470
  264.7 5.4 %pad_maximum_fusion.18 = (f32[2,16,256,1]{3,2,1,0:T(8,128)}, f32[2,16,256,1]{3,2,1,0:T(8,128)}) fusion(f32[1,16,256,512]{3,2,1,0:T(8,128)S(1)} %bitcast.42, f32[1,16,256,512]{3,2,1,0:T(8,128)S(1)} %bitcast.48), kind=kLoop, calls=%fused_computation.48 | loop fusion | flops 16384 | bytes 16842752 | tf_op jit(solution)/shard_map/slice | solution.py:513
  270.6 2.8 copy-done.3
  273.3 2.8 copy.31
  280.9 3.0 collective-permute-start.21
  283.9 2.8 copy.35
  290.9 10.2 %fusion.7 = f32[16,256,513]{2,1,0:T(8,128)} fusion(f32[2,16,256,1]{3,2,1,0:T(8,128)} %copy.32, f32[1,16,256,512]{3,2,1,0:T(8,128)} %bitcast.43, f32[1,16,256,512]{3,2,1,0:T(8,128)} %bitcast.49), kind=kLoop, calls=%fused_computation.26 | loop fusion | flops 6303744 | bytes 25214976 | tf_op jit(solution)/shard_map/mul | solution.py:474
  306.9 26.3 %fusion = f32[2,16,256,513]{3,2,1,0:T(8,128)} fusion(f32[1,16,256,512]{3,2,1,0:T(8,128)} %bitcast.63, f32[1,16,256,512]{3,2,1,0:T(8,128)} %bitcast.55, f32[2,16,256,1]{3,2,1,0:T(8,128)} %copy.28, f32[2,16,256,1]{3,2,1,0:T(8,128)} %copy.30, f32[16,256,513]{2,1,0:T(8,128)} %fusion.7), kind=kLoop, calls=%fused_computation.7 | loop fusion | flops 25214976 | bytes 42057728 | tf_op jit(solution)/shard_map/mul | solution.py:474
  333.3 6.1 %fusion.9 = f32[16,257,512]{2,1,0:T(8,128)} fusion(f32[2,16,1,514]{3,2,1,0:T(1,128)S(1)} %collective-permute-done.24, f32[2,16,256,1]{3,2,1,0:T(8,128)} %copy.37, f32[2,16,256,1]{3,2,1,0:T(8,128)} %copy.32, f32[1,16,256,512]{3,2,1,0:T(8,128)S(1)} %bitcast.47, f32[1,16,256,512]{3,2,1,0:T(8,128)S(1)} %bitcast.53), kind=kLoop, calls=%fused_computation.30 | loop fusion | flops 10526720 | bytes 25329920 | tf_op jit(solution)/shard_map/mul | solution.py:475
  339.4 19.2 %fusion.2 = f32[2,16,257,512]{3,2,1,0:T(8,128)} fusion(f32[2,16,1,514]{3,2,1,0:T(1,128)S(1)} %collective-permute-done.22, f32[2,16,256,1]{3,2,1,0:T(8,128)} %copy.30, f32[2,16,256,1]{3,2,1,0:T(8,128)} %copy.28, f32[1,16,256,512]{3,2,1,0:T(8,128)} %bitcast.64, f32[1,16,256,512]{3,2,1,0:T(8,128)S(1)} %bitcast.60, ...), kind=kLoop, calls=%fused_computation.10 | loop fusion | flops 42106880 | bytes 42238464 | tf_op jit(solution)/shard_map/mul | solution.py:475
  358.6 38.2 %fusion.4 = f32[2,16,256,512]{3,2,1,0:T(8,128)} fusion(f32[1,16,256,512]{3,2,1,0:T(8,128)} %bitcast.65, f32[1,16,256,512]{3,2,1,0:T(8,128)} %bitcast.56, f32[2,16,257,512]{3,2,1,0:T(8,128)} %fusion.2, f32[2,16,256,513]{3,2,1,0:T(8,128)} %fusion, f32[16,256,512]{2,1,0:T(8,128)} %fusion.10), kind=kLoop, calls=%fused_computation.19 | loop fusion | flops 29360128 | bytes 109051904 | tf_op jit(solution)/shard_map/mul | solution.py:477
  396.8 10.7 %slice_bitcast_fusion = (f32[16,256,512]{2,1,0:T(8,128)}, f32[16,256,512]{2,1,0:T(8,128)}) fusion(f32[2,16,256,512]{3,2,1,0:T(8,128)} %fusion.4), kind=kLoop, calls=%fused_computation.34 | loop fusion | bytes 33554432 | tf_op jit(solution)/shard_map/squeeze | solution.py:486
  (144 shorter events, 74.9 us)
Async XLA Ops:
  9.3 109.3 %collective-permute-start.1 = (f32[5,256,32]{1,2,0:T(8,128)}, f32[5,256,32]{1,2,0:T(8,128)}, u32[]{:S(2)}, u32[]{:S(2)}) collective-permute-start(f32[5,256,32]{1,2,0:T(8,128)} %copy.19), channel_id=1, source_target_pairs={{0,2},{2,4},{4,6},{6,0},{1,3},{3,5},{5,7},{7,1}} | collective-permute-start | bytes 491528 | tf_op jit(solution)/shard_map/ppermute | solution.py:521
  12.8 39.8 %collective-permute-start.10 = (s32[256,1]{1,0:T(8,128)S(1)}, s32[256,1]{1,0:T(8,128)S(1)}, u32[]{:S(2)}, u32[]{:S(2)}) collective-permute-start(s32[256,1]{1,0:T(8,128)S(1)} %get-tuple-element.60), channel_id=1, source_target_pairs={{0,6},{2,0},{4,2},{6,4},{1,7},{3,1},{5,3},{7,5}} | collective-permute-start | bytes 3080 | tf_op jit(solution)/shard_map/ppermute | solution.py:512
  13.8 38.8 %collective-permute-start.15 = (s32[256,1]{1,0:T(8,128)S(1)}, s32[256,1]{1,0:T(8,128)S(1)}, u32[]{:S(2)}, u32[]{:S(2)}) collective-permute-start(s32[256,1]{1,0:T(8,128)S(1)} %get-tuple-element.59), channel_id=1, source_target_pairs={{0,2},{2,4},{4,6},{6,0},{1,3},{3,5},{5,7},{7,1}} | collective-permute-start | bytes 3080 | tf_op jit(solution)/shard_map/ppermute | solution.py:513
  15.9 38.7 %collective-permute-start.12 = (f32[256,1]{1,0:T(8,128)S(1)}, f32[256,1]{1,0:T(8,128)S(1)}, u32[]{:S(2)}, u32[]{:S(2)}) collective-permute-start(f32[256,1]{1,0:T(8,128)S(1)} %get-tuple-element.58), channel_id=1, source_target_pairs={{0,6},{2,0},{4,2},{6,4},{1,7},{3,1},{5,3},{7,5}} | collective-permute-start | bytes 3080 | tf_op jit(solution)/shard_map/ppermute | solution.py:512
  17.8 36.8 %collective-permute-start.11 = (f32[256,1]{1,0:T(8,128)S(1)}, f32[256,1]{1,0:T(8,128)S(1)}, u32[]{:S(2)}, u32[]{:S(2)}) collective-permute-start(f32[256,1]{1,0:T(8,128)S(1)} %get-tuple-element.57), channel_id=1, source_target_pairs={{0,2},{2,4},{4,6},{6,0},{1,3},{3,5},{5,7},{7,1}} | collective-permute-start | bytes 3080 | tf_op jit(solution)/shard_map/ppermute | solution.py:513
  53.3 29.4 %collective-permute-start.17 = (s32[1,514]{1,0:T(1,128)}, s32[1,514]{1,0:T(1,128)}, u32[]{:S(2)}, u32[]{:S(2)}) collective-permute-start(s32[1,514]{1,0:T(1,128)} %get-tuple-element.50), channel_id=1, source_target_pairs={{1,0},{3,2},{5,4},{7,6}} | collective-permute-start | bytes 6176 | tf_op jit(solution)/shard_map/ppermute | solution.py:515
  55.3 29.7 %collective-permute-start.14 = (f32[1,514]{1,0:T(1,128)}, f32[1,514]{1,0:T(1,128)}, u32[]{:S(2)}, u32[]{:S(2)}) collective-permute-start(f32[1,514]{1,0:T(1,128)} %get-tuple-element.52), channel_id=1, source_target_pairs={{1,0},{3,2},{5,4},{7,6}} | collective-permute-start | bytes 6176 | tf_op jit(solution)/shard_map/ppermute | solution.py:515
  56.6 29.0 %collective-permute-start.13 = (f32[1,514]{1,0:T(1,128)}, f32[1,514]{1,0:T(1,128)}, u32[]{:S(2)}, u32[]{:S(2)}) collective-permute-start(f32[1,514]{1,0:T(1,128)} %get-tuple-element.51), channel_id=1, source_target_pairs={{0,1},{2,3},{4,5},{6,7}} | collective-permute-start | bytes 6176 | tf_op jit(solution)/shard_map/ppermute | solution.py:516
  61.3 26.6 %collective-permute-start.16 = (s32[1,514]{1,0:T(1,128)}, s32[1,514]{1,0:T(1,128)}, u32[]{:S(2)}, u32[]{:S(2)}) collective-permute-start(s32[1,514]{1,0:T(1,128)} %get-tuple-element.49), channel_id=1, source_target_pairs={{0,1},{2,3},{4,5},{6,7}} | collective-permute-start | bytes 6176 | tf_op jit(solution)/shard_map/ppermute | solution.py:516
  82.7 38.0 %collective-permute-start = (f32[5,256,32]{1,2,0:T(8,128)}, f32[5,256,32]{1,2,0:T(8,128)}, u32[]{:S(2)}, u32[]{:S(2)}) collective-permute-start(f32[5,256,32]{1,2,0:T(8,128)} %copy.18), channel_id=1, source_target_pairs={{0,6},{2,0},{4,2},{6,4},{1,7},{3,1},{5,3},{7,5}} | collective-permute-start | bytes 491528 | tf_op jit(solution)/shard_map/ppermute | solution.py:520
  85.0 6.0 %collective-permute-start.4 = (f32[4,16,256,1]{2,1,3,0:T(8,128)}, f32[4,16,256,1]{2,1,3,0:T(8,128)}, u32[]{:S(2)}, u32[]{:S(2)}) collective-permute-start(f32[4,16,256,1]{2,1,3,0:T(8,128)} %copy.23), channel_id=1, source_target_pairs={{0,2},{2,4},{4,6},{6,0},{1,3},{3,5},{5,7},{7,1}} | collective-permute-start | bytes 196616 | tf_op jit(solution)/shard_map/ppermute | solution.py:530
  85.6 10.8 %collective-permute-start.3 = (f32[4,16,256,1]{2,1,3,0:T(8,128)}, f32[4,16,256,1]{2,1,3,0:T(8,128)}, u32[]{:S(2)}, u32[]{:S(2)}) collective-permute-start(f32[4,16,256,1]{2,1,3,0:T(8,128)} %copy.22), channel_id=1, source_target_pairs={{0,6},{2,0},{4,2},{6,4},{1,7},{3,1},{5,3},{7,5}} | collective-permute-start | bytes 196616 | tf_op jit(solution)/shard_map/ppermute | solution.py:529
  113.0 14.8 %collective-permute-start.6 = (f32[4,16,1,640]{3,2,1,0:T(1,128)}, f32[4,16,1,640]{3,2,1,0:T(1,128)}, u32[]{:S(2)}, u32[]{:S(2)}) collective-permute-start(f32[4,16,1,640]{3,2,1,0:T(1,128)} %get-tuple-element.28), channel_id=1, source_target_pairs={{1,0},{3,2},{5,4},{7,6}} | collective-permute-start | bytes 491528 | tf_op jit(solution)/shard_map/ppermute | solution.py:535
  114.3 13.5 %collective-permute-start.5 = (f32[4,16,1,640]{3,2,1,0:T(1,128)}, f32[4,16,1,640]{3,2,1,0:T(1,128)}, u32[]{:S(2)}, u32[]{:S(2)}) collective-permute-start(f32[4,16,1,640]{3,2,1,0:T(1,128)} %get-tuple-element.27), channel_id=1, source_target_pairs={{0,1},{2,3},{4,5},{6,7}} | collective-permute-start | bytes 491528 | tf_op jit(solution)/shard_map/ppermute | solution.py:536
  124.0 5.5 %collective-permute-start.2 = (f32[5,32,640]{2,1,0:T(8,128)S(1)}, f32[5,32,640]{2,1,0:T(8,128)S(1)}, u32[]{:S(2)}, u32[]{:S(2)}) collective-permute-start(f32[5,32,640]{2,1,0:T(8,128)S(1)} %fusion.21), channel_id=1, source_target_pairs={{0,1},{1,0},{2,3},{3,2},{4,5},{5,4},{6,7},{7,6}} | collective-permute-start | bytes 1228808 | tf_op jit(solution)/shard_map/ppermute | solution.py:525
  132.1 48.5 %copy-start.15 = (f32[256,512]{1,0:T(8,128)S(1)}, f32[256,512]{1,0:T(8,128)}, u32[]{:S(2)}) copy-start(f32[256,512]{1,0:T(8,128)} %get-tuple-element.54) | copy-start | bytes 1572868
  177.7 21.8 %collective-permute-start.8 = (f32[2,256,32]{2,1,0:T(8,128)S(1)}, f32[2,256,32]{2,1,0:T(8,128)S(1)}, u32[]{:S(2)}, u32[]{:S(2)}) collective-permute-start(f32[2,256,32]{2,1,0:T(8,128)S(1)} %get-tuple-element.48), channel_id=1, source_target_pairs={{0,2},{2,4},{4,6},{6,0},{1,3},{3,5},{5,7},{7,1}} | collective-permute-start | bytes 196616 | tf_op jit(solution)/shard_map/ppermute | solution.py:521
  178.4 21.1 %collective-permute-start.7 = (f32[2,256,32]{2,1,0:T(8,128)S(1)}, f32[2,256,32]{2,1,0:T(8,128)S(1)}, u32[]{:S(2)}, u32[]{:S(2)}) collective-permute-start(f32[2,256,32]{2,1,0:T(8,128)S(1)} %get-tuple-element.47), channel_id=1, source_target_pairs={{0,6},{2,0},{4,2},{6,4},{1,7},{3,1},{5,3},{7,5}} | collective-permute-start | bytes 196616 | tf_op jit(solution)/shard_map/ppermute | solution.py:520
  194.6 11.1 %collective-permute-start.19 = (f32[2,16,256,1]{2,1,3,0:T(8,128)S(1)}, f32[2,16,256,1]{2,1,3,0:T(8,128)S(1)}, u32[]{:S(2)}, u32[]{:S(2)}) collective-permute-start(f32[2,16,256,1]{2,1,3,0:T(8,128)S(1)} %copy.29), channel_id=1, source_target_pairs={{0,6},{2,0},{4,2},{6,4},{1,7},{3,1},{5,3},{7,5}} | collective-permute-start | bytes 98312 | tf_op jit(solution)/shard_map/ppermute | solution.py:512
  198.9 9.5 %collective-permute-start.18 = (f32[2,16,256,1]{2,1,3,0:T(8,128)S(1)}, f32[2,16,256,1]{2,1,3,0:T(8,128)S(1)}, u32[]{:S(2)}, u32[]{:S(2)}) collective-permute-start(f32[2,16,256,1]{2,1,3,0:T(8,128)S(1)} %copy.27), channel_id=1, source_target_pairs={{0,2},{2,4},{4,6},{6,0},{1,3},{3,5},{5,7},{7,1}} | collective-permute-start | bytes 98312 | tf_op jit(solution)/shard_map/ppermute | solution.py:513
  200.3 10.7 %collective-permute-start.9 = (f32[2,32,640]{2,1,0:T(8,128)}, f32[2,32,640]{2,1,0:T(8,128)}, u32[]{:S(2)}, u32[]{:S(2)}) collective-permute-start(f32[2,32,640]{2,1,0:T(8,128)} %fusion.22), channel_id=1, source_target_pairs={{0,1},{1,0},{2,3},{3,2},{4,5},{5,4},{6,7},{7,6}} | collective-permute-start | bytes 491528 | tf_op jit(solution)/shard_map/ppermute | solution.py:525
  205.7 50.0 %copy-start.16 = (f32[2,256,512]{2,1,0:T(8,128)S(1)}, f32[2,256,512]{2,1,0:T(8,128)}, u32[]{:S(2)}) copy-start(f32[2,256,512]{2,1,0:T(8,128)} %fusion.13) | copy-start | bytes 3145732
  208.4 48.7 %copy-start.11 = (s32[256,512]{1,0:T(8,128)S(1)}, s32[256,512]{1,0:T(8,128)}, u32[]{:S(2)}) copy-start(s32[256,512]{1,0:T(8,128)} %copy-done.10) | copy-start | bytes 1572868
  208.4 48.7 %copy-start.13 = (s32[256,512]{1,0:T(8,128)S(1)}, s32[256,512]{1,0:T(8,128)}, u32[]{:S(2)}) copy-start(s32[256,512]{1,0:T(8,128)} %copy-done.12) | copy-start | bytes 1572868
  211.0 44.7 %copy-start.17 = (f32[256,512]{1,0:T(8,128)S(1)}, f32[256,512]{1,0:T(8,128)}, u32[]{:S(2)}) copy-start(f32[256,512]{1,0:T(8,128)} %multiply_reduce_fusion) | copy-start | bytes 1572868
  211.0 44.7 %copy-start.18 = (f32[256,512]{1,0:T(8,128)S(1)}, f32[256,512]{1,0:T(8,128)}, u32[]{:S(2)}) copy-start(f32[256,512]{1,0:T(8,128)} %multiply_reduce_fusion.1) | copy-start | bytes 1572868
  276.2 12.1 %collective-permute-start.20 = (f32[2,16,256,1]{2,1,3,0:T(8,128)S(1)}, f32[2,16,256,1]{2,1,3,0:T(8,128)S(1)}, u32[]{:S(2)}, u32[]{:S(2)}) collective-permute-start(f32[2,16,256,1]{2,1,3,0:T(8,128)S(1)} %copy.31), channel_id=1, source_target_pairs={{0,2},{2,4},{4,6},{6,0},{1,3},{3,5},{5,7},{7,1}} | collective-permute-start | bytes 98312 | tf_op jit(solution)/shard_map/ppermute | solution.py:513
  279.6 59.8 %collective-permute-start.22 = (f32[2,16,1,514]{3,2,1,0:T(1,128)S(1)}, f32[2,16,1,514]{3,2,1,0:T(1,128)S(1)}, u32[]{:S(2)}, u32[]{:S(2)}) collective-permute-start(f32[2,16,1,514]{3,2,1,0:T(1,128)S(1)} %get-tuple-element.32), channel_id=1, source_target_pairs={{1,0},{3,2},{5,4},{7,6}} | collective-permute-start | bytes 197384 | tf_op jit(solution)/shard_map/ppermute | solution.py:515
  280.9 58.5 %collective-permute-start.21 = (f32[2,16,1,514]{3,2,1,0:T(1,128)S(1)}, f32[2,16,1,514]{3,2,1,0:T(1,128)S(1)}, u32[]{:S(2)}, u32[]{:S(2)}) collective-permute-start(f32[2,16,1,514]{3,2,1,0:T(1,128)S(1)} %get-tuple-element.31), channel_id=1, source_target_pairs={{0,1},{2,3},{4,5},{6,7}} | collective-permute-start | bytes 197384 | tf_op jit(solution)/shard_map/ppermute | solution.py:516
  286.7 14.3 %collective-permute-start.23 = (f32[2,16,256,1]{2,1,3,0:T(8,128)S(1)}, f32[2,16,256,1]{2,1,3,0:T(8,128)S(1)}, u32[]{:S(2)}, u32[]{:S(2)}) collective-permute-start(f32[2,16,256,1]{2,1,3,0:T(8,128)S(1)} %copy.35), channel_id=1, source_target_pairs={{0,6},{2,0},{4,2},{6,4},{1,7},{3,1},{5,3},{7,5}} | collective-permute-start | bytes 98312 | tf_op jit(solution)/shard_map/ppermute | solution.py:512
  303.7 35.7 %slice-start.4 = ((s8[8388608]{0:T(1024)(128)(4,1)}), s8[4194304]{0:T(1024)(128)(4,1)S(1)}, s32[]{:S(2)}) async-start(s8[8388608]{0:T(1024)(128)(4,1)} %bitcast.58), calls=%async_computation.4 | async-start | bytes 8388608
  305.3 27.9 %collective-permute-start.24 = (f32[2,16,1,514]{3,2,1,0:T(1,128)S(1)}, f32[2,16,1,514]{3,2,1,0:T(1,128)S(1)}, u32[]{:S(2)}, u32[]{:S(2)}) collective-permute-start(f32[2,16,1,514]{3,2,1,0:T(1,128)S(1)} %pad_maximum_fusion.34), channel_id=1, source_target_pairs={{0,1},{2,3},{4,5},{6,7}} | collective-permute-start | bytes 197384 | tf_op jit(solution)/shard_map/ppermute | solution.py:516
  (22 other events, 257.1 us)

commit v3 on v1

v3 whole, which is shorter than its diff:
```python
import functools

import jax
import jax.numpy as jnp
from jax import lax
from jax.experimental import pallas as pl
from jax.experimental.pallas import tpu as pltpu
from jax.sharding import PartitionSpec as P

GRAVITY = 1.0
TIME_STEP = 4.0
ALPHA_T = 0.02
BETA_S = 0.015
T_REF = 1.0
S_REF = 1.0
VISC_KV = 0.001
DIFF_KT = 0.0005

LEVELS = 16
NY = 256
NX = 512
WIDE = 32
SUB = 36
EXT_Y = 8 * SUB
EXT_X = 640
LANES = 128
CHUNKS = EXT_X // LANES
TILES = NY // 8
RING = 4
CONST_R = -BETA_S * S_REF + ALPHA_T * T_REF
MIB = 1024 * 1024

VMEM_SPEC = pl.BlockSpec(memory_space=pltpu.VMEM)
ANY_SPEC = pl.BlockSpec(memory_space=pl.ANY)


def f32(*shape):
    return jax.ShapeDtypeStruct(shape, jnp.float32)


def tile_rows(t):
    return pl.ds(pl.multiple_of(t * 8, 8), 8)


def chunk(c):
    return pl.ds(c * LANES, LANES)


def lanes(x, c):
    return x[:, c * LANES : (c + 1) * LANES]


def turn(x, shift):
    return x if shift % LANES == 0 else pltpu.roll(x, shift % LANES, 1)


def iotas():
    return lax.broadcasted_iota(jnp.int32, (8, LANES), 1), lax.broadcasted_iota(jnp.int32, (8, LANES), 0)


def start(copies):
    for copy in copies:
        copy.start()


def wait(copies):
    for copy in copies:
        copy.wait()


def shift_east(xs, after, lane):
    nxt = list(xs[1:]) + [after]
    return [pltpu.roll(jnp.where(lane == 0, n, x), LANES - 1, 1) for x, n in zip(xs, nxt)]


def shift_west(xs, before, lane):
    prv = [before] + list(xs[:-1])
    return [pltpu.roll(jnp.where(lane == LANES - 1, p, x), 1, 1) for x, p in zip(xs, prv)]


def shift_north(xs, above, sub):
    return [pltpu.roll(jnp.where(sub == 0, a, x), 7, 0) for x, a in zip(xs, above)]


def shift_south(xs, below, sub):
    return [pltpu.roll(jnp.where(sub == 7, b, x), 1, 0) for x, b in zip(xs, below)]


def side_planes(east, west, q, lane):
    return jnp.where(lane < WIDE, turn(east, -q), jnp.where(lane >= LANES - WIDE, turn(west, LANES - WIDE - q), 0.0))


def side_level(east, west, q, lane):
    return jnp.where(lane == 0, turn(east, -q), turn(west, LANES - 1 - q))


def pack_kernel(u_hbm, v_hbm, t_hbm, s_hbm, k_ref, h_ref, eta_ref, tu_ref, tv_ref, a1e, a1w, a2e, a2w, kf_ref, buf, sem):
    lane, _ = iotas()
    cubes = (u_hbm, v_hbm, t_hbm, s_hbm)
    strip = 64

    def copies(i, slot):
        return [pltpu.make_async_copy(cubes[a].at[:, pl.ds(i * strip, strip), chunk(3 * e)], buf.at[slot, a, e], sem.at[slot, a, e]) for a in range(4) for e in range(2)]

    start(copies(0, 0))
    for i in range(NY // strip):
        if i + 1 < NY // strip:
            start(copies(i + 1, (i + 1) % 2))
        wait(copies(i, i % 2))

        @pl.loop(0, strip // 8)
        def _(t):
            here = tile_rows(t)
            rows = pl.ds(pl.multiple_of(i * strip + t * 8, 8), 8)
            west = jnp.zeros((8, LANES), jnp.float32)
            east = jnp.zeros((8, LANES), jnp.float32)
            for a in range(4):
                for k in range(LEVELS):
                    q = a * LEVELS + k
                    west = jnp.where(lane == q, turn(buf[i % 2, a, 0, k, here, :], q), west)
                    east = jnp.where(lane == q, turn(buf[i % 2, a, 1, k, here, :], q + 1), east)
            kf = k_ref[rows, :].astype(jnp.float32)
            kf_ref[rows, :] = kf
            west2 = jnp.zeros((8, LANES), jnp.float32)
            east2 = jnp.zeros((8, LANES), jnp.float32)
            for q, plane in ((64, kf), (96, h_ref[rows, :])):
                inside = (lane >= q) & (lane < q + WIDE)
                west = jnp.where(inside, turn(lanes(plane, 0), q), west)
                east = jnp.where(inside, turn(lanes(plane, 3), q - LANES + WIDE), east)
            for q, plane in ((0, eta_ref[rows, :]), (32, tu_ref[rows, :]), (64, tv_ref[rows, :])):
                inside = (lane >= q) & (lane < q + WIDE)
                west2 = jnp.where(inside, turn(lanes(plane, 0), q), west2)
                east2 = jnp.where(inside, turn(lanes(plane, 3), q - LANES + WIDE), east2)
            a1e[rows, :] = east
            a1w[rows, :] = west
            a2e[rows, :] = east2
            a2w[rows, :] = west2


def pack(u, v, temp, salt, k, h, eta, tu, tv):
    return pl.pallas_call(
        pack_kernel,
        out_shape=[f32(NY, LANES)] * 4 + [f32(NY, NX)],
        in_specs=[ANY_SPEC] * 4 + [VMEM_SPEC] * 5,
        out_specs=[VMEM_SPEC] * 5,
        scratch_shapes=[pltpu.VMEM((2, 4, 2, LEVELS, 64, LANES), jnp.float32), pltpu.SemaphoreType.DMA((2, 4, 2))],
        compiler_params=pltpu.CompilerParams(vmem_limit_bytes=24 * MIB),
        name="pack",
    )(u, v, temp, salt, k, h, eta, tu, tv)


def exchange_kernel(n_cols, n_packs, n_planes, n_cubes, *refs):
    n_src = 2 * n_packs + n_planes + n_cubes
    srcs, refs = refs[:n_src], refs[n_src:]
    n_dst = 2 * n_packs + (n_planes > 0) + (n_cubes > 0)
    dsts, (send_sem, recv_sem) = list(refs[:n_dst]), refs[n_dst:]
    pack_e, pack_w = srcs[:n_packs], srcs[n_packs : 2 * n_packs]
    planes, cubes = srcs[2 * n_packs : 2 * n_packs + n_planes], srcs[2 * n_packs + n_planes :]
    from_e, from_w = dsts[:n_packs], dsts[n_packs : 2 * n_packs]
    col = lax.axis_index("col")
    row = lax.axis_index("row")
    east = lax.rem(col + 1, n_cols)
    west = lax.rem(col + n_cols - 1, n_cols)
    peers = [(east, row), (west, row), (col, 1 - row), (east, 1 - row), (west, 1 - row)]
    barrier = pltpu.get_barrier_semaphore()
    for peer in peers:
        pl.semaphore_signal(barrier, inc=1, device_id=peer, device_id_type=pl.DeviceIdType.MESH)
    pl.semaphore_wait(barrier, len(peers))
    edge = pl.multiple_of((1 - row) * (NY - WIDE), 8)
    moves = []
    for p in range(n_packs):
        moves.append((pack_e[p], from_w[p].at[pl.ds(0, NY), :], peers[0]))
        moves.append((pack_w[p], from_e[p].at[pl.ds(0, NY), :], peers[1]))
    for p in range(n_packs):
        moves.append((pack_e[p].at[pl.ds(edge, WIDE), :], from_w[p].at[pl.ds(NY, WIDE), :], peers[3]))
        moves.append((pack_w[p].at[pl.ds(edge, WIDE), :], from_e[p].at[pl.ds(NY, WIDE), :], peers[4]))
    for p in range(n_planes):
        moves.append((planes[p].at[pl.ds(edge, WIDE), :], dsts[2 * n_packs].at[p], peers[2]))
    tile = pl.multiple_of((1 - row) * (NY - 8), 8)
    for p in range(n_cubes):
        moves.append((cubes[p].at[:, pl.ds(tile, 8), :], dsts[2 * n_packs + (n_planes > 0)].at[p], peers[2]))
    copies = [
        pltpu.make_async_remote_copy(src_ref=src, dst_ref=dst, send_sem=send_sem.at[i], recv_sem=recv_sem.at[i], device_id=peer, device_id_type=pl.DeviceIdType.MESH)
        for i, (src, dst, peer) in enumerate(moves)
    ]
    start(copies)
    wait(copies)


def exchange(n_cols, name, collective_id, packs_e, packs_w, planes, cubes):
    n_packs, n_planes, n_cubes = len(packs_e), len(planes), len(cubes)
    n_moves = 4 * n_packs + n_planes + n_cubes
    outs = [f32(EXT_Y, LANES)] * (2 * n_packs)
    if n_planes:
        outs.append(f32(n_planes, WIDE, NX))
    if n_cubes:
        outs.append(f32(n_cubes, LEVELS, 8, NX))
    return pl.pallas_call(
        functools.partial(exchange_kernel, n_cols, n_packs, n_planes, n_cubes),
        out_shape=outs,
        in_specs=[ANY_SPEC] * (2 * n_packs + n_planes + n_cubes),
        out_specs=[ANY_SPEC] * len(outs),
        scratch_shapes=[pltpu.SemaphoreType.DMA((n_moves,)), pltpu.SemaphoreType.DMA((n_moves,))],
        compiler_params=pltpu.CompilerParams(collective_id=collective_id, has_side_effects=True, vmem_limit_bytes=4 * MIB),
        name=name,
    )(*packs_e, *packs_w, *planes, *cubes)


def predict_kernel(kf_ref, hf_ref, rows_ref, east_ref, west_ref, u_hbm, v_hbm, t_hbm, s_hbm, hy_hbm, ustar_hbm, vstar_hbm, tmix_hbm, smix_hbm, force_ref, usum_ref, be_ref, bw_ref, ring, kh, geo, carry, stage, part, in_sem, out_sem):
    row = lax.axis_index("row")
    lane, sub = iotas()
    cubes = (u_hbm, v_hbm, t_hbm, s_hbm)
    outs = (ustar_hbm, vstar_hbm, tmix_hbm, smix_hbm)

    def tile_copies(t, slot):
        rows = pl.ds(pl.multiple_of(t * 8, 8), 8)
        return [pltpu.make_async_copy(cubes[a].at[:, rows, :], ring.at[slot, a], in_sem.at[slot, a]) for a in range(4)]

    def edge_copies(slot):
        return [pltpu.make_async_copy(hy_hbm.at[a], ring.at[slot, a], in_sem.at[slot, a]) for a in range(4)]

    def out_copies(t, slot):
        rows = pl.ds(pl.multiple_of(t * 8, 8), 8)
        return [pltpu.make_async_copy(stage.at[slot, a], outs[a].at[:, rows, :], out_sem.at[slot, a]) for a in range(4)]

    start(edge_copies(RING - 1))
    start(tile_copies(0, 0))
    start(tile_copies(1, 1))
    start(tile_copies(2, 2))

    @pl.loop(0, TILES)
    def _(t):
        kh[0, tile_rows(t), pl.ds(0, NX)] = kf_ref[tile_rows(t), :]
        kh[1, tile_rows(t), pl.ds(0, NX)] = hf_ref[tile_rows(t), :]

    kh[0, pl.ds(NY, WIDE), pl.ds(0, NX)] = rows_ref[0]
    kh[1, pl.ds(NY, WIDE), pl.ds(0, NX)] = rows_ref[1]

    @pl.loop(0, SUB)
    def _(t):
        for q in range(2):
            kh[q, tile_rows(t), chunk(4)] = side_planes(east_ref[tile_rows(t), :], west_ref[tile_rows(t), :], 64 + WIDE * q, lane)

    cut = jnp.where(row == 0, EXT_Y - 1, NY - 1)

    def layout(t, t_next):
        k = [lanes(kh[0, tile_rows(t), :], c) for c in range(CHUNKS)]
        h = [lanes(kh[1, tile_rows(t), :], c) for c in range(CHUNKS)]
        kn = [lanes(kh[0, tile_rows(t_next), :], c) for c in range(CHUNKS)]
        hn = [lanes(kh[1, tile_rows(t_next), :], c) for c in range(CHUNKS)]
        dz = [a / jnp.maximum(b, 1.0) for a, b in zip(h, k)]
        dzn = [a / jnp.maximum(b, 1.0) for a, b in zip(hn, kn)]
        k_e = shift_east(k, k[0], lane)
        dz_e = shift_east(dz, dz[0], lane)
        k_n = [jnp.where(sub + t * 8 == cut, 0.0, x) for x in shift_north(k, kn, sub)]
        dz_n = shift_north(dz, dzn, sub)
        for c in range(CHUNKS):
            at = pl.ds(c * LANES, LANES)
            k_u = jnp.minimum(k[c], k_e[c])
            k_v = jnp.minimum(k[c], k_n[c])
            dz_u = 0.5 * (dz[c] + dz_e[c])
            dz_v = 0.5 * (dz[c] + dz_n[c])
            geo[0, t, :, at] = k[c]
            geo[1, t, :, at] = k_u
            geo[2, t, :, at] = k_v
            geo[3, t, :, at] = dz[c]
            geo[4, t, :, at] = dz_u
            geo[5, t, :, at] = dz_v
            safe_c = jnp.where(k[c] > 0, dz[c], 1.0)
            safe_u = jnp.where(k_u > 0, dz_u, 1.0)
            safe_v = jnp.where(k_v > 0, dz_v, 1.0)
            geo[6, t, :, at] = (TIME_STEP * DIFF_KT) / (safe_c * safe_c)
            geo[7, t, :, at] = (TIME_STEP * VISC_KV) / (safe_u * safe_u)
            geo[8, t, :, at] = (TIME_STEP * VISC_KV) / (safe_v * safe_v)

    @pl.loop(0, SUB - 1)
    def _(t):
        layout(t, t + 1)

    layout(SUB - 1, 0)
    wall = jnp.where(row == 0, SUB - 1, TILES)
    for q in range(3):
        geo[q, wall] = jnp.zeros((8, EXT_X), jnp.float32)

    def body(t, slot_now, slot_next, first, work):
        g_next = lax.rem(t + 1 + SUB, SUB)

        def plane(q, tt, n):
            return [geo[q, tt, :, pl.ds(c * LANES, LANES)] for c in range(n)]

        k1 = plane(0, g_next, 5)
        ku1 = plane(1, g_next, 5)
        kv1 = plane(2, g_next, 5)
        dz1 = [(TIME_STEP * GRAVITY) * x for x in plane(3, g_next, 5)]
        csum = [jnp.zeros((8, LANES), jnp.float32)] * 5
        side_e = east_ref[tile_rows(g_next), :]
        side_w = west_ref[tile_rows(g_next), :]
        if work:
            kc0 = plane(0, t, 4)
            ku0 = plane(1, t, 4)
            kv0 = plane(2, t, 4)
            cc = plane(6, t, 4)
            cu = plane(7, t, 4)
            cv = plane(8, t, 4)
            zero = [jnp.zeros((8, LANES), jnp.float32)] * 4
            one = [jnp.ones((8, LANES), jnp.float32)] * 4
            chains = {n: {"q": one, "cl": zero, "parts": {}} for n in "cuv"}
            prev = {n: zero for n in ("u", "v", "T", "S")}
            total_m = {"u": zero, "v": zero}

        for k in range(LEVELS):

            def tile(slot, a, n):
                got = [ring[slot, a, k, :, pl.ds(c * LANES, LANES)] for c in range(4)]
                return got + [side_level(side_e, side_w, a * LEVELS + k, lane)] if n == 5 else got

            raw_u, raw_v, raw_t, raw_s = (tile(slot_next, a, 5) for a in range(4))
            um1 = [jnp.where(m > k, x, 0.0) for m, x in zip(ku1, raw_u)]
            vm1 = [jnp.where(m > k, x, 0.0) for m, x in zip(kv1, raw_v)]
            half = [jnp.where(m > k, (0.5 * BETA_S) * s - (0.5 * ALPHA_T) * x + 0.5 * CONST_R, 0.0) for m, x, s in zip(k1, raw_t, raw_s)]
            mid = [a + b for a, b in zip(csum, half)]
            csum = [a + b for a, b in zip(mid, half)]
            p1 = [a * b for a, b in zip(mid, dz1)]
            u_w = shift_west(um1, um1[4], lane)
            e1 = [(a + b) * (a + b) + p for a, b, p in zip(u_w, um1, p1)]
            e_e = shift_east(e1[:4], e1[4], lane)
            ed1 = [a - b for a, b in zip(e_e, e1)]
            v_e = shift_east(vm1, vm1[0], lane)
            ve1 = [a + b for a, b in zip(vm1, v_e)]
            old = lambda q, n: [carry[q, k, :, pl.ds(c * LANES, LANES)] for c in range(n)]
            if first:
                b1 = [jnp.zeros((8, LANES), jnp.float32)] * 4
            else:
                vm0 = old(1, 4)
                um0 = old(0, 5)
                ve0 = old(2, 5)
                v_s = shift_south(vm1[:4], vm0, sub)
                b1 = [(a + b) * (a + b) + p for a, b, p in zip(v_s, vm1, p1)]
                u_n = shift_north(um0, um1, sub)
                q0 = [(a + b) * x for a, b, x in zip(um0, u_n, ve0)]
            if work:
                ed0 = old(3, 4)
                b0 = old(4, 4)
                q_s = shift_south(q0[:4], old(5, 4), sub)
                q_w = shift_west(q0[:4], q0[4], lane)
                b_n = shift_north(b0, b1, sub)
                src = {
                    "u": [jnp.where(m > k, u - (e + (q - s)), 0.0) for m, u, e, q, s in zip(ku0, um0, ed0, q0, q_s)],
                    "v": [jnp.where(m > k, v - ((bn - b) + (q - w)), 0.0) for m, v, bn, b, q, w in zip(kv0, vm0, b_n, b0, q0, q_w)],
                    "T": [jnp.where(m > k, x, 0.0) for m, x in zip(kc0, tile(slot_now, 2, 4))],
                    "S": [jnp.where(m > k, x, 0.0) for m, x in zip(kc0, tile(slot_now, 3, 4))],
                }
                total_m = {"u": [a + b for a, b in zip(total_m["u"], um0)], "v": [a + b for a, b in zip(total_m["v"], vm0)]}
                for name, coef, mask, fields in (("u", cu, ku0, "u"), ("v", cv, kv0, "v"), ("c", cc, kc0, "TS")):
                    chain = chains[name]
                    down = [jnp.where(m > k + 1, c, 0.0) for m, c in zip(mask, coef)] if k < LEVELS - 1 else zero
                    inv = [1.0 / (q + d) for q, d in zip(chain["q"], down)]
                    gain = [d * r for d, r in zip(down, inv)]
                    for f in fields:
                        prev[f] = [(s + l * p) * r for s, l, p, r in zip(src[f], chain["cl"], prev[f], inv)]
                        for c in range(4):
                            part["uvTS".index(f), k, :, pl.ds(c * LANES, LANES)] = prev[f][c]
                    for c in range(4):
                        part[4 + "uvc".index(name), k, :, pl.ds(c * LANES, LANES)] = gain[c]
                    chain["q"] = [1.0 + g * q for g, q in zip(gain, chain["q"])]
                    chain["cl"] = down
            new = [(0, um1, 5), (1, vm1, 4), (2, ve1, 5), (3, ed1, 4), (4, b1, 4)]
            if not first:
                new.append((5, q0, 4))
            for q, vals, n in new:
                for c in range(n):
                    carry[q, k, :, pl.ds(c * LANES, LANES)] = vals[c]

        if not work:
            return
        out_slot = lax.rem(t, 2)
        below = dict(prev)
        pack_e = jnp.zeros((8, LANES), jnp.float32)
        pack_w = jnp.zeros((8, LANES), jnp.float32)

        def put(k, f, vals):
            nonlocal pack_e, pack_w
            if f == "v":
                return
            q = 2 * WIDE + "TSu".index(f) * LEVELS + k
            pack_e = jnp.where(lane == q, turn(vals[3], q + 1), pack_e)
            if f != "u":
                pack_w = jnp.where(lane == q, turn(vals[0], q), pack_w)

        total = {"u": below["u"], "v": below["v"]}
        for f in "uvTS":
            for c in range(4):
                stage[out_slot, "uvTS".index(f), LEVELS - 1, :, pl.ds(c * LANES, LANES)] = below[f][c]
            put(LEVELS - 1, f, below[f])
        for k in range(LEVELS - 2, -1, -1):
            for f in "uvTS":
                a = "uvTS".index(f)
                g = 4 + "uvcc".index({"u": "u", "v": "v", "T": "c", "S": "c"}[f])
                here = []
                for c in range(4):
                    at = pl.ds(c * LANES, LANES)
                    val = part[a, k, :, at] + part[g, k, :, at] * below[f][c]
                    stage[out_slot, a, k, :, at] = val
                    here.append(val)
                below[f] = here
                put(k, f, here)
                if f in total:
                    total[f] = [x + y for x, y in zip(total[f], here)]
        rows = pl.ds(pl.multiple_of(t * 8, 8), 8)
        dzu = plane(4, t, 4)
        dzv = plane(5, t, 4)
        for q, (f, dz) in enumerate((("u", dzu), ("v", dzv))):
            force = [(1.0 / TIME_STEP) * (dz[c] * (total[f][c] - total_m[f][c])) for c in range(4)]
            for c in range(4):
                force_ref[q, rows, chunk(c)] = force[c]
                usum_ref[q, rows, chunk(c)] = dz[c] * total[f][c]
            inside = (lane >= WIDE * q) & (lane < WIDE * (q + 1))
            pack_e = jnp.where(inside, turn(force[3], WIDE * q - LANES + WIDE), pack_e)
            pack_w = jnp.where(inside, turn(force[0], WIDE * q), pack_w)
        be_ref[rows, :] = pack_e
        bw_ref[rows, :] = pack_w

    wait(edge_copies(RING - 1))
    body(-2, 0, RING - 1, True, False)
    wait(tile_copies(0, 0))
    body(-1, RING - 1, 0, False, False)

    @pl.loop(0, TILES)
    def _(t):
        @pl.when(t + 3 < TILES)
        def _():
            start(tile_copies(t + 3, lax.rem(t + 3, RING)))

        @pl.when(t + 3 == TILES)
        def _():
            start(edge_copies(TILES % RING))

        @pl.when(t >= 2)
        def _():
            wait(out_copies(t - 2, lax.rem(t, 2)))

        @pl.when(t + 1 < TILES)
        def _():
            wait(tile_copies(t + 1, lax.rem(t + 1, RING)))

        @pl.when(t + 1 == TILES)
        def _():
            wait(edge_copies(TILES % RING))

        body(t, lax.rem(t, RING), lax.rem(t + 1, RING), False, True)
        start(out_copies(t, lax.rem(t, 2)))

    wait(out_copies(TILES - 2, 0))
    wait(out_copies(TILES - 1, 1))


def predict(kf, hf, rows, east, west, u, v, temp, salt, hy):
    return pl.pallas_call(
        predict_kernel,
        out_shape=[f32(LEVELS, NY, NX)] * 4 + [f32(2, NY, NX)] * 2 + [f32(NY, LANES)] * 2,
        in_specs=[VMEM_SPEC] * 5 + [ANY_SPEC] * 5,
        out_specs=[ANY_SPEC] * 4 + [VMEM_SPEC] * 4,
        scratch_shapes=[
            pltpu.VMEM((RING, 4, LEVELS, 8, NX), jnp.float32),
            pltpu.VMEM((2, EXT_Y, EXT_X), jnp.float32),
            pltpu.VMEM((9, SUB, 8, EXT_X), jnp.float32),
            pltpu.VMEM((6, LEVELS, 8, EXT_X), jnp.float32),
            pltpu.VMEM((2, 4, LEVELS, 8, NX), jnp.float32),
            pltpu.VMEM((7, LEVELS, 8, NX), jnp.float32),
            pltpu.SemaphoreType.DMA((RING, 4)),
            pltpu.SemaphoreType.DMA((2, 4)),
        ],
        compiler_params=pltpu.CompilerParams(vmem_limit_bytes=48 * MIB),
        name="predict",
    )(kf, hf, rows, east, west, u, v, temp, salt, hy)


def east_of(x):
    return pltpu.roll(x, EXT_X - 1, 1)


def west_of(x):
    return pltpu.roll(x, 1, 1)


def north_wrap(x):
    return pltpu.roll(x, 7, 0)


def south_wrap(x):
    return pltpu.roll(x, 1, 0)


def finish_kernel(n_sub, tide_ref, a1_e, a1_w, a2_e, a2_w, b_e, b_w, usum_ref, kf_hbm, h_hbm, eta_in, tu_in, tv_in, rows_a, force_hbm, rows_b, ustar_hbm, vstar_hbm, tmix_hbm, smix_hbm, tiles_b, eta_hbm, u_hbm, v_hbm, uc_hbm, vc_hbm, tn_hbm, sn_hbm, nat, eta, u, v, au, fu, av, fv, ub, vb, cube, fy_old, stage, nat_sem, cube_sem, tile_sem, plane_sem, out_sem):
    dt_sub = TIME_STEP / n_sub
    weight_norm = 6.0 / (n_sub * (n_sub + 1) * (n_sub + 2))
    row = lax.axis_index("row")
    lane, sub = iotas()

    def plane_copies():
        copies = []
        for p, src in enumerate((kf_hbm, h_hbm, eta_in, tu_in, tv_in, force_hbm.at[0], force_hbm.at[1])):
            edge = rows_a.at[p] if p < 5 else rows_b.at[p - 5]
            for c in range(4):
                copies.append(pltpu.make_async_copy(src.at[:, chunk(c)], nat.at[p, c, pl.ds(0, NY), :], nat_sem.at[0, p, c]))
                copies.append(pltpu.make_async_copy(edge.at[:, chunk(c)], nat.at[p, c, pl.ds(NY, WIDE), :], nat_sem.at[1, p, c]))
        return copies

    cubes = (ustar_hbm, vstar_hbm, tmix_hbm, smix_hbm)
    strip = 64

    def cube_copies(i):
        rows = pl.ds(pl.multiple_of(i * strip, 8), strip)
        return [pltpu.make_async_copy(cubes[a].at[:, rows, :], cube.at[a, :, rows, :], cube_sem.at[a, i]) for a in range(4)]

    edge_copies = [pltpu.make_async_copy(tiles_b.at[i], cube.at[a, :, pl.ds(NY, 8), :], tile_sem.at[i]) for i, a in enumerate((1, 2, 3))]

    start(plane_copies())
    start(edge_copies)
    for i in range(NY // strip):
        start(cube_copies(i))

    @pl.loop(0, SUB)
    def _(t):
        rows = tile_rows(t)
        packs = [(a1_e[rows, :], a1_w[rows, :]), (a2_e[rows, :], a2_w[rows, :]), (b_e[rows, :], b_w[rows, :])]
        for p, (s, q) in enumerate(((0, 64), (0, 96), (1, 0), (1, 32), (1, 64), (2, 0), (2, 32))):
            nat[p, 4, rows, :] = side_planes(packs[s][0], packs[s][1], q, lane)

    wait(plane_copies())

    def plane(p, t):
        return jnp.concatenate([nat[p, c, pl.ds(t, 8, stride=SUB), :] for c in range(CHUNKS)], axis=1)

    cut = jnp.where(row == 0, EXT_Y - 1, NY - 1)
    sub_id = lax.broadcasted_iota(jnp.int32, (8, EXT_X), 0)

    def prepare(t, k_next, h_next):
        k = plane(0, t)
        dz = plane(1, t) / jnp.maximum(k, 1.0)
        k_n = jnp.where(sub_id * SUB + t == cut, 0.0, k_next)
        dz_n = h_next / jnp.maximum(k_next, 1.0)
        k_e = east_of(k)
        dz_e = east_of(dz)
        k_u = jnp.minimum(k, k_e)
        k_v = jnp.minimum(k, k_n)
        depth_u = k_u * (0.5 * (dz + dz_e))
        depth_v = k_v * (0.5 * (dz + dz_n))
        wet_u = k_u > 0
        wet_v = k_v > 0
        eta[t] = jnp.where(k > 0, plane(2, t), 0.0)
        u[t] = jnp.where(wet_u, dt_sub * plane(3, t), 0.0)
        v[t] = jnp.where(wet_v, dt_sub * plane(4, t), 0.0)
        au[t] = (dt_sub * dt_sub) * jnp.where(wet_u, depth_u, 0.0)
        av[t] = (dt_sub * dt_sub) * jnp.where(wet_v, depth_v, 0.0)
        fu[t] = jnp.where(wet_u, (dt_sub * dt_sub) * plane(5, t), 0.0)
        fv[t] = jnp.where(wet_v, (dt_sub * dt_sub) * plane(6, t), 0.0)
        ub[t] = jnp.zeros((8, EXT_X), jnp.float32)
        vb[t] = jnp.zeros((8, EXT_X), jnp.float32)

    @pl.loop(0, SUB - 1)
    def _(t):
        prepare(t, plane(0, t + 1), plane(1, t + 1))

    prepare(SUB - 1, north_wrap(plane(0, 0)), north_wrap(plane(1, 0)))

    @pl.loop(0, n_sub)
    def _(n):
        tide_x = tide_ref[n, 0]
        tide_y = tide_ref[n, 1]
        weight = (weight_norm / dt_sub) * ((n + 1) * (n_sub - n)).astype(jnp.float32)

        def level(t, v_south):
            u_now = u[t]
            v_now = v[t]
            return eta[t] - ((u_now - west_of(u_now)) + (v_now - v_south)), v_now

        def accelerate(t, eta_now, eta_north):
            u_new = u[t] + (au[t] * ((tide_x + eta_now) - east_of(eta_now)) + fu[t])
            v_new = v[t] + (av[t] * ((tide_y + eta_now) - eta_north) + fv[t])
            u[t] = u_new
            v[t] = v_new
            ub[t] = ub[t] + weight * u_new
            vb[t] = vb[t] + weight * v_new

        eta_first, v_first = level(0, south_wrap(v[SUB - 1]))
        eta[0] = eta_first

        def sweep(t, carry):
            eta_now, v_now = carry
            eta_north, v_north = level(t + 1, v_now)
            eta[t + 1] = eta_north
            accelerate(t, eta_now, eta_north)
            return eta_north, v_north

        carry = (eta_first, v_first)
        for t in range(SUB - 1):
            carry = sweep(t, carry)
        eta_last = carry[0]
        accelerate(SUB - 1, eta_last, north_wrap(eta_first))

    @pl.loop(0, SUB)
    def _(t):
        wet = plane(0, t) > 0
        for q, val in enumerate((jnp.where(wet, eta[t], 0.0), (1.0 / dt_sub) * u[t], (1.0 / dt_sub) * v[t], ub[t], vb[t])):
            for c in range(CHUNKS):
                nat[2 + q, c, pl.ds(t, 8, stride=SUB), :] = lanes(val, c)

    plane_outs = [pltpu.make_async_copy(nat.at[2 + q, c, pl.ds(0, NY), :], out.at[:, chunk(c)], plane_sem.at[q, c]) for q, out in enumerate((eta_hbm, u_hbm, v_hbm)) for c in range(4)]
    start(plane_outs)

    def faces(t, t_next):
        k = [nat[0, c, tile_rows(t), :] for c in range(CHUNKS)]
        kn = [nat[0, c, tile_rows(t_next), :] for c in range(4)]
        dz = [nat[1, c, tile_rows(t), :] / jnp.maximum(k[c], 1.0) for c in range(CHUNKS)]
        dzn = [nat[1, c, tile_rows(t_next), :] / jnp.maximum(kn[c], 1.0) for c in range(4)]
        k_e = shift_east(k, k[0], lane)
        dz_e = shift_east(dz, dz[0], lane)
        k_n = [jnp.where(sub + t * 8 == cut, 0.0, x) for x in shift_north(k[:4], kn, sub)]
        dz_n = shift_north(dz[:4], dzn, sub)
        k_u = [jnp.minimum(a, b) for a, b in zip(k, k_e)]
        k_v = [jnp.minimum(a, b) for a, b in zip(k, k_n)]
        dz_u = [0.5 * (a + b) for a, b in zip(dz, dz_e)]
        dz_v = [0.5 * (a + b) for a, b in zip(dz, dz_n)]
        return k, k_u, k_v, dz_u, dz_v

    def correction(mean, total, k, dz):
        depth = k * dz
        return (mean - total) / jnp.where(depth > 0, depth, 1.0)

    def cube_tile(a, t, k):
        return [cube[a, k, tile_rows(t), chunk(c)] for c in range(4)]

    wait(edge_copies)
    wait(cube_copies(0))

    _, _, kv_low, _, dzv_low = faces(SUB - 1, 0)
    low = [jnp.zeros((8, LANES), jnp.float32)] * 4
    for k in range(LEVELS):
        low = [a + b for a, b in zip(low, cube_tile(1, TILES, k))]
    dv_low = [correction(nat[6, c, tile_rows(SUB - 1), :], dzv_low[c] * low[c], kv_low[c], dzv_low[c]) for c in range(4)]
    for k in range(LEVELS):
        vc = [jnp.where(m > k, x + d, 0.0) for m, x, d in zip(kv_low, cube_tile(1, TILES, k), dv_low)]
        for f in range(2):
            x = cube_tile(2 + f, TILES, k)
            x_n = shift_north(x, cube_tile(2 + f, 0, k), sub)
            for c in range(4):
                fy_old[f, k, :, chunk(c)] = vc[c] * (x[c] + x_n[c])

    outs = (uc_hbm, vc_hbm, tn_hbm, sn_hbm)

    def out_copies(t, slot):
        return [pltpu.make_async_copy(stage.at[slot, a], outs[a].at[:, tile_rows(t), :], out_sem.at[slot, a]) for a in range(4)]

    @pl.loop(0, TILES)
    def _(t):
        slot = lax.rem(t, 2)

        @pl.when(t >= 2)
        def _():
            wait(out_copies(t - 2, slot))

        for i in range(1, NY // strip):

            @pl.when(t == i * (strip // 8) - 1)
            def _():
                wait(cube_copies(i))

        kc, ku, kv, dz_u, dz_v = faces(t, t + 1)
        east = b_e[tile_rows(t), :]
        west = b_w[tile_rows(t), :]
        rows = tile_rows(t)
        side_u = [turn(west, LANES - 1 - (2 * WIDE + 2 * LEVELS + k)) for k in range(LEVELS)]
        side_sum = functools.reduce(lambda a, b: a + b, side_u)
        du = [correction(nat[5, c, rows, :], usum_ref[0, rows, chunk(c)] if c < 4 else dz_u[4] * side_sum, ku[c], dz_u[c]) for c in range(CHUNKS)]
        dv = [correction(nat[6, c, rows, :], usum_ref[1, rows, chunk(c)], kv[c], dz_v[c]) for c in range(4)]
        for k in range(LEVELS):
            uc = [jnp.where(m > k, x + d, 0.0) for m, x, d in zip(ku, cube_tile(0, t, k) + [side_u[k]], du)]
            vc = [jnp.where(m > k, x + d, 0.0) for m, x, d in zip(kv, cube_tile(1, t, k), dv)]
            for c in range(4):
                stage[slot, 0, k, :, chunk(c)] = uc[c]
                stage[slot, 1, k, :, chunk(c)] = vc[c]
            for f in range(2):
                x = cube_tile(2 + f, t, k) + [side_level(east, west, 2 * WIDE + f * LEVELS + k, lane)]
                x_e = shift_east(x, x[0], lane)
                x_n = shift_north(x[:4], cube_tile(2 + f, t + 1, k), sub)
                fx = [a * (b + e) for a, b, e in zip(uc, x, x_e)]
                fy = [a * (b + n) for a, b, n in zip(vc, x, x_n)]
                fx_w = shift_west(fx[:4], fx[4], lane)
                fy_s = shift_south(fy, [fy_old[f, k, :, chunk(c)] for c in range(4)], sub)
                for c in range(4):
                    fy_old[f, k, :, chunk(c)] = fy[c]
                    step = (fx[c] - fx_w[c]) + (fy[c] - fy_s[c])
                    stage[slot, 2 + f, k, :, chunk(c)] = jnp.where(kc[c] > k, x[c] - (0.5 * TIME_STEP) * step, 0.0)
        start(out_copies(t, slot))

    wait(out_copies(TILES - 2, 0))
    wait(out_copies(TILES - 1, 1))
    wait(plane_outs)


def finish(tide_force, packs, usum, planes, rows_a, force, rows_b, cubes, tiles_b):
    n_sub = tide_force.shape[0]
    big = pltpu.VMEM((SUB, 8, EXT_X), jnp.float32)
    return pl.pallas_call(
        functools.partial(finish_kernel, n_sub),
        out_shape=[f32(NY, NX)] * 3 + [f32(LEVELS, NY, NX)] * 4,
        in_specs=[pl.BlockSpec(memory_space=pltpu.SMEM)] + [VMEM_SPEC] * 7 + [ANY_SPEC] * 13,
        out_specs=[ANY_SPEC] * 7,
        scratch_shapes=[pltpu.VMEM((7, CHUNKS, EXT_Y, LANES), jnp.float32)]
        + [big] * 9
        + [
            pltpu.VMEM((4, LEVELS, NY + 8, NX), jnp.float32),
            pltpu.VMEM((2, LEVELS, 8, NX), jnp.float32),
            pltpu.VMEM((2, 4, LEVELS, 8, NX), jnp.float32),
            pltpu.SemaphoreType.DMA((2, 7, 4)),
            pltpu.SemaphoreType.DMA((4, 4)),
            pltpu.SemaphoreType.DMA((3,)),
            pltpu.SemaphoreType.DMA((3, 4)),
            pltpu.SemaphoreType.DMA((2, 4)),
        ],
        compiler_params=pltpu.CompilerParams(vmem_limit_bytes=60 * MIB),
        name="finish",
    )(tide_force, *packs, usum, *planes, rows_a, force, rows_b, *cubes, tiles_b)


def solution(mesh):
    n_cols = mesh.shape["col"]

    def local_step(vel_u, vel_v, value_a11, salinity, sea_level, trans_u, trans_v, bathymetry, kmt_levels, tide_force):
        a1e, a1w, a2e, a2w, kf = pack(vel_u, vel_v, value_a11, salinity, kmt_levels, bathymetry, sea_level, trans_u, trans_v)
        planes = (kf, bathymetry, sea_level, trans_u, trans_v)
        e1, e2, w1, w2, rows_a, tiles_a = exchange(n_cols, "exchange_inputs", 0, (a1e, a2e), (a1w, a2w), planes, (vel_u, vel_v, value_a11, salinity))
        u_star, v_star, temp_mix, salt_mix, force, usum, be, bw = predict(kf, bathymetry, rows_a, e1, w1, vel_u, vel_v, value_a11, salinity, tiles_a)
        e3, w3, rows_b, tiles_b = exchange(n_cols, "exchange_forcing", 1, (be,), (bw,), (force[0], force[1]), (v_star, temp_mix, salt_mix))
        return tuple(finish(tide_force, (e1, w1, e2, w2, e3, w3), usum, planes, rows_a, force, rows_b, (u_star, v_star, temp_mix, salt_mix), tiles_b))

    spec_cube = P(None, "row", "col")
    spec_plane = P("row", "col")
    return jax.shard_map(local_step, mesh=mesh, in_specs=(spec_cube, spec_cube, spec_cube, spec_cube, spec_plane, spec_plane, spec_plane, spec_plane, spec_plane, P(None, None)), out_specs=(spec_plane, spec_plane, spec_plane, spec_cube, spec_cube, spec_cube, spec_cube), check_vma=False)
```

time: 1020 us -> 311 us (0.30)
  other arithmetic: 717 us -> 0 us
  Pallas kernels: 105 us -> 267 us
  local copies, waits for them, and re-layouts: 149 us -> 42.1 us
  starting transfers between devices: 29.6 us -> 0 us
  waiting for transfers between devices: 12.8 us -> 0 us
    dynamic_update_slice x128 -> x0, other arithmetic: 353 us -> none  [column_solve(): _, (gains, parts) = lax.scan(forward, start, (lower, diag, upper, source))]
    mul x13 -> x0, other arithmetic: 227 us -> none  [the longest x1 45 us: baroclinic_predict(): mask_u * (vel_um + TIME_STEP * tend_u)]
    pallas_call x1 -> x5, Pallas kernels: 105 us -> 267 us  [the longest x1 137 us: finish(): pl.pallas_call(functools.partial(finish_kernel, n_sub), out_shape=[f32(NY...]
    another operation x14 -> x0, local copies, waits for them, and re-layouts: 61.9 us -> none
    concatenate x5 -> x0, other arithmetic: 42.8 us -> none  [the longest x2 36.9 us: column_solve(): lower = jnp.concatenate([edge, couple], axis=0)]
    slice x11 -> x0, local copies, waits for them, and re-layouts: 38.8 us -> none  [the longest x5 27.2 us: halo_swap(): from_west = lax.ppermute(field[..., -1:], 'col', west_perm)]
    ppermute x21 -> x0, starting transfers between devices: 29.6 us -> none  [the longest x4 8.26 us: halo_swap(): from_east = lax.ppermute(field[..., :1], 'col', east_perm)]
    squeeze x1 -> x0, other arithmetic: 25.3 us -> none  [baroclinic_predict(): tend_u, tend_v = momentum_tend(edges[0], edges[1], edges[2])]
  transfers between devices with their start and end apart: 21 -> 0, of which waited for: 3 -> 0; matrix products, arithmetic and copies ran while one was open for 12% -> 0% of each run, Pallas kernels for 0% -> 0%
where the time goes in v3:
time: 311 us; the launch traced here: 310 us
  Pallas kernels  267 us (86%)
  local copies, waits for them, and re-layouts  42.1 us (14%)
    pallas_call x1, Pallas kernels, finish(): pl.pallas_call(functools.partial(finish_kernel, n_sub), out_shape=[f32(NY...  137 us
    pallas_call x1, Pallas kernels, predict(): pl.pallas_call(predict_kernel, out_shape=[f32(LEVELS, NY, NX)] * 4 + [f32...  92.4 us
    unnamed x57, local copies, waits for them, and re-layouts  42 us
    pallas_call x2, Pallas kernels, exchange(): pl.pallas_call(functools.partial(exchange_kernel, n_cols, n_packs, n_plan...  28.1 us
    pallas_call x1, Pallas kernels, pack(): pl.pallas_call(pack_kernel, out_shape=[f32(NY, LANES)] * 4 + [f32(NY, NX)...  9.62 us

profile of v3, /device:TPU:0, one launch (start us, length us, event | category | flops | bytes accessed | tf_op | source)
XLA Modules:
  0.0 309.8 jit_solution(4056037487098246806)
XLA Ops:
  0.6 1.4 copy.17.tide_ref
  2.0 3.4 %copy-done = f32[16,256,512]{2,1,0:T(8,128)S(1)} copy-done((f32[16,256,512]{2,1,0:T(8,128)S(1)}, f32[16,256,512]{2,1,0:T(8,128)}, u32[]{:S(2)}) %copy-start) | copy-done | bytes 8388632
  5.4 3.4 %copy-done.2 = f32[16,256,512]{2,1,0:T(8,128)S(1)} copy-done((f32[16,256,512]{2,1,0:T(8,128)S(1)}, f32[16,256,512]{2,1,0:T(8,128)}, u32[]{:S(2)}) %copy-start.2) | copy-done | bytes 8388632
  8.8 3.4 %copy-done.4 = f32[16,256,512]{2,1,0:T(8,128)S(1)} copy-done((f32[16,256,512]{2,1,0:T(8,128)S(1)}, f32[16,256,512]{2,1,0:T(8,128)}, u32[]{:S(2)}) %copy-start.4) | copy-done | bytes 8388632
  12.1 1.0 copy-done.10
  13.2 1.0 copy-done.12
  14.2 1.0 copy-done.13
  15.3 1.0 copy-done.14
  16.3 1.0 copy-done.22
  17.4 9.6 %pack.1 = (f32[256,128]{1,0:T(8,128)S(1)}, f32[256,128]{1,0:T(8,128)S(1)}, f32[256,128]{1,0:T(8,128)S(1)}, f32[256,128]{1,0:T(8,128)S(1)}, f32[256,512]{1,0:T(8,128)S(1)}) custom-call(f32[16,256,512]{2,1,0:T(8,128)S(1)} %copy-done, f32[16,256,512]{2,1,0:T(8,128)S(1)} %copy-done.2, f32[16,256,512]{2,1,0:T(8,128)S(1)} %copy-done.4, f32[16,256,512]{2,1,0:T(8,128)} %s_hbm.3, ...), custom_call_target="tpu_custom_call" | custom-call | tf_op jit(solution)/shard_map/pack/pallas_call | solution.py:141
  27.0 0.0 copy-start.15
  27.0 0.0 copy-done.1
  27.0 0.0 copy-done.11
  27.0 0.0 copy-start.3
  27.0 3.5 %copy-done.3 = f32[16,256,512]{2,1,0:T(8,128)S(1)} copy-done((f32[16,256,512]{2,1,0:T(8,128)S(1)}, f32[16,256,512]{2,1,0:T(8,128)}, u32[]{:S(2)}) %copy-start.3) | copy-done | bytes 8388632
  30.6 3.4 %copy-done.5 = f32[16,256,512]{2,1,0:T(8,128)S(1)} copy-done((f32[16,256,512]{2,1,0:T(8,128)S(1)}, f32[16,256,512]{2,1,0:T(8,128)}, u32[]{:S(2)}) %copy-start.5) | copy-done | bytes 8388632
  34.0 3.4 %copy-done.6 = f32[16,256,512]{2,1,0:T(8,128)S(1)} copy-done((f32[16,256,512]{2,1,0:T(8,128)S(1)}, f32[16,256,512]{2,1,0:T(8,128)}, u32[]{:S(2)}) %copy-start.6) | copy-done | bytes 8388632
  37.3 18.1 %exchange_inputs.1 = (f32[288,128]{1,0:T(8,128)S(1)}, f32[288,128]{1,0:T(8,128)S(1)}, f32[288,128]{1,0:T(8,128)S(1)}, f32[288,128]{1,0:T(8,128)S(1)}, f32[5,32,5...) custom-call(f32[256,128]{1,0:T(8,128)S(1)} %get-tuple-element.30.refs_0_, f32[256,128]{1,0:T(8,128)S(1)} %get-tuple-element.31.refs_1_, ...), custom_call_target="tpu_custom_call" | custom-call | tf_op jit(solution)/shard_map/exchange_inputs/pallas_call | solution.py:198
  55.4 0.0 copy-start.23
  55.4 0.6 copy-done.23
  56.1 0.7 copy-done.24
  56.8 92.4 %predict.1 = (f32[16,256,512]{2,1,0:T(8,128)}, f32[16,256,512]{2,1,0:T(8,128)}, f32[16,256,512]{2,1,0:T(8,128)}, f32[16,256,512]{2,1,0:T(8,128)}, f32[2,256,512]...) custom-call(f32[256,512]{1,0:T(8,128)S(1)} %get-tuple-element.34.refs_4_.kf_ref.kf_h, ...), custom_call_target="tpu_custom_call" | custom-call | tf_op jit(solution)/shard_map/predict/pallas_call | solution.py:458
  149.2 0.1 slice_bitcast_fusion
  149.3 4.0 %copy-done.7 = f32[16,256,512]{2,1,0:T(8,128)S(1)} copy-done((f32[16,256,512]{2,1,0:T(8,128)S(1)}, f32[16,256,512]{2,1,0:T(8,128)}, u32[]{:S(2)}) %copy-start.7) | copy-done | bytes 8388632
  153.4 3.4 %copy-done.8 = f32[16,256,512]{2,1,0:T(8,128)S(1)} copy-done((f32[16,256,512]{2,1,0:T(8,128)S(1)}, f32[16,256,512]{2,1,0:T(8,128)}, u32[]{:S(2)}) %copy-start.8) | copy-done | bytes 8388632
  156.7 3.4 %copy-done.9 = f32[16,256,512]{2,1,0:T(8,128)S(1)} copy-done((f32[16,256,512]{2,1,0:T(8,128)S(1)}, f32[16,256,512]{2,1,0:T(8,128)}, u32[]{:S(2)}) %copy-start.9) | copy-done | bytes 8388632
  160.1 10.0 %exchange_forcing.1 = (f32[288,128]{1,0:T(8,128)S(1)}, f32[288,128]{1,0:T(8,128)S(1)}, f32[2,32,512]{2,1,0:T(8,128)S(1)}, f32[3,16,8,512]{3,2,1,0:T(8,128)S(1)}) custom-call(f32[256,128]{1,0:T(8,128)S(1)} %get-tuple-element.41.refs_0_, f32[256,128]{1,0:T(8,128)S(1)} %get-tuple-element.42.refs_1_, f32[256,512]{1,0:T(8,128)S(1)} %get-tuple-element.54.refs_2_, ...), custom_call_target="tpu_custom_call" | custom-call | tf_op jit(solution)/shard_map/exchange_forcing/pallas_call | solution.py:198
  170.1 0.9 copy-done.19
  171.0 0.6 copy-done.25
  171.7 0.7 copy-done.26
  172.3 0.6 copy-done.27
  173.0 136.8 %finish.1 = (f32[256,512]{1,0:T(8,128)}, f32[256,512]{1,0:T(8,128)}, f32[256,512]{1,0:T(8,128)}, f32[16,256,512]{2,1,0:T(8,128)}, f32[16,256,512]{2,1,0:T(8,128)...) custom-call(f32[30,2]{1,0:T(8,128)} %copy.17.tide_ref, f32[288,128]{1,0:T(8,128)} %copy-done.20, ...), custom_call_target="tpu_custom_call" | custom-call | tf_op jit(solution)/shard_map/finish/pallas_call | solution.py:705
  (31 shorter events, 0.1 us)
Async XLA Ops:
  2.0 3.4 %copy-start = (f32[16,256,512]{2,1,0:T(8,128)S(1)}, f32[16,256,512]{2,1,0:T(8,128)}, u32[]{:S(2)}) copy-start(f32[16,256,512]{2,1,0:T(8,128)} %u_hbm.3) | copy-start | bytes 25165828
  5.4 3.4 %copy-start.2 = (f32[16,256,512]{2,1,0:T(8,128)S(1)}, f32[16,256,512]{2,1,0:T(8,128)}, u32[]{:S(2)}) copy-start(f32[16,256,512]{2,1,0:T(8,128)} %v_hbm.3) | copy-start | bytes 25165828
  8.8 3.4 %copy-start.4 = (f32[16,256,512]{2,1,0:T(8,128)S(1)}, f32[16,256,512]{2,1,0:T(8,128)}, u32[]{:S(2)}) copy-start(f32[16,256,512]{2,1,0:T(8,128)} %t_hbm.3) | copy-start | bytes 25165828
  12.1 1.0 copy-start.10
  13.2 1.0 copy-start.12
  14.2 1.0 copy-start.13
  15.3 1.0 copy-start.14
  16.3 1.0 copy-start.22
  17.4 9.6 %copy-start.1 = (f32[16,256,512]{2,1,0:T(8,128)S(1)}, f32[16,256,512]{2,1,0:T(8,128)}, u32[]{:S(2)}) copy-start(f32[16,256,512]{2,1,0:T(8,128)} %u_hbm.3) | copy-start | bytes 25165828
  17.4 9.7 %copy-start.11 = (f32[256,512]{1,0:T(8,128)S(1)}, f32[256,512]{1,0:T(8,128)}, u32[]{:S(2)}) copy-start(f32[256,512]{1,0:T(8,128)} %h_hbm.1) | copy-start | bytes 1572868
  27.0 29.8 %copy-start.15 = (f32[256,512]{1,0:T(8,128)}, f32[256,512]{1,0:T(8,128)S(1)}, u32[]{:S(2)}) copy-start(f32[256,512]{1,0:T(8,128)S(1)} %get-tuple-element.34.refs_4_.kf_ref.kf_hbm) | copy-start | bytes 1572868
  27.0 3.6 %copy-start.3 = (f32[16,256,512]{2,1,0:T(8,128)S(1)}, f32[16,256,512]{2,1,0:T(8,128)}, u32[]{:S(2)}) copy-start(f32[16,256,512]{2,1,0:T(8,128)} %v_hbm.3) | copy-start | bytes 25165828
  30.6 3.4 %copy-start.5 = (f32[16,256,512]{2,1,0:T(8,128)S(1)}, f32[16,256,512]{2,1,0:T(8,128)}, u32[]{:S(2)}) copy-start(f32[16,256,512]{2,1,0:T(8,128)} %t_hbm.3) | copy-start | bytes 25165828
  34.0 3.4 %copy-start.6 = (f32[16,256,512]{2,1,0:T(8,128)S(1)}, f32[16,256,512]{2,1,0:T(8,128)}, u32[]{:S(2)}) copy-start(f32[16,256,512]{2,1,0:T(8,128)} %s_hbm.3) | copy-start | bytes 25165828
  55.4 0.7 copy-start.23
  56.1 0.7 copy-start.24
  56.7 92.4 %copy-start.17 = (f32[5,32,512]{2,1,0:T(8,128)}, f32[5,32,512]{2,1,0:T(8,128)S(1)}, u32[]{:S(2)}) copy-start(f32[5,32,512]{2,1,0:T(8,128)S(1)} %get-tuple-element.39.rows_ref.rows_a) | copy-start | bytes 983044
  56.7 92.4 %copy-start.20 = (f32[288,128]{1,0:T(8,128)}, f32[288,128]{1,0:T(8,128)S(1)}, u32[]{:S(2)}) copy-start(f32[288,128]{1,0:T(8,128)S(1)} %get-tuple-element.35.east_ref.a1_e) | copy-start | bytes 442372
  56.7 92.4 %copy-start.21 = (f32[288,128]{1,0:T(8,128)}, f32[288,128]{1,0:T(8,128)S(1)}, u32[]{:S(2)}) copy-start(f32[288,128]{1,0:T(8,128)S(1)} %get-tuple-element.36.west_ref.a1_w) | copy-start | bytes 442372
  149.2 20.9 %copy-start.16 = (f32[2,256,512]{2,1,0:T(8,128)}, f32[2,256,512]{2,1,0:T(8,128)S(1)}, u32[]{:S(2)}) copy-start(f32[2,256,512]{2,1,0:T(8,128)S(1)} %get-tuple-element.43.force_hbm) | copy-start | bytes 3145732
  149.2 20.9 %copy-start.18 = (f32[2,256,512]{2,1,0:T(8,128)}, f32[2,256,512]{2,1,0:T(8,128)S(1)}, u32[]{:S(2)}) copy-start(f32[2,256,512]{2,1,0:T(8,128)S(1)} %get-tuple-element.49.usum_ref) | copy-start | bytes 3145732
  149.3 4.1 %copy-start.7 = (f32[16,256,512]{2,1,0:T(8,128)S(1)}, f32[16,256,512]{2,1,0:T(8,128)}, u32[]{:S(2)}) copy-start(f32[16,256,512]{2,1,0:T(8,128)} %get-tuple-element.44.refs_4_.vstar_hbm) | copy-start | bytes 25165828
  153.4 3.4 %copy-start.8 = (f32[16,256,512]{2,1,0:T(8,128)S(1)}, f32[16,256,512]{2,1,0:T(8,128)}, u32[]{:S(2)}) copy-start(f32[16,256,512]{2,1,0:T(8,128)} %get-tuple-element.45.refs_5_.tmix_hbm) | copy-start | bytes 25165828
  156.7 3.4 %copy-start.9 = (f32[16,256,512]{2,1,0:T(8,128)S(1)}, f32[16,256,512]{2,1,0:T(8,128)}, u32[]{:S(2)}) copy-start(f32[16,256,512]{2,1,0:T(8,128)} %get-tuple-element.46.refs_6_.smix_hbm) | copy-start | bytes 25165828
  170.1 0.9 copy-start.19
  171.0 0.6 copy-start.25
  171.7 0.7 copy-start.26
  172.3 0.6 copy-start.27

commit v4 on v3

--- a/solution.py
+++ b/solution.py
@@ -31,7 +31,7 @@
 MIB = 1024 * 1024
 
 VMEM_SPEC = pl.BlockSpec(memory_space=pltpu.VMEM)
-ANY_SPEC = pl.BlockSpec(memory_space=pl.ANY)
+ANY_SPEC = pl.BlockSpec(memory_space=pltpu.HBM)
 
 
 def f32(*shape):
@@ -90,8 +90,16 @@
     return jnp.where(lane < WIDE, turn(east, -q), jnp.where(lane >= LANES - WIDE, turn(west, LANES - WIDE - q), 0.0))
 
 
-def side_level(east, west, q, lane):
-    return jnp.where(lane == 0, turn(east, -q), turn(west, LANES - 1 - q))
+def column(x, q):
+    return jnp.broadcast_to(x[:, q : q + 1], (8, LANES))
+
+
+def pick(x, index):
+    return jnp.take_along_axis(x, index, axis=1, mode="promise_in_bounds")
+
+
+def braid(even, even_at, odd, odd_at, lane):
+    return jnp.where((lane & 1) == 0, pick(even, (lane >> 1) + even_at), pick(odd, (((lane + 1) >> 1) & 63) + odd_at))
 
 
 def pack_kernel(u_hbm, v_hbm, t_hbm, s_hbm, k_ref, h_ref, eta_ref, tu_ref, tv_ref, a1e, a1w, a2e, a2w, kf_ref, buf, sem):
@@ -144,7 +152,7 @@
         in_specs=[ANY_SPEC] * 4 + [VMEM_SPEC] * 5,
         out_specs=[VMEM_SPEC] * 5,
         scratch_shapes=[pltpu.VMEM((2, 4, 2, LEVELS, 64, LANES), jnp.float32), pltpu.SemaphoreType.DMA((2, 4, 2))],
-        compiler_params=pltpu.CompilerParams(vmem_limit_bytes=24 * MIB),
+        compiler_params=pltpu.CompilerParams(vmem_limit_bytes=62 * MIB),
         name="pack",
     )(u, v, temp, salt, k, h, eta, tu, tv)
 
@@ -201,15 +209,16 @@
         in_specs=[ANY_SPEC] * (2 * n_packs + n_planes + n_cubes),
         out_specs=[ANY_SPEC] * len(outs),
         scratch_shapes=[pltpu.SemaphoreType.DMA((n_moves,)), pltpu.SemaphoreType.DMA((n_moves,))],
-        compiler_params=pltpu.CompilerParams(collective_id=collective_id, has_side_effects=True, vmem_limit_bytes=4 * MIB),
+        compiler_params=pltpu.CompilerParams(collective_id=collective_id, has_side_effects=True, vmem_limit_bytes=62 * MIB),
         name=name,
     )(*packs_e, *packs_w, *planes, *cubes)
 
 
-def predict_kernel(kf_ref, hf_ref, rows_ref, east_ref, west_ref, u_hbm, v_hbm, t_hbm, s_hbm, hy_hbm, ustar_hbm, vstar_hbm, tmix_hbm, smix_hbm, force_ref, usum_ref, be_ref, bw_ref, ring, kh, geo, carry, stage, part, in_sem, out_sem):
+def predict_kernel(kf_ref, hf_ref, rows_ref, east_ref, west_ref, own_e_ref, own_w_ref, u_hbm, v_hbm, t_hbm, s_hbm, hy_hbm, ustar_hbm, vstar_hbm, tmix_hbm, smix_hbm, force_ref, usum_ref, be_ref, bw_ref, ring, kh, geo, carry, stage, part, in_sem, out_sem):
     row = lax.axis_index("row")
     lane, sub = iotas()
     cubes = (u_hbm, v_hbm, t_hbm, s_hbm)
+    level = (lane & (LEVELS - 1)).astype(jnp.float32)
     outs = (ustar_hbm, vstar_hbm, tmix_hbm, smix_hbm)
 
     def tile_copies(t, slot):
@@ -286,15 +295,39 @@
         g_next = lax.rem(t + 1 + SUB, SUB)
 
         def plane(q, tt, n):
-            return [geo[q, tt, :, pl.ds(c * LANES, LANES)] for c in range(n)]
-
-        k1 = plane(0, g_next, 5)
-        ku1 = plane(1, g_next, 5)
-        kv1 = plane(2, g_next, 5)
-        dz1 = [(TIME_STEP * GRAVITY) * x for x in plane(3, g_next, 5)]
-        csum = [jnp.zeros((8, LANES), jnp.float32)] * 5
-        side_e = east_ref[tile_rows(g_next), :]
-        side_w = west_ref[tile_rows(g_next), :]
+            return [geo[q, tt, :, chunk(c)] for c in range(n)]
+
+        def count(q, tt, c, x):
+            return column(geo[q, tt, :, chunk(c)], x)
+
+        k1 = plane(0, g_next, 4)
+        ku1 = plane(1, g_next, 4)
+        kv1 = plane(2, g_next, 4)
+        dz1 = [(TIME_STEP * GRAVITY) * x for x in plane(3, g_next, 4)]
+        csum = [jnp.zeros((8, LANES), jnp.float32)] * 4
+
+        east = east_ref[tile_rows(g_next), :]
+        west = west_ref[tile_rows(g_next), :]
+        east_u = jnp.where(count(1, g_next, 4, 0) > level, east, 0.0)
+        east_v = jnp.where(count(2, g_next, 4, 0) > level, east, 0.0)
+        west_u = jnp.where(count(1, g_next, 4, LANES - 1) > level, west, 0.0)
+        outer = braid(east_v, 16, west_u, 0, lane)
+        if not first:
+            own_u = jnp.where(count(1, g_next, 3, LANES - 1) > level, own_e_ref[tile_rows(jnp.minimum(t + 1, TILES - 1)), :], 0.0)
+            half = jnp.where(count(0, g_next, 4, 0) > level, (0.5 * BETA_S) * turn(east, -16) - (0.5 * ALPHA_T) * east + 0.5 * CONST_R, 0.0)
+            run = half
+            for reach in (1, 2, 4, 8):
+                run = run + jnp.where(level >= reach, turn(run, reach), 0.0)
+            pair = turn(own_u + east_u, 32)
+            east_e = pair * pair + ((run + run) - half) * ((TIME_STEP * GRAVITY) * count(3, g_next, 4, 0))
+            west_q = jnp.zeros((8, LANES), jnp.float32)
+            if work:
+                low = west_ref[tile_rows(t), :]
+                low_u = jnp.where(count(1, t, 4, LANES - 1) > level, low, 0.0)
+                low_v = jnp.where(count(2, t, 4, LANES - 1) > level, low, 0.0) + jnp.where(count(2, t, 0, 0) > level, own_w_ref[tile_rows(t), :], 0.0)
+                west_q = (low_u + shift_north([low_u], [west_u], sub)[0]) * turn(low_v, -16)
+            inner = braid(east_e, 32, west_q, 0, lane)
+
         if work:
             kc0 = plane(0, t, 4)
             ku0 = plane(1, t, 4)
@@ -310,45 +343,46 @@
 
         for k in range(LEVELS):
 
-            def tile(slot, a, n):
-                got = [ring[slot, a, k, :, pl.ds(c * LANES, LANES)] for c in range(4)]
-                return got + [side_level(side_e, side_w, a * LEVELS + k, lane)] if n == 5 else got
-
-            raw_u, raw_v, raw_t, raw_s = (tile(slot_next, a, 5) for a in range(4))
+            def tile(slot, a):
+                return [ring[slot, a, k, :, chunk(c)] for c in range(4)]
+
+            def old(q):
+                return [carry[q, k, :, chunk(c)] for c in range(4)]
+
+            raw_u, raw_v, raw_t, raw_s = (tile(slot_next, a) for a in range(4))
+            outer_k = turn(outer, -2 * k)
             um1 = [jnp.where(m > k, x, 0.0) for m, x in zip(ku1, raw_u)]
             vm1 = [jnp.where(m > k, x, 0.0) for m, x in zip(kv1, raw_v)]
-            half = [jnp.where(m > k, (0.5 * BETA_S) * s - (0.5 * ALPHA_T) * x + 0.5 * CONST_R, 0.0) for m, x, s in zip(k1, raw_t, raw_s)]
-            mid = [a + b for a, b in zip(csum, half)]
-            csum = [a + b for a, b in zip(mid, half)]
-            p1 = [a * b for a, b in zip(mid, dz1)]
-            u_w = shift_west(um1, um1[4], lane)
-            e1 = [(a + b) * (a + b) + p for a, b, p in zip(u_w, um1, p1)]
-            e_e = shift_east(e1[:4], e1[4], lane)
-            ed1 = [a - b for a, b in zip(e_e, e1)]
-            v_e = shift_east(vm1, vm1[0], lane)
+            v_e = shift_east(vm1, outer_k, lane)
             ve1 = [a + b for a, b in zip(vm1, v_e)]
-            old = lambda q, n: [carry[q, k, :, pl.ds(c * LANES, LANES)] for c in range(n)]
             if first:
-                b1 = [jnp.zeros((8, LANES), jnp.float32)] * 4
+                ed1 = b1 = [jnp.zeros((8, LANES), jnp.float32)] * 4
             else:
-                vm0 = old(1, 4)
-                um0 = old(0, 5)
-                ve0 = old(2, 5)
-                v_s = shift_south(vm1[:4], vm0, sub)
+                inner_k = turn(inner, -2 * k)
+                half_k = [jnp.where(m > k, (0.5 * BETA_S) * s - (0.5 * ALPHA_T) * x + 0.5 * CONST_R, 0.0) for m, x, s in zip(k1, raw_t, raw_s)]
+                mid = [a + b for a, b in zip(csum, half_k)]
+                csum = [a + b for a, b in zip(mid, half_k)]
+                p1 = [a * b for a, b in zip(mid, dz1)]
+                u_w = shift_west(um1, outer_k, lane)
+                e1 = [(a + b) * (a + b) + p for a, b, p in zip(u_w, um1, p1)]
+                ed1 = [a - b for a, b in zip(shift_east(e1, inner_k, lane), e1)]
+                vm0 = old(1)
+                um0 = old(0)
+                v_s = shift_south(vm1, vm0, sub)
                 b1 = [(a + b) * (a + b) + p for a, b, p in zip(v_s, vm1, p1)]
                 u_n = shift_north(um0, um1, sub)
-                q0 = [(a + b) * x for a, b, x in zip(um0, u_n, ve0)]
+                q0 = [(a + b) * x for a, b, x in zip(um0, u_n, old(2))]
             if work:
-                ed0 = old(3, 4)
-                b0 = old(4, 4)
-                q_s = shift_south(q0[:4], old(5, 4), sub)
-                q_w = shift_west(q0[:4], q0[4], lane)
+                ed0 = old(3)
+                b0 = old(4)
+                q_s = shift_south(q0, old(5), sub)
+                q_w = shift_west(q0, inner_k, lane)
                 b_n = shift_north(b0, b1, sub)
                 src = {
                     "u": [jnp.where(m > k, u - (e + (q - s)), 0.0) for m, u, e, q, s in zip(ku0, um0, ed0, q0, q_s)],
                     "v": [jnp.where(m > k, v - ((bn - b) + (q - w)), 0.0) for m, v, bn, b, q, w in zip(kv0, vm0, b_n, b0, q0, q_w)],
-                    "T": [jnp.where(m > k, x, 0.0) for m, x in zip(kc0, tile(slot_now, 2, 4))],
-                    "S": [jnp.where(m > k, x, 0.0) for m, x in zip(kc0, tile(slot_now, 3, 4))],
+                    "T": [jnp.where(m > k, x, 0.0) for m, x in zip(kc0, tile(slot_now, 2))],
+                    "S": [jnp.where(m > k, x, 0.0) for m, x in zip(kc0, tile(slot_now, 3))],
                 }
                 total_m = {"u": [a + b for a, b in zip(total_m["u"], um0)], "v": [a + b for a, b in zip(total_m["v"], vm0)]}
                 for name, coef, mask, fields in (("u", cu, ku0, "u"), ("v", cv, kv0, "v"), ("c", cc, kc0, "TS")):
@@ -364,28 +398,25 @@
                         part[4 + "uvc".index(name), k, :, pl.ds(c * LANES, LANES)] = gain[c]
                     chain["q"] = [1.0 + g * q for g, q in zip(gain, chain["q"])]
                     chain["cl"] = down
-            new = [(0, um1, 5), (1, vm1, 4), (2, ve1, 5), (3, ed1, 4), (4, b1, 4)]
-            if not first:
-                new.append((5, q0, 4))
-            for q, vals, n in new:
-                for c in range(n):
-                    carry[q, k, :, pl.ds(c * LANES, LANES)] = vals[c]
+            new = [um1, vm1, ve1, ed1, b1] if first else [um1, vm1, ve1, ed1, b1, q0]
+            for q, vals in enumerate(new):
+                for c in range(4):
+                    carry[q, k, :, chunk(c)] = vals[c]
 
         if not work:
             return
         out_slot = lax.rem(t, 2)
         below = dict(prev)
-        pack_e = jnp.zeros((8, LANES), jnp.float32)
-        pack_w = jnp.zeros((8, LANES), jnp.float32)
+        braided = jnp.zeros((8, LANES), jnp.float32)
+        pair_id = ((lane + 1) >> 1) & 63
 
         def put(k, f, vals):
-            nonlocal pack_e, pack_w
+            nonlocal braided
             if f == "v":
                 return
-            q = 2 * WIDE + "TSu".index(f) * LEVELS + k
-            pack_e = jnp.where(lane == q, turn(vals[3], q + 1), pack_e)
-            if f != "u":
-                pack_w = jnp.where(lane == q, turn(vals[0], q), pack_w)
+            q = "TSu".index(f) * LEVELS + k
+            both = jnp.where(lane == LANES - 1, vals[3], vals[0]) if f != "u" else vals[3]
+            braided = jnp.where(pair_id == q, turn(both, 2 * q), braided)
 
         total = {"u": below["u"], "v": below["v"]}
         for f in "uvTS":
@@ -409,6 +440,8 @@
         rows = pl.ds(pl.multiple_of(t * 8, 8), 8)
         dzu = plane(4, t, 4)
         dzv = plane(5, t, 4)
+        pack_e = pick(braided, (2 * lane + (LANES - 1)) & (LANES - 1))
+        pack_w = pick(braided, (2 * lane) & (LANES - 1))
         for q, (f, dz) in enumerate((("u", dzu), ("v", dzv))):
             force = [(1.0 / TIME_STEP) * (dz[c] * (total[f][c] - total_m[f][c])) for c in range(4)]
             for c in range(4):
@@ -454,25 +487,25 @@
     wait(out_copies(TILES - 1, 1))
 
 
-def predict(kf, hf, rows, east, west, u, v, temp, salt, hy):
+def predict(kf, hf, rows, east, west, own_e, own_w, u, v, temp, salt, hy):
     return pl.pallas_call(
         predict_kernel,
         out_shape=[f32(LEVELS, NY, NX)] * 4 + [f32(2, NY, NX)] * 2 + [f32(NY, LANES)] * 2,
-        in_specs=[VMEM_SPEC] * 5 + [ANY_SPEC] * 5,
+        in_specs=[VMEM_SPEC] * 7 + [ANY_SPEC] * 5,
         out_specs=[ANY_SPEC] * 4 + [VMEM_SPEC] * 4,
         scratch_shapes=[
             pltpu.VMEM((RING, 4, LEVELS, 8, NX), jnp.float32),
             pltpu.VMEM((2, EXT_Y, EXT_X), jnp.float32),
             pltpu.VMEM((9, SUB, 8, EXT_X), jnp.float32),
-            pltpu.VMEM((6, LEVELS, 8, EXT_X), jnp.float32),
+            pltpu.VMEM((6, LEVELS, 8, NX), jnp.float32),
             pltpu.VMEM((2, 4, LEVELS, 8, NX), jnp.float32),
             pltpu.VMEM((7, LEVELS, 8, NX), jnp.float32),
             pltpu.SemaphoreType.DMA((RING, 4)),
             pltpu.SemaphoreType.DMA((2, 4)),
         ],
-        compiler_params=pltpu.CompilerParams(vmem_limit_bytes=48 * MIB),
+        compiler_params=pltpu.CompilerParams(vmem_limit_bytes=62 * MIB),
         name="predict",
-    )(kf, hf, rows, east, west, u, v, temp, salt, hy)
+    )(kf, hf, rows, east, west, own_e, own_w, u, v, temp, salt, hy)
 
 
 def east_of(x):
@@ -491,7 +524,7 @@
     return pltpu.roll(x, 1, 0)
 
 
-def finish_kernel(n_sub, tide_ref, a1_e, a1_w, a2_e, a2_w, b_e, b_w, usum_ref, kf_hbm, h_hbm, eta_in, tu_in, tv_in, rows_a, force_hbm, rows_b, ustar_hbm, vstar_hbm, tmix_hbm, smix_hbm, tiles_b, eta_hbm, u_hbm, v_hbm, uc_hbm, vc_hbm, tn_hbm, sn_hbm, nat, eta, u, v, au, fu, av, fv, ub, vb, cube, fy_old, stage, nat_sem, cube_sem, tile_sem, plane_sem, out_sem):
+def finish_kernel(n_sub, tide_ref, a1_e, a1_w, a2_e, a2_w, b_e, b_w, own_ref, usum_ref, kf_hbm, h_hbm, eta_in, tu_in, tv_in, rows_a, force_hbm, rows_b, ustar_hbm, vstar_hbm, tmix_hbm, smix_hbm, tiles_b, eta_hbm, u_hbm, v_hbm, uc_hbm, vc_hbm, tn_hbm, sn_hbm, nat, eta, u, v, au, fu, av, fv, ub, vb, cube, fy_old, stage, nat_sem, cube_sem, tile_sem, plane_sem, out_sem):
     dt_sub = TIME_STEP / n_sub
     weight_norm = 6.0 / (n_sub * (n_sub + 1) * (n_sub + 2))
     row = lax.axis_index("row")
@@ -647,6 +680,7 @@
             for c in range(4):
                 fy_old[f, k, :, chunk(c)] = vc[c] * (x[c] + x_n[c])
 
+    level = (lane & (LEVELS - 1)).astype(jnp.float32)
     outs = (uc_hbm, vc_hbm, tn_hbm, sn_hbm)
 
     def out_copies(t, slot):
@@ -667,26 +701,31 @@
                 wait(cube_copies(i))
 
         kc, ku, kv, dz_u, dz_v = faces(t, t + 1)
-        east = b_e[tile_rows(t), :]
-        west = b_w[tile_rows(t), :]
         rows = tile_rows(t)
-        side_u = [turn(west, LANES - 1 - (2 * WIDE + 2 * LEVELS + k)) for k in range(LEVELS)]
-        side_sum = functools.reduce(lambda a, b: a + b, side_u)
-        du = [correction(nat[5, c, rows, :], usum_ref[0, rows, chunk(c)] if c < 4 else dz_u[4] * side_sum, ku[c], dz_u[c]) for c in range(CHUNKS)]
+        east = b_e[rows, :]
+        west = b_w[rows, :]
+        in_u = (lane >= 96) & (lane < 112)
+        side_sum = jnp.broadcast_to(jnp.sum(jnp.where(in_u, west, 0.0), axis=1, keepdims=True), (8, LANES))
+        side_d = column(correction(nat[5, 4, rows, :], dz_u[4] * side_sum, ku[4], dz_u[4]), LANES - 1)
+        side_u = jnp.where(column(ku[4], LANES - 1) > level, west + side_d, 0.0)
+        side_u = jnp.where(lane < 80, turn(side_u, -32), turn(side_u, -16))
+        outer = braid(east, 64, side_u * (west + own_ref[rows, :]), 64, lane)
+        du = [correction(nat[5, c, rows, :], usum_ref[0, rows, chunk(c)], ku[c], dz_u[c]) for c in range(4)]
         dv = [correction(nat[6, c, rows, :], usum_ref[1, rows, chunk(c)], kv[c], dz_v[c]) for c in range(4)]
         for k in range(LEVELS):
-            uc = [jnp.where(m > k, x + d, 0.0) for m, x, d in zip(ku, cube_tile(0, t, k) + [side_u[k]], du)]
+            uc = [jnp.where(m > k, x + d, 0.0) for m, x, d in zip(ku, cube_tile(0, t, k), du)]
             vc = [jnp.where(m > k, x + d, 0.0) for m, x, d in zip(kv, cube_tile(1, t, k), dv)]
             for c in range(4):
                 stage[slot, 0, k, :, chunk(c)] = uc[c]
                 stage[slot, 1, k, :, chunk(c)] = vc[c]
             for f in range(2):
-                x = cube_tile(2 + f, t, k) + [side_level(east, west, 2 * WIDE + f * LEVELS + k, lane)]
-                x_e = shift_east(x, x[0], lane)
-                x_n = shift_north(x[:4], cube_tile(2 + f, t + 1, k), sub)
+                x = cube_tile(2 + f, t, k)
+                edge = turn(outer, -2 * (f * LEVELS + k))
+                x_e = shift_east(x, edge, lane)
+                x_n = shift_north(x, cube_tile(2 + f, t + 1, k), sub)
                 fx = [a * (b + e) for a, b, e in zip(uc, x, x_e)]
                 fy = [a * (b + n) for a, b, n in zip(vc, x, x_n)]
-                fx_w = shift_west(fx[:4], fx[4], lane)
+                fx_w = shift_west(fx, edge, lane)
                 fy_s = shift_south(fy, [fy_old[f, k, :, chunk(c)] for c in range(4)], sub)
                 for c in range(4):
                     fy_old[f, k, :, chunk(c)] = fy[c]
@@ -699,13 +738,13 @@
     wait(plane_outs)
 
 
-def finish(tide_force, packs, usum, planes, rows_a, force, rows_b, cubes, tiles_b):
+def finish(tide_force, packs, own, usum, planes, rows_a, force, rows_b, cubes, tiles_b):
     n_sub = tide_force.shape[0]
     big = pltpu.VMEM((SUB, 8, EXT_X), jnp.float32)
     return pl.pallas_call(
         functools.partial(finish_kernel, n_sub),
         out_shape=[f32(NY, NX)] * 3 + [f32(LEVELS, NY, NX)] * 4,
-        in_specs=[pl.BlockSpec(memory_space=pltpu.SMEM)] + [VMEM_SPEC] * 7 + [ANY_SPEC] * 13,
+        in_specs=[pl.BlockSpec(memory_space=pltpu.SMEM)] + [VMEM_SPEC] * 8 + [ANY_SPEC] * 13,
         out_specs=[ANY_SPEC] * 7,
         scratch_shapes=[pltpu.VMEM((7, CHUNKS, EXT_Y, LANES), jnp.float32)]
         + [big] * 9
@@ -719,9 +758,9 @@
             pltpu.SemaphoreType.DMA((3, 4)),
             pltpu.SemaphoreType.DMA((2, 4)),
         ],
-        compiler_params=pltpu.CompilerParams(vmem_limit_bytes=60 * MIB),
+        compiler_params=pltpu.CompilerParams(vmem_limit_bytes=62 * MIB),
         name="finish",
-    )(tide_force, *packs, usum, *planes, rows_a, force, rows_b, *cubes, tiles_b)
+    )(tide_force, *packs, own, usum, *planes, rows_a, force, rows_b, *cubes, tiles_b)
 
 
 def solution(mesh):
@@ -731,9 +770,9 @@
         a1e, a1w, a2e, a2w, kf = pack(vel_u, vel_v, value_a11, salinity, kmt_levels, bathymetry, sea_level, trans_u, trans_v)
         planes = (kf, bathymetry, sea_level, trans_u, trans_v)
         e1, e2, w1, w2, rows_a, tiles_a = exchange(n_cols, "exchange_inputs", 0, (a1e, a2e), (a1w, a2w), planes, (vel_u, vel_v, value_a11, salinity))
-        u_star, v_star, temp_mix, salt_mix, force, usum, be, bw = predict(kf, bathymetry, rows_a, e1, w1, vel_u, vel_v, value_a11, salinity, tiles_a)
+        u_star, v_star, temp_mix, salt_mix, force, usum, be, bw = predict(kf, bathymetry, rows_a, e1, w1, a1e, a1w, vel_u, vel_v, value_a11, salinity, tiles_a)
         e3, w3, rows_b, tiles_b = exchange(n_cols, "exchange_forcing", 1, (be,), (bw,), (force[0], force[1]), (v_star, temp_mix, salt_mix))
-        return tuple(finish(tide_force, (e1, w1, e2, w2, e3, w3), usum, planes, rows_a, force, rows_b, (u_star, v_star, temp_mix, salt_mix), tiles_b))
+        return tuple(finish(tide_force, (e1, w1, e2, w2, e3, w3), bw, usum, planes, rows_a, force, rows_b, (u_star, v_star, temp_mix, salt_mix), tiles_b))
 
     spec_cube = P(None, "row", "col")
     spec_plane = P("row", "col")

time: 311 us -> 220 us (0.71)
  Pallas kernels: 267 us -> 216 us
  local copies, waits for them, and re-layouts: 42.1 us -> 3.6 us
    unnamed x57 -> x1, local copies, waits for them, and re-layouts: 42 us -> 1.36 us
    pallas_call x1, Pallas kernels: 137 us -> 101 us  [finish(): pl.pallas_call(functools.partial(finish_kernel, n_sub), out_shape=[f32(NY...]
    pallas_call x1, Pallas kernels: 92.4 us -> 74.8 us  [predict(): pl.pallas_call(predict_kernel, out_shape=[f32(LEVELS, NY, NX)] * 4 + [f32...]
where the time goes in v4:
time: 220 us
  Pallas kernels  216 us (98%)
  local copies, waits for them, and re-layouts  3.6 us (2%)
    pallas_call x1, Pallas kernels, finish(): pl.pallas_call(functools.partial(finish_kernel, n_sub), out_shape=[f32(NY...  101 us
    pallas_call x1, Pallas kernels, predict(): pl.pallas_call(predict_kernel, out_shape=[f32(LEVELS, NY, NX)] * 4 + [f32...  74.8 us
    pallas_call x2, Pallas kernels, exchange(): pl.pallas_call(functools.partial(exchange_kernel, n_cols, n_packs, n_plan...  28.1 us
    pallas_call x1, Pallas kernels, pack(): pl.pallas_call(pack_kernel, out_shape=[f32(NY, LANES)] * 4 + [f32(NY, NX)...  12.5 us

profile of v4, /device:TPU:0, one launch (start us, length us, event | category | flops | bytes accessed | tf_op | source)
XLA Modules:
  0.0 220.2 jit_solution(15172901017525575136)
XLA Ops:
  0.6 1.4 copy.17.tide_ref
  2.0 12.5 %pack.1 = (f32[256,128]{1,0:T(8,128)}, f32[256,128]{1,0:T(8,128)}, f32[256,128]{1,0:T(8,128)}, f32[256,128]{1,0:T(8,128)}, f32[256,512]{1,0:T(8,128)}) custom-call(f32[16,256,512]{2,1,0:T(8,128)} %u_hbm.3, f32[16,256,512]{2,1,0:T(8,128)} %v_hbm.3, f32[16,256,512]{2,1,0:T(8,128)} %t_hbm.3, f32[16,256,512]{2,1,0:T(8,128)} %s_hbm.3, s32[256,512]{1,0:T(8,128)} %k_ref.1, ...), custom_call_target="tpu_custom_call" | custom-call | tf_op jit(solution)/shard_map/pack/pallas_call | solution.py:149
  14.5 18.1 %exchange_inputs.1 = (f32[288,128]{1,0:T(8,128)}, f32[288,128]{1,0:T(8,128)}, f32[288,128]{1,0:T(8,128)}, f32[288,128]{1,0:T(8,128)}, f32[5,32,512]{2,1,0:T(8,128)}, /*index=5*/f32[4,16,8,512]{3,2,1,0:T(8,128)}) custom-call(f32[256,128]{1,0:T(8,128)} %get-tuple-element.30.refs_0_.own_e_ref, f32[256,128]{1,0:T(8,128)} %get-tuple-element.31.refs_1_, ...), custom_call_target="tpu_custom_call" | custom-call | tf_op jit(solution)/shard_map/exchange_inputs/pallas_call | solution.py:206
  32.6 74.8 %predict.1 = (f32[16,256,512]{2,1,0:T(8,128)}, f32[16,256,512]{2,1,0:T(8,128)}, f32[16,256,512]{2,1,0:T(8,128)}, f32[16,256,512]{2,1,0:T(8,128)}, f32[2,256,512]...) custom-call(f32[256,512]{1,0:T(8,128)} %get-tuple-element.34.refs_4_.kf_ref.kf_hbm, ...), custom_call_target="tpu_custom_call" | custom-call | tf_op jit(solution)/shard_map/predict/pallas_call | solution.py:491
  107.5 2.2 %slice_bitcast_fusion = (f32[256,512]{1,0:T(8,128)}, f32[256,512]{1,0:T(8,128)}) fusion(f32[2,256,512]{2,1,0:T(8,128)} %get-tuple-element.43.force_hbm), kind=kLoop, calls=%fused_computation | loop fusion | bytes 2097152 | tf_op jit(solution)/shard_map/squeeze | solution.py:774
  109.7 10.0 %exchange_forcing.1 = (f32[288,128]{1,0:T(8,128)}, f32[288,128]{1,0:T(8,128)}, f32[2,32,512]{2,1,0:T(8,128)}, f32[3,16,8,512]{3,2,1,0:T(8,128)}) custom-call(f32[256,128]{1,0:T(8,128)} %get-tuple-element.41.refs_0_, f32[256,128]{1,0:T(8,128)} %get-tuple-element.42.refs_1_.own_ref, f32[256,512]{1,0:T(8,128)} %get-tuple-element.54.refs_2_, ...), custom_call_target="tpu_custom_call" | custom-call | tf_op jit(solution)/shard_map/exchange_forcing/pallas_call | solution.py:206
  119.7 100.5 %finish.1 = (f32[256,512]{1,0:T(8,128)}, f32[256,512]{1,0:T(8,128)}, f32[256,512]{1,0:T(8,128)}, f32[16,256,512]{2,1,0:T(8,128)}, f32[16,256,512]{2,1,0:T(8,128)...) custom-call(f32[30,2]{1,0:T(8,128)} %copy.17.tide_ref, f32[288,128]{1,0:T(8,128)} %get-tuple-element.35.east_ref.a1_e, ...), custom_call_target="tpu_custom_call" | custom-call | tf_op jit(solution)/shard_map/finish/pallas_call | solution.py:744

commit v5 on v4

v5 whole, which is shorter than its diff:
```python
import functools

import jax
import jax.numpy as jnp
from jax import lax
from jax.experimental import pallas as pl
from jax.experimental.pallas import tpu as pltpu
from jax.sharding import PartitionSpec as P

GRAVITY = 1.0
TIME_STEP = 4.0
ALPHA_T = 0.02
BETA_S = 0.015
T_REF = 1.0
S_REF = 1.0
VISC_KV = 0.001
DIFF_KT = 0.0005

LEVELS = 16
NY = 256
NX = 512
WIDE = 32
SUB = 36
EXT_Y = 8 * SUB
EXT_X = 640
LANES = 128
CHUNKS = EXT_X // LANES
TILES = NY // 8
RING = 4
CONST_R = -BETA_S * S_REF + ALPHA_T * T_REF
MIB = 1024 * 1024

VMEM_SPEC = pl.BlockSpec(memory_space=pltpu.VMEM)
ANY_SPEC = pl.BlockSpec(memory_space=pltpu.HBM)


def f32(*shape):
    return jax.ShapeDtypeStruct(shape, jnp.float32)


def tile_rows(t):
    return pl.ds(pl.multiple_of(t * 8, 8), 8)


def chunk(c):
    return pl.ds(c * LANES, LANES)


def lanes(x, c):
    return x[:, c * LANES : (c + 1) * LANES]


def turn(x, shift):
    return x if shift % LANES == 0 else pltpu.roll(x, shift % LANES, 1)


def iotas():
    return lax.broadcasted_iota(jnp.int32, (8, LANES), 1), lax.broadcasted_iota(jnp.int32, (8, LANES), 0)


def start(copies):
    for copy in copies:
        copy.start()


def wait(copies):
    for copy in copies:
        copy.wait()


def shift_east(xs, after, lane):
    nxt = list(xs[1:]) + [after]
    return [pltpu.roll(jnp.where(lane == 0, n, x), LANES - 1, 1) for x, n in zip(xs, nxt)]


def shift_west(xs, before, lane):
    prv = [before] + list(xs[:-1])
    return [pltpu.roll(jnp.where(lane == LANES - 1, p, x), 1, 1) for x, p in zip(xs, prv)]


def shift_north(xs, above, sub):
    return [pltpu.roll(jnp.where(sub == 0, a, x), 7, 0) for x, a in zip(xs, above)]


def shift_south(xs, below, sub):
    return [pltpu.roll(jnp.where(sub == 7, b, x), 1, 0) for x, b in zip(xs, below)]


def side_planes(east, west, q, lane):
    return jnp.where(lane < WIDE, turn(east, -q), jnp.where(lane >= LANES - WIDE, turn(west, LANES - WIDE - q), 0.0))


def column(x, q):
    return jnp.broadcast_to(x[:, q : q + 1], (8, LANES))


def pick(x, index):
    return jnp.take_along_axis(x, index, axis=1, mode="promise_in_bounds")


def braid(even, even_at, odd, odd_at, lane):
    return jnp.where((lane & 1) == 0, pick(even, (lane >> 1) + even_at), pick(odd, (((lane + 1) >> 1) & 63) + odd_at))


def pack_kernel(u_hbm, v_hbm, t_hbm, s_hbm, k_ref, h_ref, eta_ref, tu_ref, tv_ref, a1e, a1w, a2e, a2w, kf_ref, buf, sem):
    lane, _ = iotas()
    pair_id = ((lane + 1) >> 1) & 63
    cubes = (u_hbm, v_hbm, t_hbm, s_hbm)
    strip = 64

    def copies(i):
        return [pltpu.make_async_copy(cubes[a].at[:, pl.ds(i * strip, strip), chunk(3 * e)], buf.at[i, a, e], sem.at[i, a, e]) for a in range(4) for e in range(2)]

    for i in range(NY // strip):
        start(copies(i))
    for i in range(NY // strip):
        wait(copies(i))

        @pl.loop(0, strip // 8)
        def _(t):
            here = tile_rows(t)
            rows = pl.ds(pl.multiple_of(i * strip + t * 8, 8), 8)
            braided = jnp.zeros((8, LANES), jnp.float32)
            for a in range(4):
                for k in range(LEVELS):
                    q = a * LEVELS + k
                    both = jnp.where(lane == LANES - 1, buf[i, a, 1, k, here, :], buf[i, a, 0, k, here, :])
                    braided = jnp.where(pair_id == q, turn(both, 2 * q), braided)
            west = pick(braided, (2 * lane) & (LANES - 1))
            east = pick(braided, (2 * lane + (LANES - 1)) & (LANES - 1))
            kf = k_ref[rows, :].astype(jnp.float32)
            kf_ref[rows, :] = kf
            west2 = jnp.zeros((8, LANES), jnp.float32)
            east2 = jnp.zeros((8, LANES), jnp.float32)
            for q, plane in ((64, kf), (96, h_ref[rows, :])):
                inside = (lane >= q) & (lane < q + WIDE)
                west = jnp.where(inside, turn(lanes(plane, 0), q), west)
                east = jnp.where(inside, turn(lanes(plane, 3), q - LANES + WIDE), east)
            for q, plane in ((0, eta_ref[rows, :]), (32, tu_ref[rows, :]), (64, tv_ref[rows, :])):
                inside = (lane >= q) & (lane < q + WIDE)
                west2 = jnp.where(inside, turn(lanes(plane, 0), q), west2)
                east2 = jnp.where(inside, turn(lanes(plane, 3), q - LANES + WIDE), east2)
            a1e[rows, :] = east
            a1w[rows, :] = west
            a2e[rows, :] = east2
            a2w[rows, :] = west2


def pack(u, v, temp, salt, k, h, eta, tu, tv):
    return pl.pallas_call(
        pack_kernel,
        out_shape=[f32(NY, LANES)] * 4 + [f32(NY, NX)],
        in_specs=[ANY_SPEC] * 4 + [VMEM_SPEC] * 5,
        out_specs=[VMEM_SPEC] * 5,
        scratch_shapes=[pltpu.VMEM((4, 4, 2, LEVELS, 64, LANES), jnp.float32), pltpu.SemaphoreType.DMA((4, 4, 2))],
        compiler_params=pltpu.CompilerParams(vmem_limit_bytes=62 * MIB),
        name="pack",
    )(u, v, temp, salt, k, h, eta, tu, tv)


def meet(n_cols):
    col = lax.axis_index("col")
    row = lax.axis_index("row")
    east = lax.rem(col + 1, n_cols)
    west = lax.rem(col + n_cols - 1, n_cols)
    peers = [(east, row), (west, row), (col, 1 - row), (east, 1 - row), (west, 1 - row)]
    barrier = pltpu.get_barrier_semaphore()
    for peer in peers:
        pl.semaphore_signal(barrier, inc=1, device_id=peer, device_id_type=pl.DeviceIdType.MESH)
    pl.semaphore_wait(barrier, len(peers))
    return peers, row


def pack_moves(peers, row, pack_e, pack_w, from_e, from_w):
    edge = pl.multiple_of((1 - row) * (NY - WIDE), 8)
    part = pl.ds(edge, WIDE)
    tail = pl.ds(NY, WIDE)
    return [
        (pack_e, from_w.at[pl.ds(0, NY), :], peers[0]),
        (pack_w, from_e.at[pl.ds(0, NY), :], peers[1]),
        (pack_e.at[part, :], from_w.at[tail, :], peers[3]),
        (pack_w.at[part, :], from_e.at[tail, :], peers[4]),
    ]


def row_moves(peers, row, planes, dsts):
    edge = pl.multiple_of((1 - row) * (NY - WIDE), 8)
    return [(src.at[pl.ds(edge, WIDE), :], dst, peers[2]) for src, dst in zip(planes, dsts)]


def tile_moves(peers, row, cubes, dst):
    tile = pl.multiple_of((1 - row) * (NY - 8), 8)
    return [(src.at[:, pl.ds(tile, 8), :], dst.at[i], peers[2]) for i, src in enumerate(cubes)]


def remote(moves, send_sem, recv_sem, first=0):
    return [
        pltpu.make_async_remote_copy(src_ref=src, dst_ref=dst, send_sem=send_sem.at[first + i], recv_sem=recv_sem.at[first + i], device_id=peer, device_id_type=pl.DeviceIdType.MESH)
        for i, (src, dst, peer) in enumerate(moves)
    ]


def exchange_kernel(n_cols, be, bw, fx, fy, vs, tm, sm, e3, w3, rows_b, tiles_b, send_sem, recv_sem):
    peers, row = meet(n_cols)
    moves = pack_moves(peers, row, be, bw, e3, w3) + row_moves(peers, row, (fx, fy), [rows_b.at[0], rows_b.at[1]]) + tile_moves(peers, row, (vs, tm, sm), tiles_b)
    copies = remote(moves, send_sem, recv_sem)
    start(copies)
    wait(copies)


def exchange(n_cols, *args):
    return pl.pallas_call(
        functools.partial(exchange_kernel, n_cols),
        out_shape=[f32(EXT_Y, LANES)] * 2 + [f32(2, WIDE, NX), f32(3, LEVELS, 8, NX)],
        in_specs=[ANY_SPEC] * 7,
        out_specs=[ANY_SPEC] * 4,
        scratch_shapes=[pltpu.SemaphoreType.DMA((9,)), pltpu.SemaphoreType.DMA((9,))],
        compiler_params=pltpu.CompilerParams(collective_id=1, has_side_effects=True, vmem_limit_bytes=62 * MIB),
        name="exchange",
    )(*args)


MIX = 32


def mix_kernel(n_cols, a1e, a1w, a2e, a2w, kf_ref, hf_ref, eta_hbm, tu_hbm, tv_hbm, u_hbm, v_hbm, t_hbm, s_hbm, e1, w1, e2, w2, rows_a, tiles_a, tmix_hbm, smix_hbm, mixed, ring, stage, part, in_sem, out_sem, send_sem, recv_sem):
    peers, row = meet(n_cols)
    moves = pack_moves(peers, row, a1e, a1w, e1, w1) + pack_moves(peers, row, a2e, a2w, e2, w2)
    moves += row_moves(peers, row, (kf_ref, hf_ref, eta_hbm, tu_hbm, tv_hbm), [rows_a.at[q] for q in range(5)])
    moves += tile_moves(peers, row, (u_hbm, v_hbm, t_hbm, s_hbm), tiles_a)
    copies = remote(moves, send_sem, recv_sem)
    start(copies)
    lane = lax.broadcasted_iota(jnp.int32, (MIX, LANES), 1)
    pair_id = ((lane + 1) >> 1) & 63
    n_tiles = NY // MIX

    def rows_of(t):
        return pl.ds(pl.multiple_of(t * MIX, MIX), MIX)

    def ins(t, slot):
        return [pltpu.make_async_copy(src.at[:, rows_of(t), :], ring.at[slot, f], in_sem.at[slot, f]) for f, src in enumerate((t_hbm, s_hbm))]

    def outs(t, slot):
        return [pltpu.make_async_copy(stage.at[slot, f], dst.at[:, rows_of(t), :], out_sem.at[slot, f]) for f, dst in enumerate((tmix_hbm, smix_hbm))]

    start(ins(0, 0))
    start(ins(1, 1))

    @pl.loop(0, n_tiles)
    def _(t):
        slot = lax.rem(t, 3)
        out_slot = lax.rem(t, 2)

        @pl.when(t + 2 < n_tiles)
        def _():
            start(ins(t + 2, lax.rem(t + 2, 3)))

        @pl.when(t >= 2)
        def _():
            wait(outs(t - 2, out_slot))

        wait(ins(t, slot))
        count = kf_ref[rows_of(t), :]
        thick = hf_ref[rows_of(t), :] / jnp.maximum(count, 1.0)
        safe = jnp.where(count > 0, thick, 1.0)
        coef = (TIME_STEP * DIFF_KT) / (safe * safe)
        zero = jnp.zeros((MIX, NX), jnp.float32)

        def down(k, state):
            pivot, lower, above_t, above_s = state
            level = k.astype(jnp.float32)
            upper = jnp.where(count > level + 1.0, coef, 0.0)
            inv = 1.0 / (pivot + upper)
            gain = upper * inv
            wet = count > level
            part_t = (jnp.where(wet, ring[slot, 0, k], 0.0) + lower * above_t) * inv
            part_s = (jnp.where(wet, ring[slot, 1, k], 0.0) + lower * above_s) * inv
            part[0, k] = part_t
            part[1, k] = part_s
            part[2, k] = gain
            return 1.0 + gain * pivot, upper, part_t, part_s

        lax.fori_loop(0, LEVELS, down, (zero + 1.0, zero, zero, zero))

        def up(i, state):
            below_t, below_s, braided = state
            k = LEVELS - 1 - i
            here_t = part[0, k] + part[2, k] * below_t
            here_s = part[1, k] + part[2, k] * below_s
            stage[out_slot, 0, k] = here_t
            stage[out_slot, 1, k] = here_s
            for f, vals in enumerate((here_t, here_s)):
                q = f * LEVELS + k
                both = jnp.where(lane == LANES - 1, vals[:, NX - LANES :], vals[:, :LANES])
                braided = jnp.where(pair_id == q, pltpu.roll(both, 2 * q, 1), braided)
            return here_t, here_s, braided

        mixed[rows_of(t), :] = lax.fori_loop(0, LEVELS, up, (zero, zero, jnp.zeros((MIX, LANES), jnp.float32)))[2]
        start(outs(t, out_slot))

    wait(outs(n_tiles - 2, 0))
    wait(outs(n_tiles - 1, 1))
    wait(copies)


def mix(n_cols, *args):
    cube = f32(LEVELS, NY, NX)
    return pl.pallas_call(
        functools.partial(mix_kernel, n_cols),
        out_shape=[f32(EXT_Y, LANES)] * 4 + [f32(5, WIDE, NX), f32(4, LEVELS, 8, NX), cube, cube, f32(NY, LANES)],
        in_specs=[ANY_SPEC] * 4 + [VMEM_SPEC] * 2 + [ANY_SPEC] * 7,
        out_specs=[ANY_SPEC] * 8 + [VMEM_SPEC],
        scratch_shapes=[
            pltpu.VMEM((3, 2, LEVELS, MIX, NX), jnp.float32),
            pltpu.VMEM((2, 2, LEVELS, MIX, NX), jnp.float32),
            pltpu.VMEM((3, LEVELS, MIX, NX), jnp.float32),
            pltpu.SemaphoreType.DMA((3, 2)),
            pltpu.SemaphoreType.DMA((2, 2)),
            pltpu.SemaphoreType.DMA((17,)),
            pltpu.SemaphoreType.DMA((17,)),
        ],
        compiler_params=pltpu.CompilerParams(collective_id=0, has_side_effects=True, vmem_limit_bytes=62 * MIB),
        name="mix",
    )(*args)


def predict_kernel(kf_ref, hf_ref, rows_ref, east_ref, west_ref, own_e_ref, own_w_ref, mixed, u_hbm, v_hbm, t_hbm, s_hbm, hy_hbm, ustar_hbm, vstar_hbm, fx_ref, fy_ref, usum_ref, be_ref, bw_ref, ring, kh, geo, carry, stage, part, sums, in_sem, out_sem):
    lane, sub = iotas()
    row = lax.axis_index("row")
    cubes = (u_hbm, v_hbm, t_hbm, s_hbm)
    level = (lane & (LEVELS - 1)).astype(jnp.float32)
    outs = (ustar_hbm, vstar_hbm)

    def tile_copies(t, slot):
        rows = pl.ds(pl.multiple_of(t * 8, 8), 8)
        return [pltpu.make_async_copy(cubes[a].at[:, rows, :], ring.at[slot, a], in_sem.at[slot, a]) for a in range(4)]

    def edge_copies(slot):
        return [pltpu.make_async_copy(hy_hbm.at[a], ring.at[slot, a], in_sem.at[slot, a]) for a in range(4)]

    def out_copies(t, slot):
        rows = pl.ds(pl.multiple_of(t * 8, 8), 8)
        return [pltpu.make_async_copy(stage.at[slot, a], outs[a].at[:, rows, :], out_sem.at[slot, a]) for a in range(2)]

    pair_id = ((lane + 1) >> 1) & 63
    zero = [jnp.zeros((8, LANES), jnp.float32)] * 4

    def eliminate(k, chain, mask, coef, fields, gain_at):
        down = [jnp.where(m > k + 1, c, 0.0) for m, c in zip(mask, coef)] if k < LEVELS - 1 else zero
        inv = [1.0 / (q + d) for q, d in zip(chain["q"], down)]
        gain = [d * r for d, r in zip(down, inv)]
        out = {}
        for a, (source, above) in fields.items():
            out[a] = [(s + l * x) * r for s, l, x, r in zip(source, chain["cl"], above, inv)]
            for c in range(4):
                part[a, k, :, chunk(c)] = out[a][c]
        for c in range(4):
            part[gain_at, k, :, chunk(c)] = gain[c]
        chain["q"] = [1.0 + g * q for g, q in zip(gain, chain["q"])]
        chain["cl"] = down
        return out

    def substitute(below, gain_of, slot, visit):
        for k in range(LEVELS - 1, -1, -1):
            for a, g in gain_of.items():
                if k < LEVELS - 1:
                    below[a] = [part[a, k, :, chunk(c)] + part[g, k, :, chunk(c)] * below[a][c] for c in range(4)]
                for c in range(4):
                    stage[slot, a, k, :, chunk(c)] = below[a][c]
                visit(k, a, below[a])

    start(tile_copies(0, 0))
    start(tile_copies(1, 1))
    start(tile_copies(2, 2))
    start(edge_copies(RING - 1))

    @pl.loop(0, SUB // 6)
    def _(i):
        for n in range(6):
            rows = tile_rows(i * 6 + n)
            for q in range(2):
                kh[q, rows, :] = side_planes(east_ref[rows, :], west_ref[rows, :], 64 + WIDE * q, lane)

    cut = jnp.where(row == 0, EXT_Y - 1, NY - 1)

    def chunks_of(q, t):
        if isinstance(t, int) and t >= TILES:
            main = rows_ref[q, (t - TILES) * 8 : (t - TILES + 1) * 8, :]
        else:
            main = (kf_ref, hf_ref)[q][tile_rows(t), :]
        return [lanes(main, c) for c in range(4)] + [kh[q, tile_rows(t), :]]

    def layout(t, t_next):
        k, h, kn, hn = chunks_of(0, t), chunks_of(1, t), chunks_of(0, t_next), chunks_of(1, t_next)
        dz = [a / jnp.maximum(b, 1.0) for a, b in zip(h, k)]
        dzn = [a / jnp.maximum(b, 1.0) for a, b in zip(hn, kn)]
        k_e = shift_east(k, k[0], lane)
        dz_e = shift_east(dz, dz[0], lane)
        k_n = [jnp.where(sub + t * 8 == cut, 0.0, x) for x in shift_north(k, kn, sub)]
        dz_n = shift_north(dz, dzn, sub)
        for c in range(CHUNKS):
            at = pl.ds(c * LANES, LANES)
            k_u = jnp.minimum(k[c], k_e[c])
            k_v = jnp.minimum(k[c], k_n[c])
            dz_u = 0.5 * (dz[c] + dz_e[c])
            dz_v = 0.5 * (dz[c] + dz_n[c])
            safe_c = jnp.where(k[c] > 0, dz[c], 1.0)
            safe_u = jnp.where(k_u > 0, dz_u, 1.0)
            safe_v = jnp.where(k_v > 0, dz_v, 1.0)
            cc = (TIME_STEP * DIFF_KT) / (safe_c * safe_c)
            cu = (TIME_STEP * VISC_KV) / (safe_u * safe_u)
            cv = (TIME_STEP * VISC_KV) / (safe_v * safe_v)
            for q, val in enumerate((k[c], k_u, k_v, dz[c], dz_u, dz_v, cc, cu, cv)):
                geo[q, t, :, at] = val

    @pl.loop(0, 7)
    def _(i):
        for n in range(4):
            layout(i * 4 + n, i * 4 + n + 1)

    for t in (28, 29, 30, 31, 32, 33):
        layout(t, t + 1)
    layout(SUB - 1, 0)
    wall = jnp.where(row == 0, SUB - 1, TILES)
    for q in range(3):
        geo[q, wall] = jnp.zeros((8, EXT_X), jnp.float32)

    def body(t, do_b, do_c):
        g2 = lax.rem(t + 2 + SUB, SUB)
        g1 = lax.rem(t + 1 + SUB, SUB)
        slot2 = lax.rem(t + 2 + RING, RING)
        slot1 = lax.rem(t + 1 + RING, RING)

        def plane(q, tt):
            return [geo[q, tt, :, chunk(c)] for c in range(4)]

        def count(q, tt, c, x):
            return column(geo[q, tt, :, chunk(c)], x)

        def west_u_of(g):
            return jnp.where(count(1, g, 4, LANES - 1) > level, west_ref[tile_rows(g), :], 0.0)

        ku2 = plane(1, g2)
        kv2 = plane(2, g2)
        west_u = west_u_of(g2)
        east_v = jnp.where(count(2, g2, 4, 0) > level, east_ref[tile_rows(g2), :], 0.0)
        outer = braid(east_v, 16, west_u, 0, lane)
        if do_b:
            k1 = plane(0, g1)
            ku1 = plane(1, g1)
            dz1 = [(TIME_STEP * GRAVITY) * x for x in plane(3, g1)]
            csum = zero
            sum_u = zero
            sum_v = zero
            east = east_ref[tile_rows(g1), :]
            inside = jnp.maximum(jnp.minimum(t + 1, TILES - 1), 0)
            own_u = jnp.where(count(1, g1, 3, LANES - 1) > level, own_e_ref[tile_rows(inside), :], 0.0)
            east_u = jnp.where(count(1, g1, 4, 0) > level, east, 0.0)
            half = jnp.where(count(0, g1, 4, 0) > level, (0.5 * BETA_S) * turn(east, -16) - (0.5 * ALPHA_T) * east + 0.5 * CONST_R, 0.0)
            run = half
            for reach in (1, 2, 4, 8):
                run = run + jnp.where(level >= reach, turn(run, reach), 0.0)
            pair = turn(own_u + east_u, 32)
            east_e = pair * pair + ((run + run) - half) * ((TIME_STEP * GRAVITY) * count(3, g1, 4, 0))
            low_u = west_u_of(g1)
            low_v = jnp.where(count(2, g1, 4, LANES - 1) > level, west_ref[tile_rows(g1), :], 0.0) + jnp.where(count(2, g1, 0, 0) > level, own_w_ref[tile_rows(inside), :], 0.0)
            west_q = (low_u + shift_north([low_u], [west_u], sub)[0]) * turn(low_v, -16)
            inner = braid(east_e, 32, west_q, 0, lane)
        if do_c:
            out_slot = lax.rem(t, 2)
            ku0 = plane(1, t)
            kv0 = plane(2, t)
            cu = plane(7, t)
            cv = plane(8, t)
            one = [jnp.ones((8, LANES), jnp.float32)] * 4
            chains = {n: {"q": one, "cl": zero} for n in "uv"}
            prev = {0: zero, 1: zero}
            total_m = [[sums[q, :, chunk(c)] for c in range(4)] for q in range(2)]

        for k in range(LEVELS):

            def tile(slot, a):
                return [ring[slot, a, k, :, chunk(c)] for c in range(4)]

            def old(q):
                return [carry[q, k, :, chunk(c)] for c in range(4)]

            def keep(q, vals):
                for c in range(4):
                    carry[q, k, :, chunk(c)] = vals[c]

            um2 = [jnp.where(m > k, x, 0.0) for m, x in zip(ku2, tile(slot2, 0))]
            vm2 = [jnp.where(m > k, x, 0.0) for m, x in zip(kv2, tile(slot2, 1))]
            outer_k = turn(outer, -2 * k)
            fresh = {}
            if do_b:
                um1, vm1, a1, ve1, q0, vm0 = old(5), old(6), old(7), old(8), old(3), old(4)
                inner_k = turn(inner, -2 * k)
                half_k = [jnp.where(m > k, (0.5 * BETA_S) * s - (0.5 * ALPHA_T) * x + 0.5 * CONST_R, 0.0) for m, x, s in zip(k1, tile(slot1, 2), tile(slot1, 3))]
                mid = [a + b for a, b in zip(csum, half_k)]
                csum = [a + b for a, b in zip(mid, half_k)]
                p1 = [a * b for a, b in zip(mid, dz1)]
                e1 = [a * a + p for a, p in zip(a1, p1)]
                e_e = shift_east(e1, inner_k, lane)
                v_s = shift_south(vm1, vm0, sub)
                b1 = [(a + b) * (a + b) + p for a, b, p in zip(v_s, vm1, p1)]
                u_n = shift_north(um1, um2, sub)
                q1 = [(a + b) * x for a, b, x in zip(um1, u_n, ve1)]
                q_s = shift_south(q1, q0, sub)
                q_w = shift_west(q1, inner_k, lane)
                fresh[0] = [jnp.where(m > k, u - ((f - e) + (q - s)), 0.0) for m, u, f, e, q, s in zip(ku1, um1, e_e, e1, q1, q_s)]
                fresh[1] = [(v + b) - (q - w) for v, b, q, w in zip(vm1, b1, q1, q_w)]
                fresh.update({2: b1, 3: q1, 4: vm1})
                sum_u = [a + b for a, b in zip(sum_u, um1)]
                sum_v = [a + b for a, b in zip(sum_v, vm1)]
            if do_c:
                source_u, half_v, b0 = old(0), old(1), old(2)
                source_v = [jnp.where(m > k, h - n, 0.0) for m, h, n in zip(kv0, half_v, shift_north(b0, b1, sub))]
                prev = {
                    0: eliminate(k, chains["u"], ku0, cu, {0: (source_u, prev[0])}, 4)[0],
                    1: eliminate(k, chains["v"], kv0, cv, {1: (source_v, prev[1])}, 5)[1],
                }
            fresh[5] = um2
            fresh[6] = vm2
            fresh[7] = [a + b for a, b in zip(um2, shift_west(um2, outer_k, lane))]
            fresh[8] = [a + b for a, b in zip(vm2, shift_east(vm2, outer_k, lane))]
            for q, vals in fresh.items():
                keep(q, vals)

        if do_b:
            for q, vals in enumerate((sum_u, sum_v)):
                for c in range(4):
                    sums[q, :, chunk(c)] = vals[c]
        if not do_c:
            return
        braided = [mixed[tile_rows(t), :]]
        total = {}

        def visit(k, a, vals):
            total[a] = [x + y for x, y in zip(total[a], vals)] if a in total else vals
            if a == 0:
                q = 2 * LEVELS + k
                braided[0] = jnp.where(pair_id == q, turn(vals[3], 2 * q), braided[0])

        substitute(prev, {0: 4, 1: 5}, out_slot, visit)
        rows = tile_rows(t)
        pack_e = pick(braided[0], (2 * lane + (LANES - 1)) & (LANES - 1))
        pack_w = pick(braided[0], (2 * lane) & (LANES - 1))
        for q in range(2):
            dz = plane(4 + q, t)
            force = [(1.0 / TIME_STEP) * (dz[c] * (total[q][c] - total_m[q][c])) for c in range(4)]
            for c in range(4):
                (fx_ref, fy_ref)[q][rows, chunk(c)] = force[c]
                usum_ref[q, rows, chunk(c)] = dz[c] * total[q][c]
            where = (lane >= WIDE * q) & (lane < WIDE * (q + 1))
            pack_e = jnp.where(where, turn(force[3], WIDE * q - LANES + WIDE), pack_e)
            pack_w = jnp.where(where, turn(force[0], WIDE * q), pack_w)
        be_ref[rows, :] = pack_e
        bw_ref[rows, :] = pack_w

    wait(edge_copies(RING - 1))
    body(-3, False, False)
    wait(tile_copies(0, 0))
    body(-2, True, False)
    wait(tile_copies(1, 1))
    body(-1, True, False)
    start(tile_copies(3, 3))

    @pl.loop(0, TILES)
    def _(t):
        @pl.when(t + 4 < TILES)
        def _():
            start(tile_copies(t + 4, lax.rem(t, RING)))

        @pl.when(t + 4 == TILES)
        def _():
            start(edge_copies(TILES % RING))

        @pl.when(t >= 2)
        def _():
            wait(out_copies(t - 2, lax.rem(t, 2)))

        @pl.when(t + 2 < TILES)
        def _():
            wait(tile_copies(t + 2, lax.rem(t + 2, RING)))

        @pl.when(t + 2 == TILES)
        def _():
            wait(edge_copies(TILES % RING))

        body(t, True, True)
        start(out_copies(t, lax.rem(t, 2)))

    wait(out_copies(TILES - 2, 0))
    wait(out_copies(TILES - 1, 1))


def predict(*args):
    return pl.pallas_call(
        predict_kernel,
        out_shape=[f32(LEVELS, NY, NX)] * 2 + [f32(NY, NX)] * 2 + [f32(2, NY, NX)] + [f32(NY, LANES)] * 2,
        in_specs=[VMEM_SPEC] * 8 + [ANY_SPEC] * 5,
        out_specs=[ANY_SPEC] * 2 + [VMEM_SPEC] * 5,
        scratch_shapes=[
            pltpu.VMEM((RING, 4, LEVELS, 8, NX), jnp.float32),
            pltpu.VMEM((2, EXT_Y, LANES), jnp.float32),
            pltpu.VMEM((9, SUB, 8, EXT_X), jnp.float32),
            pltpu.VMEM((9, LEVELS, 8, NX), jnp.float32),
            pltpu.VMEM((2, 2, LEVELS, 8, NX), jnp.float32),
            pltpu.VMEM((6, LEVELS, 8, NX), jnp.float32),
            pltpu.VMEM((2, 8, NX), jnp.float32),
            pltpu.SemaphoreType.DMA((RING, 4)),
            pltpu.SemaphoreType.DMA((2, 2)),
        ],
        compiler_params=pltpu.CompilerParams(vmem_limit_bytes=62 * MIB),
        name="predict",
    )(*args)


def east_of(x):
    return pltpu.roll(x, EXT_X - 1, 1)


def west_of(x):
    return pltpu.roll(x, 1, 1)


def north_wrap(x):
    return pltpu.roll(x, 7, 0)


def south_wrap(x):
    return pltpu.roll(x, 1, 0)


def finish_kernel(n_sub, tide_hbm, a1_e, a1_w, a2_e, a2_w, b_e, b_w, own_ref, usum_ref, kf_hbm, h_hbm, eta_in, tu_in, tv_in, rows_a, fx_hbm, fy_hbm, rows_b, ustar_hbm, vstar_hbm, tmix_hbm, smix_hbm, tiles_b, eta_hbm, u_hbm, v_hbm, uc_hbm, vc_hbm, tn_hbm, sn_hbm, nat, eta, u, v, au, fu, av, fv, ub, vb, cube, fy_old, pipe, stage, nat_sem, cube_sem, tile_sem, plane_sem, out_sem, tide_ref, tide_sem):
    dt_sub = TIME_STEP / n_sub
    weight_norm = 6.0 / (n_sub * (n_sub + 1) * (n_sub + 2))
    row = lax.axis_index("row")
    lane, sub = iotas()

    def plane_copies():
        copies = []
        for p, src in enumerate((kf_hbm, h_hbm, eta_in, tu_in, tv_in, fx_hbm, fy_hbm)):
            edge = rows_a.at[p] if p < 5 else rows_b.at[p - 5]
            for c in range(4):
                copies.append(pltpu.make_async_copy(src.at[:, chunk(c)], nat.at[p, c, pl.ds(0, NY), :], nat_sem.at[0, p, c]))
                copies.append(pltpu.make_async_copy(edge.at[:, chunk(c)], nat.at[p, c, pl.ds(NY, WIDE), :], nat_sem.at[1, p, c]))
        return copies

    cubes = (ustar_hbm, vstar_hbm, tmix_hbm, smix_hbm)
    strip = 64

    def cube_copies(i):
        rows = pl.ds(pl.multiple_of(i * strip, 8), strip)
        return [pltpu.make_async_copy(cubes[a].at[:, rows, :], cube.at[a, :, rows, :], cube_sem.at[a, i]) for a in range(4)]

    edge_copies = [pltpu.make_async_copy(tiles_b.at[i], cube.at[a, :, pl.ds(NY, 8), :], tile_sem.at[i]) for i, a in enumerate((1, 2, 3))]

    tide_copy = pltpu.make_async_copy(tide_hbm, tide_ref, tide_sem)
    tide_copy.start()
    start(plane_copies())

    @pl.loop(0, SUB // 4)
    def _(i):
        for n in range(4):
            rows = tile_rows(i * 4 + n)
            packs = [(a1_e[rows, :], a1_w[rows, :]), (a2_e[rows, :], a2_w[rows, :]), (b_e[rows, :], b_w[rows, :])]
            for p, (s, q) in enumerate(((0, 64), (0, 96), (1, 0), (1, 32), (1, 64), (2, 0), (2, 32))):
                nat[p, 4, rows, :] = side_planes(packs[s][0], packs[s][1], q, lane)

    wait(plane_copies())
    tide_copy.wait()
    start(edge_copies)
    for i in range(NY // strip):
        start(cube_copies(i))

    def plane(p, t):
        return jnp.concatenate([nat[p, c, pl.ds(t, 8, stride=SUB), :] for c in range(CHUNKS)], axis=1)

    cut = jnp.where(row == 0, EXT_Y - 1, NY - 1)
    sub_id = lax.broadcasted_iota(jnp.int32, (8, EXT_X), 0)

    def prepare(t, k_next, h_next):
        k = plane(0, t)
        dz = plane(1, t) / jnp.maximum(k, 1.0)
        k_n = jnp.where(sub_id * SUB + t == cut, 0.0, k_next)
        dz_n = h_next / jnp.maximum(k_next, 1.0)
        k_e = east_of(k)
        dz_e = east_of(dz)
        k_u = jnp.minimum(k, k_e)
        k_v = jnp.minimum(k, k_n)
        depth_u = k_u * (0.5 * (dz + dz_e))
        depth_v = k_v * (0.5 * (dz + dz_n))
        wet_u = k_u > 0
        wet_v = k_v > 0
        eta[t] = jnp.where(k > 0, plane(2, t), 0.0)
        u[t] = jnp.where(wet_u, dt_sub * plane(3, t), 0.0)
        v[t] = jnp.where(wet_v, dt_sub * plane(4, t), 0.0)
        au[t] = (dt_sub * dt_sub) * jnp.where(wet_u, depth_u, 0.0)
        av[t] = (dt_sub * dt_sub) * jnp.where(wet_v, depth_v, 0.0)
        fu[t] = jnp.where(wet_u, (dt_sub * dt_sub) * plane(5, t), 0.0)
        fv[t] = jnp.where(wet_v, (dt_sub * dt_sub) * plane(6, t), 0.0)
        ub[t] = jnp.zeros((8, EXT_X), jnp.float32)
        vb[t] = jnp.zeros((8, EXT_X), jnp.float32)

    @pl.loop(0, 7)
    def _(i):
        for n in range(5):
            prepare(i * 5 + n, plane(0, i * 5 + n + 1), plane(1, i * 5 + n + 1))

    prepare(SUB - 1, north_wrap(plane(0, 0)), north_wrap(plane(1, 0)))

    @pl.loop(0, n_sub)
    def _(n):
        tide_x = tide_ref[n, 0]
        tide_y = tide_ref[n, 1]
        weight = (weight_norm / dt_sub) * ((n + 1) * (n_sub - n)).astype(jnp.float32)

        def level(t, v_south):
            v_now = v[t]
            u_now = u[t]
            return eta[t] - ((u_now - west_of(u_now)) + (v_now - v_south)), v_now

        def accelerate(t, eta_now, eta_north):
            u_new = u[t] + (au[t] * ((tide_x + eta_now) - east_of(eta_now)) + fu[t])
            v_new = v[t] + (av[t] * ((tide_y + eta_now) - eta_north) + fv[t])
            u[t] = u_new
            v[t] = v_new
            ub[t] = ub[t] + weight * u_new
            vb[t] = vb[t] + weight * v_new

        eta_first, v_first = level(0, south_wrap(v[SUB - 1]))
        eta[0] = eta_first

        def sweep(t, carry):
            eta_now, v_now = carry
            eta_north, v_north = level(t + 1, v_now)
            eta[t + 1] = eta_north
            accelerate(t, eta_now, eta_north)
            return eta_north, v_north

        carry = (eta_first, v_first)
        for t in range(SUB - 1):
            carry = sweep(t, carry)
        eta_last = carry[0]
        accelerate(SUB - 1, eta_last, north_wrap(eta_first))

    @pl.loop(0, SUB // 6)
    def _(i):
        for n in range(6):
            t = i * 6 + n
            wet = plane(0, t) > 0
            for q, val in enumerate((jnp.where(wet, eta[t], 0.0), (1.0 / dt_sub) * u[t], (1.0 / dt_sub) * v[t], ub[t], vb[t])):
                for c in range(CHUNKS):
                    nat[2 + q, c, pl.ds(t, 8, stride=SUB), :] = lanes(val, c)

    plane_outs = [pltpu.make_async_copy(nat.at[2 + q, c, pl.ds(0, NY), :], out.at[:, chunk(c)], plane_sem.at[q, c]) for q, out in enumerate((eta_hbm, u_hbm, v_hbm)) for c in range(4)]
    start(plane_outs)

    def faces(t, t_next):
        k = [nat[0, c, tile_rows(t), :] for c in range(CHUNKS)]
        kn = [nat[0, c, tile_rows(t_next), :] for c in range(4)]
        dz = [nat[1, c, tile_rows(t), :] / jnp.maximum(k[c], 1.0) for c in range(CHUNKS)]
        dzn = [nat[1, c, tile_rows(t_next), :] / jnp.maximum(kn[c], 1.0) for c in range(4)]
        k_e = shift_east(k, k[0], lane)
        dz_e = shift_east(dz, dz[0], lane)
        k_n = [jnp.where(sub + t * 8 == cut, 0.0, x) for x in shift_north(k[:4], kn, sub)]
        dz_n = shift_north(dz[:4], dzn, sub)
        k_u = [jnp.minimum(a, b) for a, b in zip(k, k_e)]
        k_v = [jnp.minimum(a, b) for a, b in zip(k, k_n)]
        dz_u = [0.5 * (a + b) for a, b in zip(dz, dz_e)]
        dz_v = [0.5 * (a + b) for a, b in zip(dz, dz_n)]
        return k, k_u, k_v, dz_u, dz_v

    def correction(mean, total, k, dz):
        depth = k * dz
        return (mean - total) / jnp.where(depth > 0, depth, 1.0)

    def cube_tile(a, t, k):
        return [cube[a, k, tile_rows(t), chunk(c)] for c in range(4)]

    wait(edge_copies)
    wait(cube_copies(0))

    _, _, kv_low, _, dzv_low = faces(SUB - 1, 0)
    low = [jnp.zeros((8, LANES), jnp.float32)] * 4
    for k in range(LEVELS):
        low = [a + b for a, b in zip(low, cube_tile(1, TILES, k))]
    dv_low = [correction(nat[6, c, tile_rows(SUB - 1), :], dzv_low[c] * low[c], kv_low[c], dzv_low[c]) for c in range(4)]
    for k in range(LEVELS):
        vc = [jnp.where(m > k, x + d, 0.0) for m, x, d in zip(kv_low, cube_tile(1, TILES, k), dv_low)]
        for f in range(2):
            x = cube_tile(2 + f, TILES, k)
            x_n = shift_north(x, cube_tile(2 + f, 0, k), sub)
            for c in range(4):
                fy_old[f, k, :, chunk(c)] = vc[c] * (x[c] + x_n[c])

    level = (lane & (LEVELS - 1)).astype(jnp.float32)
    outs = (uc_hbm, vc_hbm, tn_hbm, sn_hbm)

    def out_copies(t, slot, fields):
        return [pltpu.make_async_copy(stage.at[slot, a], outs[a].at[:, tile_rows(t), :], out_sem.at[slot, a]) for a in fields]

    def pair_up(t, f, k, edge):
        x = cube_tile(2 + f, t, k)
        for c, e in enumerate(shift_east(x, edge, lane)):
            pipe[0, f, k, :, chunk(c)] = x[c] + e

    def conclude(kc, f, k, slot):
        for c in range(4):
            done = pipe[1, f, k, :, chunk(c)] - (0.5 * TIME_STEP) * pipe[2, f, k, :, chunk(c)]
            stage[slot, 2 + f, k, :, chunk(c)] = jnp.where(kc[c] > k, done, 0.0)

    first = braid(b_e[tile_rows(0), :], 64, b_w[tile_rows(0), :], 64, lane)
    for f in range(2):
        for k in range(LEVELS):
            pair_up(0, f, k, turn(first, -2 * (f * LEVELS + k)))

    @pl.loop(0, TILES)
    def _(t):
        slot = lax.rem(t, 2)

        @pl.when(t >= 2)
        def _():
            wait(out_copies(t - 2, slot, (0, 1)))

        @pl.when(t >= 3)
        def _():
            wait(out_copies(t - 3, slot, (2, 3)))

        for i in range(1, NY // strip):

            @pl.when(t == i * (strip // 8) - 1)
            def _():
                wait(cube_copies(i))

        kc_low = [nat[0, c, tile_rows(jnp.maximum(t - 1, 0)), :] for c in range(4)]
        kc, ku, kv, dz_u, dz_v = faces(t, t + 1)
        rows = tile_rows(t)
        west = b_w[rows, :]
        in_u = (lane >= 96) & (lane < 112)
        side_sum = jnp.broadcast_to(jnp.sum(jnp.where(in_u, west, 0.0), axis=1, keepdims=True), (8, LANES))
        side_d = column(correction(nat[5, 4, rows, :], dz_u[4] * side_sum, ku[4], dz_u[4]), LANES - 1)
        side_u = jnp.where(column(ku[4], LANES - 1) > level, west + side_d, 0.0)
        side_u = jnp.where(lane < 80, turn(side_u, -32), turn(side_u, -16))
        outer = braid(b_e[tile_rows(t + 1), :], 64, side_u * (west + own_ref[rows, :]), 64, lane)
        du = [correction(nat[5, c, rows, :], usum_ref[0, rows, chunk(c)], ku[c], dz_u[c]) for c in range(4)]
        dv = [correction(nat[6, c, rows, :], usum_ref[1, rows, chunk(c)], kv[c], dz_v[c]) for c in range(4)]
        for k in range(LEVELS):
            uc = [jnp.where(m > k, x + d, 0.0) for m, x, d in zip(ku, cube_tile(0, t, k), du)]
            vc = [jnp.where(m > k, x + d, 0.0) for m, x, d in zip(kv, cube_tile(1, t, k), dv)]
            for c in range(4):
                stage[slot, 0, k, :, chunk(c)] = uc[c]
                stage[slot, 1, k, :, chunk(c)] = vc[c]
            for f in range(2):
                edge = turn(outer, -2 * (f * LEVELS + k))
                conclude(kc_low, f, k, slot)
                fx = [a * pipe[0, f, k, :, chunk(c)] for c, a in enumerate(uc)]
                x = cube_tile(2 + f, t, k)
                x_n = shift_north(x, cube_tile(2 + f, t + 1, k), sub)
                fy = [a * (b + n) for a, b, n in zip(vc, x, x_n)]
                fy_s = shift_south(fy, [fy_old[f, k, :, chunk(c)] for c in range(4)], sub)
                fx_w = shift_west(fx, edge, lane)
                for c in range(4):
                    fy_old[f, k, :, chunk(c)] = fy[c]
                    pipe[1, f, k, :, chunk(c)] = x[c] - (0.5 * TIME_STEP) * (fy[c] - fy_s[c])
                    pipe[2, f, k, :, chunk(c)] = fx[c] - fx_w[c]
                pair_up(t + 1, f, k, edge)
        start(out_copies(t, slot, (0, 1)))

        @pl.when(t >= 1)
        def _():
            start(out_copies(t - 1, slot, (2, 3)))

    last = TILES - 1
    wait(out_copies(last - 2, TILES % 2, (2, 3)))
    kc_last = [nat[0, c, tile_rows(last), :] for c in range(4)]
    for f in range(2):
        for k in range(LEVELS):
            conclude(kc_last, f, k, TILES % 2)
    start(out_copies(last, TILES % 2, (2, 3)))
    wait(out_copies(last - 1, 0, (0, 1)))
    wait(out_copies(last, 1, (0, 1)))
    wait(out_copies(last - 1, 1, (2, 3)))
    wait(out_copies(last, 0, (2, 3)))
    wait(plane_outs)


def finish(tide_force, packs, own, usum, planes, rows_a, forces, rows_b, cubes, tiles_b):
    n_sub = tide_force.shape[0]
    big = pltpu.VMEM((SUB, 8, EXT_X), jnp.float32)
    return pl.pallas_call(
        functools.partial(finish_kernel, n_sub),
        out_shape=[f32(NY, NX)] * 3 + [f32(LEVELS, NY, NX)] * 4,
        in_specs=[ANY_SPEC] + [VMEM_SPEC] * 8 + [ANY_SPEC] * 14,
        out_specs=[ANY_SPEC] * 7,
        scratch_shapes=[pltpu.VMEM((7, CHUNKS, EXT_Y, LANES), jnp.float32)]
        + [big] * 9
        + [
            pltpu.VMEM((4, LEVELS, NY + 8, NX), jnp.float32),
            pltpu.VMEM((2, LEVELS, 8, NX), jnp.float32),
            pltpu.VMEM((3, 2, LEVELS, 8, NX), jnp.float32),
            pltpu.VMEM((2, 4, LEVELS, 8, NX), jnp.float32),
            pltpu.SemaphoreType.DMA((2, 7, 4)),
            pltpu.SemaphoreType.DMA((4, 4)),
            pltpu.SemaphoreType.DMA((3,)),
            pltpu.SemaphoreType.DMA((3, 4)),
            pltpu.SemaphoreType.DMA((2, 4)),
            pltpu.SMEM((n_sub, 2), jnp.float32),
            pltpu.SemaphoreType.DMA(()),
        ],
        compiler_params=pltpu.CompilerParams(vmem_limit_bytes=62 * MIB),
        name="finish",
    )(tide_force, *packs, own, usum, *planes, rows_a, *forces, rows_b, *cubes, tiles_b)


def solution(mesh):
    n_cols = mesh.shape["col"]

    def local_step(vel_u, vel_v, value_a11, salinity, sea_level, trans_u, trans_v, bathymetry, kmt_levels, tide_force):
        a1e, a1w, a2e, a2w, kf = pack(vel_u, vel_v, value_a11, salinity, kmt_levels, bathymetry, sea_level, trans_u, trans_v)
        planes = (kf, bathymetry, sea_level, trans_u, trans_v)
        cubes = (vel_u, vel_v, value_a11, salinity)
        e1, w1, e2, w2, rows_a, tiles_a, temp_mix, salt_mix, mixed = mix(n_cols, a1e, a1w, a2e, a2w, kf, bathymetry, sea_level, trans_u, trans_v, *cubes)
        u_star, v_star, fx, fy, usum, be, bw = predict(kf, bathymetry, rows_a, e1, w1, a1e, a1w, mixed, *cubes, tiles_a)
        e3, w3, rows_b, tiles_b = exchange(n_cols, be, bw, fx, fy, v_star, temp_mix, salt_mix)
        return tuple(finish(tide_force, (e1, w1, e2, w2, e3, w3), bw, usum, planes, rows_a, (fx, fy), rows_b, (u_star, v_star, temp_mix, salt_mix), tiles_b))

    spec_cube = P(None, "row", "col")
    spec_plane = P("row", "col")
    return jax.shard_map(local_step, mesh=mesh, in_specs=(spec_cube, spec_cube, spec_cube, spec_cube, spec_plane, spec_plane, spec_plane, spec_plane, spec_plane, P(None, None)), out_specs=(spec_plane, spec_plane, spec_plane, spec_cube, spec_cube, spec_cube, spec_cube), check_vma=False)
```

time: 220 us -> 163 us (0.74)
  Pallas kernels: 216 us -> 161 us
  local copies, waits for them, and re-layouts: 3.6 us -> 1.36 us
    pallas_call x1, Pallas kernels: 101 us -> 66.4 us  [finish(): pl.pallas_call(functools.partial(finish_kernel, n_sub), out_shape=[f32(NY...]
    pallas_call x3, Pallas kernels: 103 us -> 82.6 us  [the longest x1 43.8 us: predict(): pl.pallas_call(predict_kernel, out_shape=[f32(LEVELS, NY, NX)] * 2 + [f32...]
    squeeze x1 -> x0, local copies, waits for them, and re-layouts: 2.24 us -> none  [local_step(): force[1]]
where the time goes in v5:
time: 163 us
  Pallas kernels  161 us (99%)
    pallas_call x1, Pallas kernels, finish(): pl.pallas_call(functools.partial(finish_kernel, n_sub), out_shape=[f32(NY...  66.4 us
    pallas_call x1, Pallas kernels, predict(): pl.pallas_call(predict_kernel, out_shape=[f32(LEVELS, NY, NX)] * 2 + [f32...  43.8 us
    pallas_call x1, Pallas kernels, mix(): pl.pallas_call(functools.partial(mix_kernel, n_cols), out_shape=[f32(EXT_...  29.4 us
    pallas_call x1, Pallas kernels, pack(): pl.pallas_call(pack_kernel, out_shape=[f32(NY, LANES)] * 4 + [f32(NY, NX)...  12.2 us
    pallas_call x1, Pallas kernels, exchange(): pl.pallas_call(functools.partial(exchange_kernel, n_cols), out_shape=[f32...  9.4 us

profile of v5, /device:TPU:0, one launch (start us, length us, event | category | flops | bytes accessed | tf_op | source)
XLA Modules:
  0.0 163.1 jit_solution(8908277355329806989)
XLA Ops:
  0.6 1.4 copy.17.tide_hbm
  2.0 12.2 %pack.1 = (f32[256,128]{1,0:T(8,128)}, f32[256,128]{1,0:T(8,128)}, f32[256,128]{1,0:T(8,128)}, f32[256,128]{1,0:T(8,128)}, f32[256,512]{1,0:T(8,128)}) custom-call(f32[16,256,512]{2,1,0:T(8,128)} %u_hbm.5, f32[16,256,512]{2,1,0:T(8,128)} %v_hbm.5, f32[16,256,512]{2,1,0:T(8,128)} %t_hbm.5, f32[16,256,512]{2,1,0:T(8,128)} %s_hbm.5, s32[256,512]{1,0:T(8,128)} %k_ref.1, ...), custom_call_target="tpu_custom_call" | custom-call | tf_op jit(solution)/shard_map/pack/pallas_call | solution.py:150
  14.2 29.4 %mix.1 = (f32[288,128]{1,0:T(8,128)}, f32[288,128]{1,0:T(8,128)}, f32[288,128]{1,0:T(8,128)}, f32[288,128]{1,0:T(8,128)}, f32[5,32,512]{2,1,0:T(8,128)}, /*index...) custom-call(f32[256,128]{1,0:T(8,128)} %get-tuple-element.32.a1e.own_e_ref, ...), custom_call_target="tpu_custom_call" | custom-call | tf_op jit(solution)/shard_map/mix/pallas_call | solution.py:308
  43.6 43.8 %predict.1 = (f32[16,256,512]{2,1,0:T(8,128)}, f32[16,256,512]{2,1,0:T(8,128)}, f32[256,512]{1,0:T(8,128)}, f32[256,512]{1,0:T(8,128)}, f32[2,256,512]{2,1,0:T(8...) custom-call(f32[256,512]{1,0:T(8,128)} %get-tuple-element.36.kf_ref.kf_hbm, f32[256,512]{1,0:T(8,128)} %h_hbm.1, ...), custom_call_target="tpu_custom_call" | custom-call | tf_op jit(solution)/shard_map/predict/pallas_call | solution.py:599
  87.3 9.4 %exchange.1 = (f32[288,128]{1,0:T(8,128)}, f32[288,128]{1,0:T(8,128)}, f32[2,32,512]{2,1,0:T(8,128)}, f32[3,16,8,512]{3,2,1,0:T(8,128)}) custom-call(f32[256,128]{1,0:T(8,128)} %get-tuple-element.44.be, f32[256,128]{1,0:T(8,128)} %get-tuple-element.45.bw.own_ref, f32[256,512]{1,0:T(8,128)} %get-tuple-element.46.fx.fx_hbm, ...), custom_call_target="tpu_custom_call" | custom-call | tf_op jit(solution)/shard_map/exchange/pallas_call | solution.py:212
  96.7 66.4 %finish.1 = (f32[256,512]{1,0:T(8,128)}, f32[256,512]{1,0:T(8,128)}, f32[256,512]{1,0:T(8,128)}, f32[16,256,512]{2,1,0:T(8,128)}, f32[16,256,512]{2,1,0:T(8,128)...) custom-call(f32[30,2]{1,0:T(8,128)} %copy.17.tide_hbm, f32[288,128]{1,0:T(8,128)} %get-tuple-element.37.east_ref.a1_e, ...), custom_call_target="tpu_custom_call" | custom-call | tf_op jit(solution)/shard_map/finish/pallas_call | solution.py:893

commit v6 on v5

--- a/solution.py
+++ b/solution.py
@@ -116,8 +116,7 @@
     for i in range(NY // strip):
         wait(copies(i))
 
-        @pl.loop(0, strip // 8)
-        def _(t):
+        def tile(t, i=i):
             here = tile_rows(t)
             rows = pl.ds(pl.multiple_of(i * strip + t * 8, 8), 8)
             braided = jnp.zeros((8, LANES), jnp.float32)
@@ -146,6 +145,12 @@
             a2w[rows, :] = west2
 
 
+        @pl.loop(0, strip // 8 // 2)
+        def _(m):
+            for n in range(2):
+                tile(m * 2 + n)
+
+
 def pack(u, v, temp, salt, k, h, eta, tu, tv):
     return pl.pallas_call(
         pack_kernel,
@@ -220,10 +225,18 @@
     )(*args)
 
 
-MIX = 32
+MIX = 16
 
 
 def mix_kernel(n_cols, a1e, a1w, a2e, a2w, kf_ref, hf_ref, eta_hbm, tu_hbm, tv_hbm, u_hbm, v_hbm, t_hbm, s_hbm, e1, w1, e2, w2, rows_a, tiles_a, tmix_hbm, smix_hbm, mixed, ring, stage, part, in_sem, out_sem, send_sem, recv_sem):
+    def rows_of(t):
+        return pl.ds(pl.multiple_of(t * MIX, MIX), MIX)
+
+    def ins(t, slot):
+        return [pltpu.make_async_copy(src.at[:, rows_of(t), :], ring.at[slot, f], in_sem.at[slot, f]) for f, src in enumerate((t_hbm, s_hbm))]
+
+    start(ins(0, 0))
+    start(ins(1, 1))
     peers, row = meet(n_cols)
     moves = pack_moves(peers, row, a1e, a1w, e1, w1) + pack_moves(peers, row, a2e, a2w, e2, w2)
     moves += row_moves(peers, row, (kf_ref, hf_ref, eta_hbm, tu_hbm, tv_hbm), [rows_a.at[q] for q in range(5)])
@@ -234,17 +247,8 @@
     pair_id = ((lane + 1) >> 1) & 63
     n_tiles = NY // MIX
 
-    def rows_of(t):
-        return pl.ds(pl.multiple_of(t * MIX, MIX), MIX)
-
-    def ins(t, slot):
-        return [pltpu.make_async_copy(src.at[:, rows_of(t), :], ring.at[slot, f], in_sem.at[slot, f]) for f, src in enumerate((t_hbm, s_hbm))]
-
     def outs(t, slot):
         return [pltpu.make_async_copy(stage.at[slot, f], dst.at[:, rows_of(t), :], out_sem.at[slot, f]) for f, dst in enumerate((tmix_hbm, smix_hbm))]
-
-    start(ins(0, 0))
-    start(ins(1, 1))
 
     @pl.loop(0, n_tiles)
     def _(t):
@@ -266,37 +270,46 @@
         coef = (TIME_STEP * DIFF_KT) / (safe * safe)
         zero = jnp.zeros((MIX, NX), jnp.float32)
 
-        def down(k, state):
+        def down(i, state):
             pivot, lower, above_t, above_s = state
-            level = k.astype(jnp.float32)
-            upper = jnp.where(count > level + 1.0, coef, 0.0)
-            inv = 1.0 / (pivot + upper)
-            gain = upper * inv
-            wet = count > level
-            part_t = (jnp.where(wet, ring[slot, 0, k], 0.0) + lower * above_t) * inv
-            part_s = (jnp.where(wet, ring[slot, 1, k], 0.0) + lower * above_s) * inv
-            part[0, k] = part_t
-            part[1, k] = part_s
-            part[2, k] = gain
-            return 1.0 + gain * pivot, upper, part_t, part_s
-
-        lax.fori_loop(0, LEVELS, down, (zero + 1.0, zero, zero, zero))
+            for n in range(2):
+                k = i * 2 + n
+                level = k.astype(jnp.float32)
+                upper = jnp.where(count > level + 1.0, coef, 0.0)
+                inv = 1.0 / (pivot + upper)
+                gain = upper * inv
+                wet = count > level
+                above_t = (jnp.where(wet, ring[slot, 0, k], 0.0) + lower * above_t) * inv
+                above_s = (jnp.where(wet, ring[slot, 1, k], 0.0) + lower * above_s) * inv
+                part[0, k] = above_t
+                part[1, k] = above_s
+                part[2, k] = gain
+                pivot = 1.0 + gain * pivot
+                lower = upper
+            return pivot, lower, above_t, above_s
+
+        lax.fori_loop(0, LEVELS // 2, down, (zero + 1.0, zero, zero, zero))
 
         def up(i, state):
-            below_t, below_s, braided = state
-            k = LEVELS - 1 - i
-            here_t = part[0, k] + part[2, k] * below_t
-            here_s = part[1, k] + part[2, k] * below_s
-            stage[out_slot, 0, k] = here_t
-            stage[out_slot, 1, k] = here_s
-            for f, vals in enumerate((here_t, here_s)):
+            below_t, below_s = state
+            for n in range(2):
+                k = LEVELS - 1 - (i * 2 + n)
+                gain = part[2, k]
+                below_t = part[0, k] + gain * below_t
+                below_s = part[1, k] + gain * below_s
+                stage[out_slot, 0, k] = below_t
+                stage[out_slot, 1, k] = below_s
+            return below_t, below_s
+
+        lax.fori_loop(0, LEVELS // 2, up, (zero, zero))
+        start(outs(t, out_slot))
+        braided = jnp.zeros((MIX, LANES), jnp.float32)
+        for f in range(2):
+            for k in range(LEVELS):
                 q = f * LEVELS + k
-                both = jnp.where(lane == LANES - 1, vals[:, NX - LANES :], vals[:, :LANES])
-                braided = jnp.where(pair_id == q, pltpu.roll(both, 2 * q, 1), braided)
-            return here_t, here_s, braided
-
-        mixed[rows_of(t), :] = lax.fori_loop(0, LEVELS, up, (zero, zero, jnp.zeros((MIX, LANES), jnp.float32)))[2]
-        start(outs(t, out_slot))
+                both = jnp.where(lane == LANES - 1, stage[out_slot, f, k, :, NX - LANES :], stage[out_slot, f, k, :, :LANES])
+                braided = jnp.where(pair_id == q, turn(both, 2 * q), braided)
+        mixed[rows_of(t), :] = braided
 
     wait(outs(n_tiles - 2, 0))
     wait(outs(n_tiles - 1, 1))
@@ -633,7 +646,7 @@
     return pltpu.roll(x, 1, 0)
 
 
-def finish_kernel(n_sub, tide_hbm, a1_e, a1_w, a2_e, a2_w, b_e, b_w, own_ref, usum_ref, kf_hbm, h_hbm, eta_in, tu_in, tv_in, rows_a, fx_hbm, fy_hbm, rows_b, ustar_hbm, vstar_hbm, tmix_hbm, smix_hbm, tiles_b, eta_hbm, u_hbm, v_hbm, uc_hbm, vc_hbm, tn_hbm, sn_hbm, nat, eta, u, v, au, fu, av, fv, ub, vb, cube, fy_old, pipe, stage, nat_sem, cube_sem, tile_sem, plane_sem, out_sem, tide_ref, tide_sem):
+def finish_kernel(n_sub, tide_hbm, a1_e, a1_w, a2_e, a2_w, b_e, b_w, own_ref, usum_ref, kf_hbm, h_hbm, eta_in, tu_in, tv_in, rows_a, fx_hbm, fy_hbm, rows_b, ustar_hbm, vstar_hbm, tmix_hbm, smix_hbm, tiles_b, eta_hbm, u_hbm, v_hbm, uc_hbm, vc_hbm, tn_hbm, sn_hbm, nat, eta, u, ud, aw, fd, v, au, fu, av, fv, ub, vb, cube, fy_old, pipe, stage, nat_sem, cube_sem, tile_sem, plane_sem, out_sem, tide_ref, tide_sem):
     dt_sub = TIME_STEP / n_sub
     weight_norm = 6.0 / (n_sub * (n_sub + 1) * (n_sub + 2))
     row = lax.axis_index("row")
@@ -695,11 +708,17 @@
         wet_u = k_u > 0
         wet_v = k_v > 0
         eta[t] = jnp.where(k > 0, plane(2, t), 0.0)
-        u[t] = jnp.where(wet_u, dt_sub * plane(3, t), 0.0)
+        u_start = jnp.where(wet_u, dt_sub * plane(3, t), 0.0)
+        slope_u = (dt_sub * dt_sub) * jnp.where(wet_u, depth_u, 0.0)
+        force_u = jnp.where(wet_u, (dt_sub * dt_sub) * plane(5, t), 0.0)
+        u[t] = u_start
+        ud[t] = u_start - west_of(u_start)
         v[t] = jnp.where(wet_v, dt_sub * plane(4, t), 0.0)
-        au[t] = (dt_sub * dt_sub) * jnp.where(wet_u, depth_u, 0.0)
+        au[t] = slope_u
+        aw[t] = west_of(slope_u)
         av[t] = (dt_sub * dt_sub) * jnp.where(wet_v, depth_v, 0.0)
-        fu[t] = jnp.where(wet_u, (dt_sub * dt_sub) * plane(5, t), 0.0)
+        fu[t] = force_u
+        fd[t] = force_u - west_of(force_u)
         fv[t] = jnp.where(wet_v, (dt_sub * dt_sub) * plane(6, t), 0.0)
         ub[t] = jnp.zeros((8, EXT_X), jnp.float32)
         vb[t] = jnp.zeros((8, EXT_X), jnp.float32)
@@ -711,19 +730,20 @@
 
     prepare(SUB - 1, north_wrap(plane(0, 0)), north_wrap(plane(1, 0)))
 
-    @pl.loop(0, n_sub)
-    def _(n):
-        tide_x = tide_ref[n, 0]
-        tide_y = tide_ref[n, 1]
+    def substep(n):
+        tide_x = tide_ref[0, n]
+        tide_y = tide_ref[1, n]
         weight = (weight_norm / dt_sub) * ((n + 1) * (n_sub - n)).astype(jnp.float32)
 
         def level(t, v_south):
             v_now = v[t]
-            u_now = u[t]
-            return eta[t] - ((u_now - west_of(u_now)) + (v_now - v_south)), v_now
+            return eta[t] - (ud[t] + (v_now - v_south)), v_now
 
         def accelerate(t, eta_now, eta_north):
-            u_new = u[t] + (au[t] * ((tide_x + eta_now) - east_of(eta_now)) + fu[t])
+            push = au[t] * ((tide_x + eta_now) - east_of(eta_now))
+            push_west = aw[t] * ((tide_x + west_of(eta_now)) - eta_now)
+            u_new = u[t] + (push + fu[t])
+            ud[t] = ud[t] + ((push - push_west) + fd[t])
             v_new = v[t] + (av[t] * ((tide_y + eta_now) - eta_north) + fv[t])
             u[t] = u_new
             v[t] = v_new
@@ -745,6 +765,14 @@
             carry = sweep(t, carry)
         eta_last = carry[0]
         accelerate(SUB - 1, eta_last, north_wrap(eta_first))
+
+    per_loop = next(m for m in (1, 2, 1) if n_sub % m == 0)
+
+    @pl.loop(0, n_sub // per_loop)
+    def _(i):
+        for m in range(per_loop):
+            substep(i * per_loop + m)
+
 
     @pl.loop(0, SUB // 6)
     def _(i):
@@ -888,7 +916,7 @@
 
 
 def finish(tide_force, packs, own, usum, planes, rows_a, forces, rows_b, cubes, tiles_b):
-    n_sub = tide_force.shape[0]
+    n_sub = tide_force.shape[1]
     big = pltpu.VMEM((SUB, 8, EXT_X), jnp.float32)
     return pl.pallas_call(
         functools.partial(finish_kernel, n_sub),
@@ -896,7 +924,7 @@
         in_specs=[ANY_SPEC] + [VMEM_SPEC] * 8 + [ANY_SPEC] * 14,
         out_specs=[ANY_SPEC] * 7,
         scratch_shapes=[pltpu.VMEM((7, CHUNKS, EXT_Y, LANES), jnp.float32)]
-        + [big] * 9
+        + [big] * 12
         + [
             pltpu.VMEM((4, LEVELS, NY + 8, NX), jnp.float32),
             pltpu.VMEM((2, LEVELS, 8, NX), jnp.float32),
@@ -907,7 +935,7 @@
             pltpu.SemaphoreType.DMA((3,)),
             pltpu.SemaphoreType.DMA((3, 4)),
             pltpu.SemaphoreType.DMA((2, 4)),
-            pltpu.SMEM((n_sub, 2), jnp.float32),
+            pltpu.SMEM((2, n_sub), jnp.float32),
             pltpu.SemaphoreType.DMA(()),
         ],
         compiler_params=pltpu.CompilerParams(vmem_limit_bytes=62 * MIB),
@@ -925,7 +953,7 @@
         e1, w1, e2, w2, rows_a, tiles_a, temp_mix, salt_mix, mixed = mix(n_cols, a1e, a1w, a2e, a2w, kf, bathymetry, sea_level, trans_u, trans_v, *cubes)
         u_star, v_star, fx, fy, usum, be, bw = predict(kf, bathymetry, rows_a, e1, w1, a1e, a1w, mixed, *cubes, tiles_a)
         e3, w3, rows_b, tiles_b = exchange(n_cols, be, bw, fx, fy, v_star, temp_mix, salt_mix)
-        return tuple(finish(tide_force, (e1, w1, e2, w2, e3, w3), bw, usum, planes, rows_a, (fx, fy), rows_b, (u_star, v_star, temp_mix, salt_mix), tiles_b))
+        return tuple(finish(tide_force.T, (e1, w1, e2, w2, e3, w3), bw, usum, planes, rows_a, (fx, fy), rows_b, (u_star, v_star, temp_mix, salt_mix), tiles_b))
 
     spec_cube = P(None, "row", "col")
     spec_plane = P("row", "col")

time: 163 us -> 138 us (0.85)
  Pallas kernels: 161 us -> 136 us
    pallas_call x1, Pallas kernels: 66.4 us -> 52.5 us  [finish(): pl.pallas_call(functools.partial(finish_kernel, n_sub), out_shape=[f32(NY...]
    pallas_call x1, Pallas kernels: 29.4 us -> 20.4 us  [mix(): pl.pallas_call(functools.partial(mix_kernel, n_cols), out_shape=[f32(EXT_...]
    pallas_call x1, Pallas kernels: 12.2 us -> 10.1 us  [pack(): pl.pallas_call(pack_kernel, out_shape=[f32(NY, LANES)] * 4 + [f32(NY, NX)...]
where the time goes in v6:
time: 138 us; the launch traced here: 137 us
  Pallas kernels  136 us (99%)
    pallas_call x1, Pallas kernels, finish(): pl.pallas_call(functools.partial(finish_kernel, n_sub), out_shape=[f32(NY...  52.5 us
    pallas_call x1, Pallas kernels, predict(): pl.pallas_call(predict_kernel, out_shape=[f32(LEVELS, NY, NX)] * 2 + [f32...  43.8 us
    pallas_call x1, Pallas kernels, mix(): pl.pallas_call(functools.partial(mix_kernel, n_cols), out_shape=[f32(EXT_...  20.4 us
    pallas_call x1, Pallas kernels, pack(): pl.pallas_call(pack_kernel, out_shape=[f32(NY, LANES)] * 4 + [f32(NY, NX)...  10.1 us
    pallas_call x1, Pallas kernels, exchange(): pl.pallas_call(functools.partial(exchange_kernel, n_cols), out_shape=[f32...  9.66 us

profile of v6, /device:TPU:0, one launch (start us, length us, event | category | flops | bytes accessed | tf_op | source)
XLA Modules:
  0.0 137.1 jit_solution(4980959917641646296)
XLA Ops:
  0.6 10.1 %pack.1 = (f32[256,128]{1,0:T(8,128)}, f32[256,128]{1,0:T(8,128)}, f32[256,128]{1,0:T(8,128)}, f32[256,128]{1,0:T(8,128)}, f32[256,512]{1,0:T(8,128)}) custom-call(f32[16,256,512]{2,1,0:T(8,128)} %u_hbm.5, f32[16,256,512]{2,1,0:T(8,128)} %v_hbm.5, f32[16,256,512]{2,1,0:T(8,128)} %t_hbm.5, f32[16,256,512]{2,1,0:T(8,128)} %s_hbm.5, s32[256,512]{1,0:T(8,128)} %k_ref.1, ...), custom_call_target="tpu_custom_call" | custom-call | tf_op jit(solution)/shard_map/pack/pallas_call | solution.py:155
  10.8 20.4 %mix.1 = (f32[288,128]{1,0:T(8,128)}, f32[288,128]{1,0:T(8,128)}, f32[288,128]{1,0:T(8,128)}, f32[288,128]{1,0:T(8,128)}, f32[5,32,512]{2,1,0:T(8,128)}, /*index...) custom-call(f32[256,128]{1,0:T(8,128)} %get-tuple-element.32.a1e.own_e_ref, ...), custom_call_target="tpu_custom_call" | custom-call | tf_op jit(solution)/shard_map/mix/pallas_call | solution.py:321
  31.2 43.8 %predict.1 = (f32[16,256,512]{2,1,0:T(8,128)}, f32[16,256,512]{2,1,0:T(8,128)}, f32[256,512]{1,0:T(8,128)}, f32[256,512]{1,0:T(8,128)}, f32[2,256,512]{2,1,0:T(8...) custom-call(f32[256,512]{1,0:T(8,128)} %get-tuple-element.36.kf_ref.kf_hbm, f32[256,512]{1,0:T(8,128)} %h_hbm.1, ...), custom_call_target="tpu_custom_call" | custom-call | tf_op jit(solution)/shard_map/predict/pallas_call | solution.py:612
  75.0 9.7 %exchange.1 = (f32[288,128]{1,0:T(8,128)}, f32[288,128]{1,0:T(8,128)}, f32[2,32,512]{2,1,0:T(8,128)}, f32[3,16,8,512]{3,2,1,0:T(8,128)}) custom-call(f32[256,128]{1,0:T(8,128)} %get-tuple-element.44.be, f32[256,128]{1,0:T(8,128)} %get-tuple-element.45.bw.own_ref, f32[256,512]{1,0:T(8,128)} %get-tuple-element.46.fx.fx_hbm, ...), custom_call_target="tpu_custom_call" | custom-call | tf_op jit(solution)/shard_map/exchange/pallas_call | solution.py:217
  84.6 52.5 %finish.1 = (f32[256,512]{1,0:T(8,128)}, f32[256,512]{1,0:T(8,128)}, f32[256,512]{1,0:T(8,128)}, f32[16,256,512]{2,1,0:T(8,128)}, f32[16,256,512]{2,1,0:T(8,128)...) custom-call(f32[2,30]{1,0:T(2,128)} %bitcast.1, f32[288,128]{1,0:T(8,128)} %get-tuple-element.37.east_ref.a1_e, ...), custom_call_target="tpu_custom_call" | custom-call | tf_op jit(solution)/shard_map/finish/pallas_call | solution.py:921

commit v7 on v6

--- a/solution.py
+++ b/solution.py
@@ -337,7 +337,7 @@
     )(*args)
 
 
-def predict_kernel(kf_ref, hf_ref, rows_ref, east_ref, west_ref, own_e_ref, own_w_ref, mixed, u_hbm, v_hbm, t_hbm, s_hbm, hy_hbm, ustar_hbm, vstar_hbm, fx_ref, fy_ref, usum_ref, be_ref, bw_ref, ring, kh, geo, carry, stage, part, sums, in_sem, out_sem):
+def predict_kernel(kf_ref, hf_ref, rows_ref, east_ref, west_ref, own_e_ref, own_w_ref, mixed, u_hbm, v_hbm, t_hbm, s_hbm, hy_hbm, ustar_hbm, vstar_hbm, fx_ref, fy_ref, usum_ref, be_ref, bw_ref, ring, kh, geo, carry, stage, part, sums, edge_now, in_sem, out_sem):
     lane, sub = iotas()
     row = lax.axis_index("row")
     cubes = (u_hbm, v_hbm, t_hbm, s_hbm)
@@ -438,6 +438,33 @@
     for q in range(3):
         geo[q, wall] = jnp.zeros((8, EXT_X), jnp.float32)
 
+    def edges(t):
+        g2 = lax.rem(t + 2 + SUB, SUB)
+        g1 = lax.rem(t + 1 + SUB, SUB)
+
+        def count(q, tt, c, x):
+            return column(geo[q, tt, :, chunk(c)], x)
+
+        def west_u_of(g):
+            return jnp.where(count(1, g, 4, LANES - 1) > level, west_ref[tile_rows(g), :], 0.0)
+
+        west_u = west_u_of(g2)
+        east_v = jnp.where(count(2, g2, 4, 0) > level, east_ref[tile_rows(g2), :], 0.0)
+        east = east_ref[tile_rows(g1), :]
+        inside = jnp.maximum(jnp.minimum(t + 1, TILES - 1), 0)
+        own_u = jnp.where(count(1, g1, 3, LANES - 1) > level, own_e_ref[tile_rows(inside), :], 0.0)
+        east_u = jnp.where(count(1, g1, 4, 0) > level, east, 0.0)
+        half = jnp.where(count(0, g1, 4, 0) > level, (0.5 * BETA_S) * turn(east, -16) - (0.5 * ALPHA_T) * east + 0.5 * CONST_R, 0.0)
+        run = half
+        for reach in (1, 2, 4, 8):
+            run = run + jnp.where(level >= reach, turn(run, reach), 0.0)
+        pair = turn(own_u + east_u, 32)
+        east_e = pair * pair + ((run + run) - half) * ((TIME_STEP * GRAVITY) * count(3, g1, 4, 0))
+        low_u = west_u_of(g1)
+        low_v = jnp.where(count(2, g1, 4, LANES - 1) > level, west_ref[tile_rows(g1), :], 0.0) + jnp.where(count(2, g1, 0, 0) > level, own_w_ref[tile_rows(inside), :], 0.0)
+        west_q = (low_u + shift_north([low_u], [west_u], sub)[0]) * turn(low_v, -16)
+        return braid(east_v, 16, west_u, 0, lane), braid(east_e, 32, west_q, 0, lane)
+
     def body(t, do_b, do_c):
         g2 = lax.rem(t + 2 + SUB, SUB)
         g1 = lax.rem(t + 1 + SUB, SUB)
@@ -447,17 +474,10 @@
         def plane(q, tt):
             return [geo[q, tt, :, chunk(c)] for c in range(4)]
 
-        def count(q, tt, c, x):
-            return column(geo[q, tt, :, chunk(c)], x)
-
-        def west_u_of(g):
-            return jnp.where(count(1, g, 4, LANES - 1) > level, west_ref[tile_rows(g), :], 0.0)
-
         ku2 = plane(1, g2)
         kv2 = plane(2, g2)
-        west_u = west_u_of(g2)
-        east_v = jnp.where(count(2, g2, 4, 0) > level, east_ref[tile_rows(g2), :], 0.0)
-        outer = braid(east_v, 16, west_u, 0, lane)
+        outer = edge_now[0]
+        inner = edge_now[1]
         if do_b:
             k1 = plane(0, g1)
             ku1 = plane(1, g1)
@@ -465,20 +485,6 @@
             csum = zero
             sum_u = zero
             sum_v = zero
-            east = east_ref[tile_rows(g1), :]
-            inside = jnp.maximum(jnp.minimum(t + 1, TILES - 1), 0)
-            own_u = jnp.where(count(1, g1, 3, LANES - 1) > level, own_e_ref[tile_rows(inside), :], 0.0)
-            east_u = jnp.where(count(1, g1, 4, 0) > level, east, 0.0)
-            half = jnp.where(count(0, g1, 4, 0) > level, (0.5 * BETA_S) * turn(east, -16) - (0.5 * ALPHA_T) * east + 0.5 * CONST_R, 0.0)
-            run = half
-            for reach in (1, 2, 4, 8):
-                run = run + jnp.where(level >= reach, turn(run, reach), 0.0)
-            pair = turn(own_u + east_u, 32)
-            east_e = pair * pair + ((run + run) - half) * ((TIME_STEP * GRAVITY) * count(3, g1, 4, 0))
-            low_u = west_u_of(g1)
-            low_v = jnp.where(count(2, g1, 4, LANES - 1) > level, west_ref[tile_rows(g1), :], 0.0) + jnp.where(count(2, g1, 0, 0) > level, own_w_ref[tile_rows(inside), :], 0.0)
-            west_q = (low_u + shift_north([low_u], [west_u], sub)[0]) * turn(low_v, -16)
-            inner = braid(east_e, 32, west_q, 0, lane)
         if do_c:
             out_slot = lax.rem(t, 2)
             ku0 = plane(1, t)
@@ -490,6 +496,7 @@
             prev = {0: zero, 1: zero}
             total_m = [[sums[q, :, chunk(c)] for c in range(4)] for q in range(2)]
 
+        outers, inners = [], []
         for k in range(LEVELS):
 
             def tile(slot, a):
@@ -504,11 +511,13 @@
 
             um2 = [jnp.where(m > k, x, 0.0) for m, x in zip(ku2, tile(slot2, 0))]
             vm2 = [jnp.where(m > k, x, 0.0) for m, x in zip(kv2, tile(slot2, 1))]
-            outer_k = turn(outer, -2 * k)
+            outer_k = turn(outer, -2 * k) if k < 3 else turn(outers[k - 3], -2 * 3)
+            outers.append(outer_k)
             fresh = {}
             if do_b:
                 um1, vm1, a1, ve1, q0, vm0 = old(5), old(6), old(7), old(8), old(3), old(4)
-                inner_k = turn(inner, -2 * k)
+                inner_k = turn(inner, -2 * k) if k < 3 else turn(inners[k - 3], -2 * 3)
+                inners.append(inner_k)
                 half_k = [jnp.where(m > k, (0.5 * BETA_S) * s - (0.5 * ALPHA_T) * x + 0.5 * CONST_R, 0.0) for m, x, s in zip(k1, tile(slot1, 2), tile(slot1, 3))]
                 mid = [a + b for a, b in zip(csum, half_k)]
                 csum = [a + b for a, b in zip(mid, half_k)]
@@ -540,6 +549,7 @@
             for q, vals in fresh.items():
                 keep(q, vals)
 
+        edge_now[0], edge_now[1] = edges(t + 1)
         if do_b:
             for q, vals in enumerate((sum_u, sum_v)):
                 for c in range(4):
@@ -571,6 +581,7 @@
         be_ref[rows, :] = pack_e
         bw_ref[rows, :] = pack_w
 
+    edge_now[0], edge_now[1] = edges(-3)
     wait(edge_copies(RING - 1))
     body(-3, False, False)
     wait(tile_copies(0, 0))
@@ -622,6 +633,7 @@
             pltpu.VMEM((2, 2, LEVELS, 8, NX), jnp.float32),
             pltpu.VMEM((6, LEVELS, 8, NX), jnp.float32),
             pltpu.VMEM((2, 8, NX), jnp.float32),
+            pltpu.VMEM((2, 8, LANES), jnp.float32),
             pltpu.SemaphoreType.DMA((RING, 4)),
             pltpu.SemaphoreType.DMA((2, 2)),
         ],
@@ -766,7 +778,7 @@
         eta_last = carry[0]
         accelerate(SUB - 1, eta_last, north_wrap(eta_first))
 
-    per_loop = next(m for m in (1, 2, 1) if n_sub % m == 0)
+    per_loop = next(m for m in (2, 1) if n_sub % m == 0)
 
     @pl.loop(0, n_sub // per_loop)
     def _(i):

time: 138 us -> 131 us (0.949)
  Pallas kernels: 136 us -> 130 us
    pallas_call x1, Pallas kernels: 43.8 us -> 37.2 us  [predict(): pl.pallas_call(predict_kernel, out_shape=[f32(LEVELS, NY, NX)] * 2 + [f32...]
where the time goes in v7:
time: 131 us; the launch traced here: 130 us
  Pallas kernels  130 us (99%)
    pallas_call x1, Pallas kernels, finish(): pl.pallas_call(functools.partial(finish_kernel, n_sub), out_shape=[f32(NY...  52.2 us
    pallas_call x1, Pallas kernels, predict(): pl.pallas_call(predict_kernel, out_shape=[f32(LEVELS, NY, NX)] * 2 + [f32...  37.2 us
    pallas_call x1, Pallas kernels, mix(): pl.pallas_call(functools.partial(mix_kernel, n_cols), out_shape=[f32(EXT_...  20.4 us
    pallas_call x1, Pallas kernels, pack(): pl.pallas_call(pack_kernel, out_shape=[f32(NY, LANES)] * 4 + [f32(NY, NX)...  10.1 us
    pallas_call x1, Pallas kernels, exchange(): pl.pallas_call(functools.partial(exchange_kernel, n_cols), out_shape=[f32...  9.66 us

profile of v7, /device:TPU:0, one launch (start us, length us, event | category | flops | bytes accessed | tf_op | source)
XLA Modules:
  0.0 130.2 jit_solution(11108193335563946888)
XLA Ops:
  0.6 10.1 %pack.1 = (f32[256,128]{1,0:T(8,128)}, f32[256,128]{1,0:T(8,128)}, f32[256,128]{1,0:T(8,128)}, f32[256,128]{1,0:T(8,128)}, f32[256,512]{1,0:T(8,128)}) custom-call(f32[16,256,512]{2,1,0:T(8,128)} %u_hbm.5, f32[16,256,512]{2,1,0:T(8,128)} %v_hbm.5, f32[16,256,512]{2,1,0:T(8,128)} %t_hbm.5, f32[16,256,512]{2,1,0:T(8,128)} %s_hbm.5, s32[256,512]{1,0:T(8,128)} %k_ref.1, ...), custom_call_target="tpu_custom_call" | custom-call | tf_op jit(solution)/shard_map/pack/pallas_call | solution.py:155
  10.8 20.4 %mix.1 = (f32[288,128]{1,0:T(8,128)}, f32[288,128]{1,0:T(8,128)}, f32[288,128]{1,0:T(8,128)}, f32[288,128]{1,0:T(8,128)}, f32[5,32,512]{2,1,0:T(8,128)}, /*index...) custom-call(f32[256,128]{1,0:T(8,128)} %get-tuple-element.32.a1e.own_e_ref, ...), custom_call_target="tpu_custom_call" | custom-call | tf_op jit(solution)/shard_map/mix/pallas_call | solution.py:321
  31.2 37.2 %predict.1 = (f32[16,256,512]{2,1,0:T(8,128)}, f32[16,256,512]{2,1,0:T(8,128)}, f32[256,512]{1,0:T(8,128)}, f32[256,512]{1,0:T(8,128)}, f32[2,256,512]{2,1,0:T(8...) custom-call(f32[256,512]{1,0:T(8,128)} %get-tuple-element.36.kf_ref.kf_hbm, f32[256,512]{1,0:T(8,128)} %h_hbm.1, ...), custom_call_target="tpu_custom_call" | custom-call | tf_op jit(solution)/shard_map/predict/pallas_call | solution.py:623
  68.4 9.7 %exchange.1 = (f32[288,128]{1,0:T(8,128)}, f32[288,128]{1,0:T(8,128)}, f32[2,32,512]{2,1,0:T(8,128)}, f32[3,16,8,512]{3,2,1,0:T(8,128)}) custom-call(f32[256,128]{1,0:T(8,128)} %get-tuple-element.44.be, f32[256,128]{1,0:T(8,128)} %get-tuple-element.45.bw.own_ref, f32[256,512]{1,0:T(8,128)} %get-tuple-element.46.fx.fx_hbm, ...), custom_call_target="tpu_custom_call" | custom-call | tf_op jit(solution)/shard_map/exchange/pallas_call | solution.py:217
  78.0 52.2 %finish.1 = (f32[256,512]{1,0:T(8,128)}, f32[256,512]{1,0:T(8,128)}, f32[256,512]{1,0:T(8,128)}, f32[16,256,512]{2,1,0:T(8,128)}, f32[16,256,512]{2,1,0:T(8,128)...) custom-call(f32[2,30]{1,0:T(2,128)} %bitcast.1, f32[288,128]{1,0:T(8,128)} %get-tuple-element.37.east_ref.a1_e, ...), custom_call_target="tpu_custom_call" | custom-call | tf_op jit(solution)/shard_map/finish/pallas_call | solution.py:933

commit v8 on v7

--- a/solution.py
+++ b/solution.py
@@ -106,7 +106,7 @@
     lane, _ = iotas()
     pair_id = ((lane + 1) >> 1) & 63
     cubes = (u_hbm, v_hbm, t_hbm, s_hbm)
-    strip = 64
+    strip = 32
 
     def copies(i):
         return [pltpu.make_async_copy(cubes[a].at[:, pl.ds(i * strip, strip), chunk(3 * e)], buf.at[i, a, e], sem.at[i, a, e]) for a in range(4) for e in range(2)]
@@ -157,7 +157,7 @@
         out_shape=[f32(NY, LANES)] * 4 + [f32(NY, NX)],
         in_specs=[ANY_SPEC] * 4 + [VMEM_SPEC] * 5,
         out_specs=[VMEM_SPEC] * 5,
-        scratch_shapes=[pltpu.VMEM((4, 4, 2, LEVELS, 64, LANES), jnp.float32), pltpu.SemaphoreType.DMA((4, 4, 2))],
+        scratch_shapes=[pltpu.VMEM((8, 4, 2, LEVELS, 32, LANES), jnp.float32), pltpu.SemaphoreType.DMA((8, 4, 2))],
         compiler_params=pltpu.CompilerParams(vmem_limit_bytes=62 * MIB),
         name="pack",
     )(u, v, temp, salt, k, h, eta, tu, tv)
@@ -778,7 +778,7 @@
         eta_last = carry[0]
         accelerate(SUB - 1, eta_last, north_wrap(eta_first))
 
-    per_loop = next(m for m in (2, 1) if n_sub % m == 0)
+    per_loop = next(m for m in (3, 1) if n_sub % m == 0)
 
     @pl.loop(0, n_sub // per_loop)
     def _(i):

time: 131 us -> 130 us (level)
  no operation moved by 1% of the time
where the time goes in v8:
time: 130 us
  Pallas kernels  129 us (99%)
    pallas_call x1, Pallas kernels, finish(): pl.pallas_call(functools.partial(finish_kernel, n_sub), out_shape=[f32(NY...  52.1 us
    pallas_call x1, Pallas kernels, predict(): pl.pallas_call(predict_kernel, out_shape=[f32(LEVELS, NY, NX)] * 2 + [f32...  37.2 us
    pallas_call x1, Pallas kernels, mix(): pl.pallas_call(functools.partial(mix_kernel, n_cols), out_shape=[f32(EXT_...  20.4 us
    pallas_call x1, Pallas kernels, pack(): pl.pallas_call(pack_kernel, out_shape=[f32(NY, LANES)] * 4 + [f32(NY, NX)...  9.83 us
    pallas_call x1, Pallas kernels, exchange(): pl.pallas_call(functools.partial(exchange_kernel, n_cols), out_shape=[f32...  9.66 us

profile of v8, /device:TPU:0, one launch (start us, length us, event | category | flops | bytes accessed | tf_op | source)
XLA Modules:
  0.0 129.8 jit_solution(18181445327170216816)
XLA Ops:
  0.6 9.8 %pack.1 = (f32[256,128]{1,0:T(8,128)}, f32[256,128]{1,0:T(8,128)}, f32[256,128]{1,0:T(8,128)}, f32[256,128]{1,0:T(8,128)}, f32[256,512]{1,0:T(8,128)}) custom-call(f32[16,256,512]{2,1,0:T(8,128)} %u_hbm.5, f32[16,256,512]{2,1,0:T(8,128)} %v_hbm.5, f32[16,256,512]{2,1,0:T(8,128)} %t_hbm.5, f32[16,256,512]{2,1,0:T(8,128)} %s_hbm.5, s32[256,512]{1,0:T(8,128)} %k_ref.1, ...), custom_call_target="tpu_custom_call" | custom-call | tf_op jit(solution)/shard_map/pack/pallas_call | solution.py:155
  10.5 20.4 %mix.1 = (f32[288,128]{1,0:T(8,128)}, f32[288,128]{1,0:T(8,128)}, f32[288,128]{1,0:T(8,128)}, f32[288,128]{1,0:T(8,128)}, f32[5,32,512]{2,1,0:T(8,128)}, /*index...) custom-call(f32[256,128]{1,0:T(8,128)} %get-tuple-element.32.a1e.own_e_ref, ...), custom_call_target="tpu_custom_call" | custom-call | tf_op jit(solution)/shard_map/mix/pallas_call | solution.py:321
  30.9 37.2 %predict.1 = (f32[16,256,512]{2,1,0:T(8,128)}, f32[16,256,512]{2,1,0:T(8,128)}, f32[256,512]{1,0:T(8,128)}, f32[256,512]{1,0:T(8,128)}, f32[2,256,512]{2,1,0:T(8...) custom-call(f32[256,512]{1,0:T(8,128)} %get-tuple-element.36.kf_ref.kf_hbm, f32[256,512]{1,0:T(8,128)} %h_hbm.1, ...), custom_call_target="tpu_custom_call" | custom-call | tf_op jit(solution)/shard_map/predict/pallas_call | solution.py:623
  68.1 9.7 %exchange.1 = (f32[288,128]{1,0:T(8,128)}, f32[288,128]{1,0:T(8,128)}, f32[2,32,512]{2,1,0:T(8,128)}, f32[3,16,8,512]{3,2,1,0:T(8,128)}) custom-call(f32[256,128]{1,0:T(8,128)} %get-tuple-element.44.be, f32[256,128]{1,0:T(8,128)} %get-tuple-element.45.bw.own_ref, f32[256,512]{1,0:T(8,128)} %get-tuple-element.46.fx.fx_hbm, ...), custom_call_target="tpu_custom_call" | custom-call | tf_op jit(solution)/shard_map/exchange/pallas_call | solution.py:217
  77.7 52.1 %finish.1 = (f32[256,512]{1,0:T(8,128)}, f32[256,512]{1,0:T(8,128)}, f32[256,512]{1,0:T(8,128)}, f32[16,256,512]{2,1,0:T(8,128)}, f32[16,256,512]{2,1,0:T(8,128)...) custom-call(f32[2,30]{1,0:T(2,128)} %bitcast.1, f32[288,128]{1,0:T(8,128)} %get-tuple-element.37.east_ref.a1_e, ...), custom_call_target="tpu_custom_call" | custom-call | tf_op jit(solution)/shard_map/finish/pallas_call | solution.py:933
